TPU v7x, 256 devices: a whole 4x4x8 slice. The times are simulated.
256 devices in a mesh: plane: 64 (over x, z, core), depth: 4 (over y).
Axes of the slice: x: 4, y: 4, z: 8, core: 2. Of those that a mesh axis runs over, the one named last changes fastest.
Arguments:
- labels: int32 [256, 64, 384], P('plane', 'depth'), may hold values from 0 to 3
- start: int32 [3, 16, 256, 64, 384], P(None, None, 'plane', 'depth'), may hold values from -8 to 8
Outputs:
- basis_cols: float32 [80, 256, 64, 384], P(None, 'plane', 'depth')
- coords: float32 [3, 80, 48], replicated
All inputs are finite; a program needn't handle non-finite values.
Results may differ from a plain program's by a relative error of at most 0.00016.
Values sent between devices are 32-bit elements; how exact they have to be, the bound alone decides.
No kernel may reach another device: no remote copies, remote signals or barrier semaphores. Data moves between devices by JAX's collectives and lax.ppermute only.
A program may use at most 64 MiB of HBM per device.

v0:
```python
import jax
import jax.numpy as jnp
from jax import lax
from jax.experimental import pallas as pl
from jax.experimental.pallas import tpu as pltpu
from jax.sharding import Mesh
from jax.sharding import PartitionSpec as P

PLANE = ("plane_0", "plane_1", "plane_2")
WIDE = ("plane_1", "depth")
NARROW = ("plane_0", "plane_2")
B = 16
S = 3 * B
V = 5 * B
A = V + 2 * B

f32 = jnp.float32
bf16 = jnp.bfloat16
highest = lax.Precision.HIGHEST
permittivity_table = (1.0, 2.5, 4.0, 6.5)
damping_table = (0.3, 1.2, 0.05, 2.0)
outer_table = (1.0, 0.5, 2.0, 0.8)
inner_table = (1.0, 3.0, 0.6, 1.5)
CHAIN = ((0, 3, 4), (1, 0, 3), (2, 1, 0))

VMEM = pltpu.VMEM
ANY = pl.ANY


def sum_over(value, axes):
    peers = lax.axis_size(axes)
    copies = jnp.broadcast_to(value[None], (peers,) + value.shape)
    return jnp.sum(lax.all_to_all(copies, axes, 0, 0, tiled=True), axis=0)


def shift(edge, axis, step):
    peers = lax.axis_size(axis)
    pairs = [(i, i + step) for i in range(peers) if 0 <= i + step < peers]
    return lax.ppermute(edge, axis, pairs)


def exchange(low, high, front, back):
    return (
        shift(high, PLANE, 1),
        shift(low, PLANE, -1),
        shift(back, "depth", 1),
        shift(front, "depth", -1),
    )


def call(body, outs, operands, scratch=(), limit=16):
    specs, shapes, results = [], [], []
    for operand, space in operands:
        specs.append(pl.BlockSpec(memory_space=space))
        results.append(operand if space is pl.ANY else pltpu.with_memory_space_constraint(operand, space))
    out_specs = []
    for shape, kind, space in outs:
        out_specs.append(pl.BlockSpec(memory_space=space))
        shapes.append(jax.ShapeDtypeStruct(shape, kind) if space is pl.ANY else space(shape, kind))
    return pl.pallas_call(
        body,
        out_shape=tuple(shapes),
        in_specs=specs,
        out_specs=tuple(out_specs),
        scratch_shapes=list(scratch),
        compiler_params=pltpu.CompilerParams(vmem_limit_bytes=limit * 2**20),
    )(*results)


def sweep(px, py, step, carry):
    for p in range(px):
        carry = step(p, 0, carry)
        carry = lax.fori_loop(1, py - 1, lambda y, value, p=p: step(p, y, value), carry)
        carry = step(p, py - 1, carry)
    return carry


def read_start(start, px, py, cz):
    halves = py // 8

    def body(start_ref, fields_ref, low_ref, high_ref, front_ref, back_ref, raw, sems):
        def copy(chunk):
            p, h = chunk // halves, chunk % halves
            return pltpu.make_async_copy(start_ref.at[:, p, pl.ds(8 * h, 8), :], raw.at[chunk], sems.at[chunk])

        for chunk in range(px * halves):
            copy(chunk).start()

        def step(chunk, carry):
            copy(chunk).wait()
            p, h = chunk // halves, chunk % halves
            rows = pl.multiple_of(8 * h, 8)
            turned = jnp.swapaxes(raw[chunk].astype(f32), 0, 1)
            fields_ref[p, pl.ds(rows, 8)] = turned.astype(bf16)

            @pl.when(p == 0)
            def _():
                low_ref[pl.ds(rows, 8)] = turned

            @pl.when(p == px - 1)
            def _():
                high_ref[pl.ds(rows, 8)] = turned

            @pl.when(h == 0)
            def _():
                front_ref[p] = turned[0]

            @pl.when(h == halves - 1)
            def _():
                back_ref[p] = turned[7]

            return carry

        lax.fori_loop(0, px * halves, step, 0)

    plane, row = ((py, S, cz), f32, VMEM), ((px, S, cz), f32, VMEM)
    return call(
        body,
        (((px, py, S, cz), bf16, VMEM), plane, plane, row, row),
        ((start, pltpu.HBM),),
        (pltpu.VMEM((px * halves, S, 8, cz), jnp.int32), pltpu.SemaphoreType.DMA((px * halves,))),
    )


def laplace(inside, edges, p, y, at, px, py, cz):
    below, above, before, behind = edges
    kept = slice(at, at + B)

    def get(p, y):
        if p < 0:
            row = below[y, kept]
        elif p == px:
            row = above[y, kept]
        elif isinstance(y, int) and y < 0:
            row = before[p, kept]
        elif isinstance(y, int) and y == py:
            row = behind[p, kept]
        else:
            row = inside[p, y, kept]
        return row.astype(f32)

    center = get(p, y)
    lane = lax.broadcasted_iota(jnp.int32, (B, cz), 1)
    left = jnp.where(lane == 0, 0.0, pltpu.roll(center, 1, 1))
    right = jnp.where(lane == cz - 1, 0.0, pltpu.roll(center, cz - 1, 1))
    beside = (get(p + 1, y) + get(p - 1, y)) + (get(p, y + 1) + get(p, y - 1)) + (left + right)
    return 6.0 * center - beside


def set_coefs(labels_ref, coefs, px):
    for p in range(px):
        labels = labels_ref[p]
        for which, table in enumerate((outer_table, damping_table, inner_table)):
            values = [-entry / eps for entry, eps in zip(table, permittivity_table)]
            result = jnp.full(labels.shape, values[0], f32)
            for region in range(1, 4):
                result = jnp.where(labels == region, values[region], result)
            coefs[which, p] = result


def first_lift(labels, fields, edges, px, py, cz):
    def body(labels_ref, fields_ref, below, above, before, behind, lifted, low, high, front, back, coefs):
        set_coefs(labels_ref, coefs, px)
        around = (below, above, before, behind)

        def step(p, y, carry):
            outer, damping, inner = [coefs[k, p, pl.ds(y, 1), :] for k in range(3)]
            out = (
                outer * laplace(fields_ref, around, p, y, 0, px, py, cz)
                + damping * fields_ref[p, y, B : 2 * B, :].astype(f32)
                + inner * laplace(fields_ref, around, p, y, 2 * B, px, py, cz)
            )
            lifted[p, y] = out
            if p == 0:
                low[y] = out
            if p == px - 1:
                high[y] = out
            if isinstance(y, int):
                (back if y else front)[p] = out
            return carry

        sweep(px, py, step, 0)

    plane, row = ((py, B, cz), f32, VMEM), ((px, B, cz), f32, VMEM)
    return call(
        body,
        (((px, py, B, cz), f32, VMEM), plane, plane, row, row),
        ((labels, VMEM), (fields, VMEM)) + tuple((edge, VMEM) for edge in edges),
        (pltpu.VMEM((3, px, py, cz), f32),),
        4,
    )


def second_lift(labels, fields, edges, lifted, ends, px, py, cz):
    def body(labels_ref, fields_ref, lifted_ref, *refs):
        edge_refs, end_refs, (parts, packed, coefs) = refs[:4], refs[4:8], refs[8:]
        set_coefs(labels_ref, coefs, px)

        def step(p, y, gram):
            outer, damping, inner = [coefs[k, p, pl.ds(y, 1), :] for k in range(3)]
            now = fields_ref[p, y]
            second = (
                outer * laplace(lifted_ref, end_refs, p, y, 0, px, py, cz)
                + damping * now[:B].astype(f32)
                + inner * laplace(fields_ref, edge_refs, p, y, B, px, py, cz)
            )
            both = jnp.concatenate([lifted_ref[p, y], second], 0)
            high = both.astype(bf16)
            low = (both - high.astype(f32)).astype(bf16)
            every = jnp.concatenate([now, high, low], 0)
            parts[p, y] = every
            return gram + lax.dot_general(every, every, (((1,), (1,)), ((), ())), preferred_element_type=f32)

        gram = sweep(px, py, step, jnp.zeros((A, A), f32))
        gram = jnp.concatenate([gram, jnp.zeros((A, 128 - A), f32)], 1)
        gram = jnp.concatenate([gram[:S], gram[S:V] + gram[V:]], 0)
        lane = lax.broadcasted_iota(jnp.int32, (V, 128), 1)
        low = pltpu.roll(gram, 128 - 2 * B, 1)
        gram = gram + jnp.where((lane >= S) & (lane < V), low, 0.0)
        half = V // 2
        lane = lax.broadcasted_iota(jnp.int32, (half, 128), 1)
        packed[...] = jnp.where(lane < V, gram[half:], pltpu.roll(gram[:half], V, 1))

    return call(
        body,
        (((px, py, A, cz), bf16, VMEM), ((V // 2, 128), f32, VMEM)),
        ((labels, VMEM), (fields, VMEM), (lifted, VMEM)) + tuple((edge, VMEM) for edge in edges + ends),
        (pltpu.VMEM((3, px, py, cz), f32),),
        4,
    )


def factorize(matrix, count):
    lane = lax.broadcasted_iota(jnp.int32, (8, 128), 1)
    sub = lax.broadcasted_iota(jnp.int32, (8, 128), 0)
    tiles = [matrix[8 * j : 8 * j + 8] for j in range(count // 8)]
    right = [jnp.where(lane == sub + 8 * j, 1.0, 0.0) for j in range(count // 8)]
    upper, inverse = [], []
    for k in range(count):
        own, s = k // 8, k % 8
        pivot = tiles[own][s : s + 1, k : k + 1]
        scale = lax.rsqrt(pivot)
        row = tiles[own][s : s + 1] * scale
        other = right[own][s : s + 1] * scale
        upper.append(row)
        inverse.append(other)
        for j in range(own, count // 8):
            factor = tiles[j][:, k : k + 1] * scale
            if j == own:
                factor = jnp.where(sub[:, :1] > s, factor, 0.0)
            tiles[j] = tiles[j] - factor * row
            right[j] = right[j] - factor * other
    upper = jnp.concatenate(upper, 0)
    inverse = jnp.concatenate(inverse, 0)
    lane = lax.broadcasted_iota(jnp.int32, (count, 128), 1)
    sub = lax.broadcasted_iota(jnp.int32, (count, 128), 0)
    return jnp.where((lane >= sub) & (lane < count), upper, 0.0), inverse


def algebra(packed, cells_total):
    half = V // 2

    def body(packed_ref, matrix_ref, coords_ref):
        table = packed_ref[...] * (1.0 / cells_total)
        turned = jnp.concatenate([table, jnp.zeros((128 - half, 128), f32)], 0).T
        first = jnp.concatenate([pltpu.roll(table, 128 - V, 1), table], 0)
        lane = lax.broadcasted_iota(jnp.int32, (V, 128), 1)
        gram = jnp.where(lane < half, first, jnp.where(lane < V, pltpu.roll(turned[:V], half, 1), 0.0))
        lane = lax.broadcasted_iota(jnp.int32, (B, 128), 1)
        rows = []
        for i in range(3):
            total = jnp.zeros((B, 128), f32)
            for blocks in CHAIN:
                strip = gram[B * blocks[i] : B * blocks[i] + B]
                for j in range(3):
                    moved = pltpu.roll(strip, (B * (j - blocks[j])) % 128, 1)
                    total = total + jnp.where((lane >= B * j) & (lane < B * j + B), moved, 0.0)
            rows.append(total)
        upper, inverse = factorize(gram, V)
        _, small = factorize(jnp.concatenate(rows, 0), S)
        small = jnp.concatenate([small, jnp.zeros((128 - S, 128), f32)], 0).T
        for i in range(3):
            pieces = [jnp.zeros((B, 128), f32)] * 8
            for j in range(3):
                pieces[CHAIN[i][j]] = small[B * j : B * j + B]
            coords = jnp.dot(upper, jnp.concatenate(pieces, 0), precision=highest, preferred_element_type=f32)
            coords_ref[i] = coords[:, :S]
        lane = lax.broadcasted_iota(jnp.int32, (V, 128), 1)
        matrix = jnp.where(lane < V, inverse, pltpu.roll(inverse, 2 * B, 1))[:, :A]
        high = matrix.astype(bf16)
        matrix_ref[:V] = high
        matrix_ref[V:] = (matrix - high.astype(f32)).astype(bf16)

    return call(
        body,
        (((2 * V, A), bf16, VMEM), ((3, V, S), f32, VMEM)),
        ((packed, VMEM),),
        limit=4,
    )


def write_basis(parts, matrix, px, py, cz):
    halves = py // 8

    def body(parts_ref, matrix_ref, out_ref, turned, ready, sems):
        weights = matrix_ref[...]

        def copy(chunk):
            p, h = chunk // halves, chunk % halves
            return pltpu.make_async_copy(ready.at[chunk], out_ref.at[:, p, pl.ds(8 * h, 8), :], sems.at[chunk])

        def step(chunk, carry):
            p, h = chunk // halves, chunk % halves
            for y in range(8):
                out = jnp.dot(weights, parts_ref[p, 8 * h + y], preferred_element_type=f32)
                turned[y] = out[:V] + out[V:]
            ready[chunk] = jnp.swapaxes(turned[...], 0, 1)
            copy(chunk).start()
            return carry

        lax.fori_loop(0, px * halves, step, 0)
        for chunk in range(px * halves):
            copy(chunk).wait()

    return call(
        body,
        (((V, px, py, cz), f32, ANY),),
        ((parts, VMEM), (matrix, VMEM)),
        (
            pltpu.VMEM((8, V, cz), f32),
            pltpu.VMEM((px * halves, V, 8, cz), f32),
            pltpu.SemaphoreType.DMA((px * halves,)),
        ),
        20,
    )[0]


def per_device(labels, start):
    px, py, cz = labels.shape
    cells_total = labels.size * lax.axis_size(PLANE) * lax.axis_size("depth")
    fields, *edges = read_start(start.reshape((S, px, py, cz)), px, py, cz)
    edges = exchange(*edges)
    lifted, *ends = first_lift(labels, fields, edges, px, py, cz)
    ends = exchange(*ends)
    parts, packed = second_lift(labels, fields, edges, lifted, ends, px, py, cz)
    packed = sum_over(sum_over(packed, WIDE), NARROW)
    matrix, coords = algebra(packed, cells_total)
    return (write_basis(parts, matrix, px, py, cz), coords)


def solution(mesh):
    finer = Mesh(
        mesh.devices.reshape(4, 8, 2, mesh.shape["depth"]),
        ("plane_0", "plane_1", "plane_2", "depth"),
    )
    return jax.shard_map(
        per_device,
        mesh=finer,
        in_specs=(P(PLANE, "depth", None), P(None, None, PLANE, "depth", None)),
        out_specs=(P(None, PLANE, "depth", None), P()),
        check_vma=False,
    )
```

profile of v0, /device:TPU:1, one launch (start us, length us, event | category | flops | bytes accessed | tf_op | source)
XLA Modules:
  0.0 121.5 jit_solution(12373899745473307742)
XLA Ops:
  0.6 0.0 copy-start.2
  0.6 2.8 %shard_map.41 = (bf16[4,16,48,384]{3,2,1,0:T(8,128)(2,1)S(1)}, f32[16,48,384]{2,1,0:T(8,128)S(1)}, f32[16,48,384]{2,1,0:T(8,128)S(1)}, f32[4,48,384]{2,1,0:T(8,128)S(1)}, f32[4,48,384]{2,1,0:T(8,128)S(1)}) custom-call(s32[48,4,16,384]{3,2,1,0:T(8,128)} %bitcast.1), custom_call_target="tpu_custom_call" | custom-call | tf_op jit(solution)/shard_map/pallas_call | solution.py:60
  3.4 4.9 %collective-permute-start = (f32[16,48,384]{2,1,0:T(8,128)S(1)}, f32[16,48,384]{2,1,0:T(8,128)S(1)}, u32[]{:S(2)}, u32[]{:S(2)}) collective-permute-start(f32[16,48,384]{2,1,0:T(8,128)S(1)} %get-tuple-element.17), channel_id=1, source_target_pairs={{0,4},{4,8},{8,12},{12,16},{16,20},{20,24},{24,28},{28,32},{32,36}... | collective-permute-start | bytes 3538952 | tf_op jit(solution)/shard_map/ppermute | solution.py:39
  8.4 1.9 %collective-permute-start.1 = (f32[16,48,384]{2,1,0:T(8,128)S(1)}, f32[16,48,384]{2,1,0:T(8,128)S(1)}, u32[]{:S(2)}, u32[]{:S(2)}) collective-permute-start(f32[16,48,384]{2,1,0:T(8,128)S(1)} %get-tuple-element.18), channel_id=1, source_target_pairs={{4,0},{8,4},{12,8},{16,12},{20,16},{24,20},{28,24},{32,28},{36,32}... | collective-permute-start | bytes 3538952 | tf_op jit(solution)/shard_map/ppermute | solution.py:39
  10.3 3.2 %collective-permute-start.2 = (f32[4,48,384]{2,1,0:T(8,128)S(1)}, f32[4,48,384]{2,1,0:T(8,128)S(1)}, u32[]{:S(2)}, u32[]{:S(2)}) collective-permute-start(f32[4,48,384]{2,1,0:T(8,128)S(1)} %get-tuple-element.19), channel_id=1, source_target_pairs={{0,1},{1,2},{2,3},{4,5},{5,6},{6,7},{8,9},{9,10},{10,11},{12,13},{... | collective-permute-start | bytes 884744 | tf_op jit(solution)/shard_map/ppermute | solution.py:39
  13.5 1.3 %collective-permute-start.3 = (f32[4,48,384]{2,1,0:T(8,128)S(1)}, f32[4,48,384]{2,1,0:T(8,128)S(1)}, u32[]{:S(2)}, u32[]{:S(2)}) collective-permute-start(f32[4,48,384]{2,1,0:T(8,128)S(1)} %get-tuple-element.20), channel_id=1, source_target_pairs={{1,0},{2,1},{3,2},{5,4},{6,5},{7,6},{9,8},{10,9},{11,10},{13,12},{... | collective-permute-start | bytes 884744 | tf_op jit(solution)/shard_map/ppermute | solution.py:39
  14.8 3.7 %collective-permute-done.2.before.refs_2_ = f32[4,48,384]{2,1,0:T(8,128)S(1)} collective-permute-done((f32[4,48,384]{2,1,0:T(8,128)S(1)}, f32[4,48,384]{2,1,0:T(8,128)S(1)}, u32[]{:S(2)}, u32[]{:S(2)}) %collective-permute-start.2) | collective-permute-done | bytes 294944 | tf_op jit(solution)/shard_map/ppermute | solution.py:39
  18.5 4.1 %collective-permute-done.3.behind.refs_3_ = f32[4,48,384]{2,1,0:T(8,128)S(1)} collective-permute-done((f32[4,48,384]{2,1,0:T(8,128)S(1)}, f32[4,48,384]{2,1,0:T(8,128)S(1)}, u32[]{:S(2)}, u32[]{:S(2)}) %collective-permute-start.3) | collective-permute-done | bytes 294944 | tf_op jit(solution)/shard_map/ppermute | solution.py:39
  22.6 0.0 collective-permute-done.below.refs_0_
  22.6 3.2 %collective-permute-done.1.above.refs_1_ = f32[16,48,384]{2,1,0:T(8,128)S(1)} collective-permute-done((f32[16,48,384]{2,1,0:T(8,128)S(1)}, f32[16,48,384]{2,1,0:T(8,128)S(1)}, u32[]{:S(2)}, u32[]{:S(2)}) %collective-permute-start.1) | collective-permute-done | bytes 1179680 | tf_op jit(solution)/shard_map/ppermute | solution.py:39
  25.9 0.0 copy-done.2
  25.9 5.8 %shard_map.42 = (f32[4,16,16,384]{3,2,1,0:T(8,128)S(1)}, f32[16,16,384]{2,1,0:T(8,128)S(1)}, f32[16,16,384]{2,1,0:T(8,128)S(1)}, f32[4,16,384]{2,1,0:T(8,128)S(1)}, f32[4,16,384]{2,1,0:T(8,128)S(1)}) custom-call(s32[4,16,384]{2,1,0:T(8,128)S(1)} %copy-done.2, bf16[4,16,48,384]{3,2,1,0:T(8,128)(2,1)S(1)} %get-tuple-element.16.fields_ref, ...), custom_call_target="tpu_custom_call" | custom-call | tf_op jit(solution)/shard_map/pallas_call | solution.py:60
  31.7 2.4 %collective-permute-start.4 = (f32[16,16,384]{2,1,0:T(8,128)S(1)}, f32[16,16,384]{2,1,0:T(8,128)S(1)}, u32[]{:S(2)}, u32[]{:S(2)}) collective-permute-start(f32[16,16,384]{2,1,0:T(8,128)S(1)} %get-tuple-element.22), channel_id=1, source_target_pairs={{0,4},{4,8},{8,12},{12,16},{16,20},{20,24},{24,28},{28,32},{32,36}... | collective-permute-start | bytes 1179656 | tf_op jit(solution)/shard_map/ppermute | solution.py:39
  34.1 2.0 %collective-permute-start.5 = (f32[16,16,384]{2,1,0:T(8,128)S(1)}, f32[16,16,384]{2,1,0:T(8,128)S(1)}, u32[]{:S(2)}, u32[]{:S(2)}) collective-permute-start(f32[16,16,384]{2,1,0:T(8,128)S(1)} %get-tuple-element.23), channel_id=1, source_target_pairs={{4,0},{8,4},{12,8},{16,12},{20,16},{24,20},{28,24},{32,28},{36,32}... | collective-permute-start | bytes 1179656 | tf_op jit(solution)/shard_map/ppermute | solution.py:39
  36.0 3.2 %collective-permute-start.6 = (f32[4,16,384]{2,1,0:T(8,128)S(1)}, f32[4,16,384]{2,1,0:T(8,128)S(1)}, u32[]{:S(2)}, u32[]{:S(2)}) collective-permute-start(f32[4,16,384]{2,1,0:T(8,128)S(1)} %get-tuple-element.24), channel_id=1, source_target_pairs={{0,1},{1,2},{2,3},{4,5},{5,6},{6,7},{8,9},{9,10},{10,11},{12,13},{... | collective-permute-start | bytes 294920 | tf_op jit(solution)/shard_map/ppermute | solution.py:39
  39.2 1.3 %collective-permute-start.7 = (f32[4,16,384]{2,1,0:T(8,128)S(1)}, f32[4,16,384]{2,1,0:T(8,128)S(1)}, u32[]{:S(2)}, u32[]{:S(2)}) collective-permute-start(f32[4,16,384]{2,1,0:T(8,128)S(1)} %get-tuple-element.25), channel_id=1, source_target_pairs={{1,0},{2,1},{3,2},{5,4},{6,5},{7,6},{9,8},{10,9},{11,10},{13,12},{... | collective-permute-start | bytes 294920 | tf_op jit(solution)/shard_map/ppermute | solution.py:39
  40.5 1.2 collective-permute-done.6.refs_6_
  41.7 4.1 %collective-permute-done.7.refs_7_ = f32[4,16,384]{2,1,0:T(8,128)S(1)} collective-permute-done((f32[4,16,384]{2,1,0:T(8,128)S(1)}, f32[4,16,384]{2,1,0:T(8,128)S(1)}, u32[]{:S(2)}, u32[]{:S(2)}) %collective-permute-start.7) | collective-permute-done | bytes 98336 | tf_op jit(solution)/shard_map/ppermute | solution.py:39
  45.8 0.0 collective-permute-done.4.refs_4_
  45.8 0.0 collective-permute-done.5.refs_5_
  45.8 16.4 %shard_map.43 = (bf16[4,16,112,384]{3,2,1,0:T(8,128)(2,1)S(1)}, f32[40,128]{1,0:T(8,128)S(1)}) custom-call(s32[4,16,384]{2,1,0:T(8,128)S(1)} %copy-done.2, bf16[4,16,48,384]{3,2,1,0:T(8,128)(2,1)S(1)} %get-tuple-element.16.fields_ref, f32[4,16,16,384]{3,2,1,0:T(8,128)S(1)} %get-tuple-element.21.lifted_ref, ...), custom_call_target="tpu_custom_call" | custom-call | tf_op jit(solution)/shard_map/pallas_call | solution.py:60
  62.2 0.0 copy-start
  62.2 2.4 %copy-done = bf16[4,16,112,384]{3,2,1,0:T(8,128)(2,1)} copy-done((bf16[4,16,112,384]{3,2,1,0:T(8,128)(2,1)}, bf16[4,16,112,384]{3,2,1,0:T(8,128)(2,1)S(1)}, u32[]{:S(2)}) %copy-start) | copy-done | bytes 5505048
  64.7 25.7 %all_to_all.10 = f32[32,40,128]{2,1,0:T(8,128)S(1)} all-to-all(f32[32,40,128]{2,1,0:T(8,128)S(1)} %broadcast_in_dim.4), channel_id=1, replica_groups=mesh['plane_0'=4,'plane_1'=8,'plane_2'=2,'depth'=4] {'plane_1','depth'}, dimensions={0} | all-to-all | bytes 1310720 | tf_op jit(solution)/shard_map/all_to_all | solution.py:33
  90.4 0.1 reduce_sum.18
  90.4 15.4 %all_to_all.11 = f32[8,40,128]{2,1,0:T(8,128)S(1)} all-to-all(f32[8,40,128]{2,1,0:T(8,128)S(1)} %broadcast_in_dim.5), channel_id=1, replica_groups=mesh['plane_0'=4,'plane_1'=8,'plane_2'=2,'depth'=4] {'plane_0','plane_2'}, dimensions={0} | all-to-all | bytes 327680 | tf_op jit(solution)/shard_map/all_to_all | solution.py:33
  105.8 7.0 %shard_map.44 = (bf16[160,112]{1,0:T(8,128)(2,1)S(1)}, f32[3,80,48]{2,1,0:T(8,128)S(1)}) custom-call(f32[40,128]{1,0:T(8,128)S(1)} %reduce_sum.19.packed_ref), custom_call_target="tpu_custom_call" | custom-call | tf_op jit(solution)/shard_map/pallas_call | solution.py:60
  112.9 0.7 copy.5
  113.6 0.0 copy-start.1
  113.6 2.6 %copy-done.1 = bf16[4,16,112,384]{3,2,1,0:T(8,128)(2,1)S(1)} copy-done((bf16[4,16,112,384]{3,2,1,0:T(8,128)(2,1)S(1)}, bf16[4,16,112,384]{3,2,1,0:T(8,128)(2,1)}, u32[]{:S(2)}) %copy-start.1) | copy-done | bytes 5505048
  116.2 5.3 %shard_map.45 = f32[80,4,16,384]{3,2,1,0:T(8,128)} custom-call(bf16[4,16,112,384]{3,2,1,0:T(8,128)(2,1)S(1)} %copy-done.1, bf16[160,112]{1,0:T(8,128)(2,1)S(1)} %get-tuple-element.28.matrix_ref), custom_call_target="tpu_custom_call" | custom-call | tf_op jit(solution)/shard_map/pallas_call | solution.py:60
  (3 shorter events, 0.1 us)
Async XLA Ops:
  0.6 25.3 %copy-start.2 = (s32[4,16,384]{2,1,0:T(8,128)S(1)}, s32[4,16,384]{2,1,0:T(8,128)}, u32[]{:S(2)}) copy-start(s32[4,16,384]{2,1,0:T(8,128)} %labels_ref.3) | copy-start | bytes 294916
  3.4 19.2 %collective-permute-start = (f32[16,48,384]{2,1,0:T(8,128)S(1)}, f32[16,48,384]{2,1,0:T(8,128)S(1)}, u32[]{:S(2)}, u32[]{:S(2)}) collective-permute-start(f32[16,48,384]{2,1,0:T(8,128)S(1)} %get-tuple-element.17), channel_id=1, source_target_pairs={{0,4},{4,8},{8,12},{12,16},{16,20},{20,24},{24,28},{28,32},{32,36}... | collective-permute-start | bytes 3538952 | tf_op jit(solution)/shard_map/ppermute | solution.py:39
  8.4 17.5 %collective-permute-start.1 = (f32[16,48,384]{2,1,0:T(8,128)S(1)}, f32[16,48,384]{2,1,0:T(8,128)S(1)}, u32[]{:S(2)}, u32[]{:S(2)}) collective-permute-start(f32[16,48,384]{2,1,0:T(8,128)S(1)} %get-tuple-element.18), channel_id=1, source_target_pairs={{4,0},{8,4},{12,8},{16,12},{20,16},{24,20},{28,24},{32,28},{36,32}... | collective-permute-start | bytes 3538952 | tf_op jit(solution)/shard_map/ppermute | solution.py:39
  10.3 8.2 %collective-permute-start.2 = (f32[4,48,384]{2,1,0:T(8,128)S(1)}, f32[4,48,384]{2,1,0:T(8,128)S(1)}, u32[]{:S(2)}, u32[]{:S(2)}) collective-permute-start(f32[4,48,384]{2,1,0:T(8,128)S(1)} %get-tuple-element.19), channel_id=1, source_target_pairs={{0,1},{1,2},{2,3},{4,5},{5,6},{6,7},{8,9},{9,10},{10,11},{12,13},{... | collective-permute-start | bytes 884744 | tf_op jit(solution)/shard_map/ppermute | solution.py:39
  13.5 9.1 %collective-permute-start.3 = (f32[4,48,384]{2,1,0:T(8,128)S(1)}, f32[4,48,384]{2,1,0:T(8,128)S(1)}, u32[]{:S(2)}, u32[]{:S(2)}) collective-permute-start(f32[4,48,384]{2,1,0:T(8,128)S(1)} %get-tuple-element.20), channel_id=1, source_target_pairs={{1,0},{2,1},{3,2},{5,4},{6,5},{7,6},{9,8},{10,9},{11,10},{13,12},{... | collective-permute-start | bytes 884744 | tf_op jit(solution)/shard_map/ppermute | solution.py:39
  31.7 14.2 %collective-permute-start.4 = (f32[16,16,384]{2,1,0:T(8,128)S(1)}, f32[16,16,384]{2,1,0:T(8,128)S(1)}, u32[]{:S(2)}, u32[]{:S(2)}) collective-permute-start(f32[16,16,384]{2,1,0:T(8,128)S(1)} %get-tuple-element.22), channel_id=1, source_target_pairs={{0,4},{4,8},{8,12},{12,16},{16,20},{20,24},{24,28},{28,32},{32,36}... | collective-permute-start | bytes 1179656 | tf_op jit(solution)/shard_map/ppermute | solution.py:39
  34.1 11.8 %collective-permute-start.5 = (f32[16,16,384]{2,1,0:T(8,128)S(1)}, f32[16,16,384]{2,1,0:T(8,128)S(1)}, u32[]{:S(2)}, u32[]{:S(2)}) collective-permute-start(f32[16,16,384]{2,1,0:T(8,128)S(1)} %get-tuple-element.23), channel_id=1, source_target_pairs={{4,0},{8,4},{12,8},{16,12},{20,16},{24,20},{28,24},{32,28},{36,32}... | collective-permute-start | bytes 1179656 | tf_op jit(solution)/shard_map/ppermute | solution.py:39
  36.0 5.7 %collective-permute-start.6 = (f32[4,16,384]{2,1,0:T(8,128)S(1)}, f32[4,16,384]{2,1,0:T(8,128)S(1)}, u32[]{:S(2)}, u32[]{:S(2)}) collective-permute-start(f32[4,16,384]{2,1,0:T(8,128)S(1)} %get-tuple-element.24), channel_id=1, source_target_pairs={{0,1},{1,2},{2,3},{4,5},{5,6},{6,7},{8,9},{9,10},{10,11},{12,13},{... | collective-permute-start | bytes 294920 | tf_op jit(solution)/shard_map/ppermute | solution.py:39
  39.2 6.6 %collective-permute-start.7 = (f32[4,16,384]{2,1,0:T(8,128)S(1)}, f32[4,16,384]{2,1,0:T(8,128)S(1)}, u32[]{:S(2)}, u32[]{:S(2)}) collective-permute-start(f32[4,16,384]{2,1,0:T(8,128)S(1)} %get-tuple-element.25), channel_id=1, source_target_pairs={{1,0},{2,1},{3,2},{5,4},{6,5},{7,6},{9,8},{10,9},{11,10},{13,12},{... | collective-permute-start | bytes 294920 | tf_op jit(solution)/shard_map/ppermute | solution.py:39
  62.2 2.5 %copy-start = (bf16[4,16,112,384]{3,2,1,0:T(8,128)(2,1)}, bf16[4,16,112,384]{3,2,1,0:T(8,128)(2,1)S(1)}, u32[]{:S(2)}) copy-start(bf16[4,16,112,384]{3,2,1,0:T(8,128)(2,1)S(1)} %get-tuple-element.26.parts_ref) | copy-start | bytes 16515076
  113.6 2.6 %copy-start.1 = (bf16[4,16,112,384]{3,2,1,0:T(8,128)(2,1)S(1)}, bf16[4,16,112,384]{3,2,1,0:T(8,128)(2,1)}, u32[]{:S(2)}) copy-start(bf16[4,16,112,384]{3,2,1,0:T(8,128)(2,1)} %copy-done) | copy-start | bytes 16515076
where the time goes:
time: 122 us; the launch traced here: 121 us
  blocking collectives  41.1 us (34%)
  Pallas kernels  37.3 us (31%)
  starting transfers between devices  20.2 us (17%)
  waiting for transfers between devices  16.4 us (13%)
  local copies, waits for them, and re-layouts  5.81 us (5%)
    all_to_all x2, blocking collectives, sum_over(): return jnp.sum(lax.all_to_all(copies, axes, 0, 0, tiled=True), axis=0)  41.1 us
    pallas_call x5, Pallas kernels, call(): pl.pallas_call(body, out_shape=tuple(shapes), in_specs=specs, out_specs=t...  37.3 us
    ppermute x8, starting transfers between devices, shift(): return lax.ppermute(edge, axis, pairs)  20.2 us
    ppermute x8, waiting for transfers between devices, shift(): return lax.ppermute(edge, axis, pairs)  16.4 us
    unnamed x7, local copies, waits for them, and re-layouts  5.75 us
  transfers between devices with their start and end apart: 8, of which 5 were waited for; matrix products, arithmetic and copies ran while one was open for 0% of the time, Pallas kernels for 0%

commit v1 on v0

v1 whole, which is shorter than its diff:
```python
import jax
import jax.numpy as jnp
from jax import lax
from jax.experimental import pallas as pl
from jax.experimental.pallas import tpu as pltpu
from jax.sharding import Mesh
from jax.sharding import PartitionSpec as P

PLANE = ("plane_0", "plane_1", "plane_2")
WIDE = ("plane_1", "depth")
B = 16
S = 3 * B
V = 5 * B
A = V + 2 * B

f32 = jnp.float32
bf16 = jnp.bfloat16
highest = lax.Precision.HIGHEST
permittivity_table = (1.0, 2.5, 4.0, 6.5)
damping_table = (0.3, 1.2, 0.05, 2.0)
outer_table = (1.0, 0.5, 2.0, 0.8)
inner_table = (1.0, 3.0, 0.6, 1.5)
CHAIN = ((0, 3, 4), (1, 0, 3), (2, 1, 0))
BLOCKS = [(i, j) for j in range(5) for i in range(j + 1)]

VMEM = pltpu.VMEM
ANY = pl.ANY


def sum_over(value, axes):
    peers = lax.axis_size(axes)
    copies = jnp.broadcast_to(value[None], (peers,) + value.shape)
    return jnp.sum(lax.all_to_all(copies, axes, 0, 0, tiled=True), axis=0)


def sum_all(table):
    both = jnp.sum(lax.all_gather(table, "plane_2"), axis=0)
    own = jnp.where(lax.axis_index("plane_2") == 0, both[:B], both[B:])
    own = sum_over(sum_over(own, WIDE), "plane_0")
    return lax.all_gather(own, "plane_2", tiled=True)


def shift(edge, axis, step):
    peers = lax.axis_size(axis)
    pairs = [(i, i + step) for i in range(peers) if 0 <= i + step < peers]
    return lax.ppermute(edge, axis, pairs)


def exchange(low, high, front, back):
    before, behind = shift(back, "depth", 1), shift(front, "depth", -1)
    return (shift(high, PLANE, 1), shift(low, PLANE, -1), before, behind)


def call(body, outs, operands, scratch=(), limit=16, work=0):
    specs, shapes, results = [], [], []
    for operand, space in operands:
        specs.append(pl.BlockSpec(memory_space=space))
        results.append(operand if space is pl.ANY else pltpu.with_memory_space_constraint(operand, space))
    out_specs = []
    for shape, kind, space in outs:
        out_specs.append(pl.BlockSpec(memory_space=space))
        shapes.append(jax.ShapeDtypeStruct(shape, kind) if space is pl.ANY else space(shape, kind))
    return pl.pallas_call(
        body,
        out_shape=tuple(shapes),
        in_specs=specs,
        out_specs=tuple(out_specs),
        scratch_shapes=list(scratch),
        cost_estimate=pl.CostEstimate(flops=work, bytes_accessed=0, transcendentals=0),
        compiler_params=pltpu.CompilerParams(vmem_limit_bytes=limit * 2**20),
    )(*results)


def sweep(px, py, step):
    group = next(count for count in (7, 6, 5, 4, 3, 2, 1) if (py - 2) % count == 0)
    for p in range(px):
        step(p, 0)

        def several(j, carry):
            for i in range(group):
                step(p, 1 + group * j + i)
            return carry

        lax.fori_loop(0, (py - 2) // group, several, 0)
        step(p, py - 1)


def read_start(start, px, py, cz):
    halves = py // 8

    def body(start_ref, fields_ref, low_ref, high_ref, front_ref, back_ref, raw, sems):
        def copy(chunk):
            p, h = chunk // halves, chunk % halves
            return pltpu.make_async_copy(start_ref.at[:, p, pl.ds(8 * h, 8), :], raw.at[chunk], sems.at[chunk])

        for chunk in range(px * halves):
            copy(chunk).start()

        def step(chunk, carry):
            copy(chunk).wait()
            p, h = chunk // halves, chunk % halves
            rows = pl.multiple_of(8 * h, 8)
            turned = jnp.swapaxes(raw[chunk].astype(f32), 0, 1)
            sent = jnp.concatenate([turned[:, :B], turned[:, 2 * B :]], 1)
            fields_ref[p, pl.ds(rows, 8)] = turned.astype(bf16)

            @pl.when(p == 0)
            def _():
                low_ref[pl.ds(rows, 8)] = sent

            @pl.when(p == px - 1)
            def _():
                high_ref[pl.ds(rows, 8)] = sent

            @pl.when(h == 0)
            def _():
                front_ref[p] = sent[0]

            @pl.when(h == halves - 1)
            def _():
                back_ref[p] = sent[7]

            return carry

        lax.fori_loop(0, px * halves, step, 0)

    plane, row = ((py, 2 * B, cz), f32, VMEM), ((px, 2 * B, cz), f32, VMEM)
    return call(
        body,
        (((px, py, S, cz), bf16, VMEM), plane, plane, row, row),
        ((start, pltpu.HBM),),
        (pltpu.VMEM((px * halves, S, 8, cz), jnp.int32), pltpu.SemaphoreType.DMA((px * halves,))),
    )


def laplace(inside, edges, p, y, at, edge_at, px, py, cz):
    below, above, before, behind = edges
    kept, outer = slice(at, at + B), slice(edge_at, edge_at + B)

    def get(p, y):
        if p < 0:
            row = below[y, outer]
        elif p == px:
            row = above[y, outer]
        elif isinstance(y, int) and y < 0:
            row = before[p, outer]
        elif isinstance(y, int) and y == py:
            row = behind[p, outer]
        else:
            row = inside[p, y, kept]
        return row.astype(inside.dtype)

    center = get(p, y)
    wide = center.astype(f32)
    lane = lax.broadcasted_iota(jnp.int32, (B, cz), 1)
    left = jnp.where(lane == 0, 0.0, pltpu.roll(wide, 1, 1))
    right = jnp.where(lane == cz - 1, 0.0, pltpu.roll(wide, cz - 1, 1))
    beside = (get(p + 1, y) + get(p - 1, y)) + (get(p, y + 1) + get(p, y - 1))
    return 6.0 * wide - (beside.astype(f32) + (left + right))


def set_coefs(labels_ref, coefs, px):
    for p in range(px):
        labels = labels_ref[p]
        for which, table in enumerate((outer_table, damping_table, inner_table)):
            values = [-entry / eps for entry, eps in zip(table, permittivity_table)]
            result = jnp.full(labels.shape, values[0], f32)
            for region in range(1, 4):
                result = jnp.where(labels == region, values[region], result)
            coefs[which, p] = result


def first_lift(labels, fields, gram, edges, px, py, cz):
    def body(labels_ref, fields_ref, gram_ref, below, above, before, behind, lifted, low, high, front, back, coefs):
        set_coefs(labels_ref, coefs, px)
        around = (below, above, before, behind)

        def step(p, y):
            outer, damping, inner = [coefs[k, p, pl.ds(y, 1), :] for k in range(3)]
            middle = fields_ref[p, y, B : 2 * B, :].astype(f32)
            out = (
                outer * laplace(fields_ref, around, p, y, 0, 0, px, py, cz)
                + damping * middle
                + inner * laplace(fields_ref, around, p, y, 2 * B, B, px, py, cz)
            )
            lifted[p, y] = out
            if p in (0, px - 1) or isinstance(y, int):
                edge = jnp.concatenate([out, middle], 0)
            if p == 0:
                low[y] = edge
            if p == px - 1:
                high[y] = edge
            if isinstance(y, int):
                (back if y else front)[p] = edge

        sweep(px, py, step)

    plane, row = ((py, 2 * B, cz), f32, VMEM), ((px, 2 * B, cz), f32, VMEM)
    return call(
        body,
        (((px, py, B, cz), f32, VMEM), plane, plane, row, row),
        ((labels, VMEM), (fields, VMEM), (gram, ANY)) + tuple((edge, VMEM) for edge in edges),
        (pltpu.VMEM((3, px, py, cz), f32),),
        4,
    )


def gram_loop(count, rows, left, right, shape):
    def step(j, total):
        lhs = jnp.concatenate([left(j * count + i) for i in range(count)], 1)
        rhs = jnp.concatenate([right(j * count + i) for i in range(count)], 1)
        return total + lax.dot_general(lhs, rhs, (((1,), (1,)), ((), ())), preferred_element_type=f32)

    return lax.fori_loop(0, rows // count, step, jnp.zeros(shape, f32))


def start_products(fields, px, py):
    def body(fields_ref, gram_ref):
        def row(r):
            return fields_ref[r // py, r % py]

        gram_ref[...] = gram_loop(16, px * py, row, row, (S, S))

    return call(body, (((S, S), f32, VMEM),), ((fields, VMEM),), limit=4, work=10**9)[0]


def split(values):
    high = values.astype(bf16)
    return jnp.concatenate([high, (values - high.astype(f32)).astype(bf16)], 0)


def lifted_products(fields, lifted, px, py, cz):
    def body(fields_ref, lifted_ref, halves_ref, gram_ref):
        def part(r):
            halves = split(lifted_ref[r // py, r % py])
            halves_ref[r // py, r % py] = halves
            return halves

        def step(j, total):
            parts = [part(8 * j + i) for i in range(8)]
            rows = [fields_ref[(8 * j + i) // py, (8 * j + i) % py] for i in range(8)]
            rhs = jnp.concatenate(parts, 1)
            lhs = jnp.concatenate([jnp.concatenate(rows, 1), rhs], 0)
            return total + lax.dot_general(lhs, rhs, (((1,), (1,)), ((), ())), preferred_element_type=f32)

        gram_ref[...] = lax.fori_loop(0, px * py // 8, step, jnp.zeros((S + 2 * B, 2 * B), f32))

    return call(
        body,
        (((px, py, 2 * B, cz), bf16, VMEM), ((S + 2 * B, 2 * B), f32, VMEM)),
        ((fields, VMEM), (lifted, VMEM)),
        limit=4,
        work=10**9,
    )


def second_lift(labels, fields, lifted, ends, halves, grams, px, py, cz):
    def body(labels_ref, fields_ref, lifted_ref, halves_ref, start_ref, middle_ref, *refs):
        end_refs, (parts_out, packed, coefs, parts, sems) = refs[:4], refs[4:]
        set_coefs(labels_ref, coefs, px)

        def copy(p):
            return pltpu.make_async_copy(parts.at[p], parts_out.at[p], sems.at[p])

        def step(p, y):
            outer, damping, inner = [coefs[k, p, pl.ds(y, 1), :] for k in range(3)]
            now = fields_ref[p, y]
            second = (
                outer * laplace(lifted_ref, end_refs, p, y, 0, 0, px, py, cz)
                + damping * now[:B].astype(f32)
                + inner * laplace(fields_ref, end_refs, p, y, B, B, px, py, cz)
            )
            parts[p, y] = jnp.concatenate([now, halves_ref[p, y], split(second)], 0)

        def left(r):
            return parts[r // py, r % py]

        def right(r):
            return parts[r // py, r % py, S + 2 * B :]

        sweep(px, py, step)
        for p in range(px):
            copy(p).start()
        last = gram_loop(8, px * py, left, right, (A, 2 * B))
        last = jnp.concatenate([last, jnp.zeros((A, 128 - 2 * B), f32)], 1)
        last = last + pltpu.roll(last, 128 - B, 1)
        middle = jnp.concatenate([middle_ref[...], jnp.zeros((S + 2 * B, 128 - 2 * B), f32)], 1)
        middle = middle + pltpu.roll(middle, 128 - B, 1)
        middle = jnp.concatenate([middle[:S], middle[S : S + B] + middle[S + B :]], 0)
        last = jnp.concatenate([last[:S], last[S : S + B] + last[S + B : S + 2 * B], last[S + 2 * B : S + 3 * B] + last[S + 3 * B :]], 0)
        first = jnp.concatenate([start_ref[...], jnp.zeros((S, 128 - S), f32)], 1)
        lane = lax.broadcasted_iota(jnp.int32, (B, 128), 1)
        sums = [jnp.zeros((B, 128), f32)] * 2
        for at, (i, j) in enumerate(BLOCKS):
            source, column = (first, j) if j < 3 else ((middle, 0) if j == 3 else (last, 0))
            moved = pltpu.roll(source[B * i : B * i + B], (B * (at % 8 - column)) % 128, 1)
            kept = (lane >= B * (at % 8)) & (lane < B * (at % 8) + B)
            sums[at // 8] = jnp.where(kept, moved, sums[at // 8])
        packed[...] = jnp.concatenate(sums, 0)
        for p in range(px):
            copy(p).wait()

    return call(
        body,
        (((px, py, A, cz), bf16, pltpu.HBM), ((2 * B, 128), f32, VMEM)),
        tuple((x, VMEM) for x in (labels, fields, lifted, halves) + tuple(grams) + ends),
        (
            pltpu.VMEM((3, px, py, cz), f32),
            pltpu.VMEM((px, py, A, cz), bf16),
            pltpu.SemaphoreType.DMA((px,)),
        ),
        12,
    )


def factorize(matrix, count):
    lane = lax.broadcasted_iota(jnp.int32, (8, 128), 1)
    sub = lax.broadcasted_iota(jnp.int32, (8, 128), 0)
    tiles = [matrix[8 * j : 8 * j + 8] for j in range(count // 8)]
    right = [jnp.where(lane == sub + 8 * j, 1.0, 0.0) for j in range(count // 8)]
    upper, inverse = [], []
    for k in range(count):
        own, s = k // 8, k % 8
        pivot = tiles[own][s : s + 1, k : k + 1]
        scale = lax.rsqrt(pivot)
        row = tiles[own][s : s + 1] * scale
        other = right[own][s : s + 1] * scale
        upper.append(row)
        inverse.append(other)
        for j in range(own, count // 8):
            factor = tiles[j][:, k : k + 1] * scale
            if j == own:
                factor = jnp.where(sub[:, :1] > s, factor, 0.0)
            tiles[j] = tiles[j] - factor * row
            right[j] = right[j] - factor * other
    upper = jnp.concatenate(upper, 0)
    inverse = jnp.concatenate(inverse, 0)
    lane = lax.broadcasted_iota(jnp.int32, (count, 128), 1)
    sub = lax.broadcasted_iota(jnp.int32, (count, 128), 0)
    return jnp.where((lane >= sub) & (lane < count), upper, 0.0), inverse


def place(strip, origin, target):
    lane = lax.broadcasted_iota(jnp.int32, strip.shape, 1)
    moved = pltpu.roll(strip, (B * (target - origin)) % 128, 1) if target != origin else strip
    return jnp.where((lane >= B * target) & (lane < B * target + B), moved, 0.0)


def algebra(packed, cells_total):
    def body(packed_ref, matrix_ref, coords_ref):
        table = packed_ref[...] * (1.0 / cells_total)
        rows = [jnp.zeros((B, 128), f32)] * 8
        for at, (i, j) in enumerate(BLOCKS):
            rows[i] = rows[i] + place(table[B * (at // 8) : B * (at // 8) + B], at % 8, j)
        square = jnp.concatenate(rows, 0)
        lane = lax.broadcasted_iota(jnp.int32, (128, 128), 1)
        sub = lax.broadcasted_iota(jnp.int32, (128, 128), 0)
        gram = jnp.where(lane // B >= sub // B, square, square.T)[:V]
        rows = []
        for i in range(3):
            total = jnp.zeros((B, 128), f32)
            for blocks in CHAIN:
                strip = gram[B * blocks[i] : B * blocks[i] + B]
                for j in range(3):
                    total = total + place(strip, blocks[j], j)
            rows.append(total)
        upper, inverse = factorize(gram, V)
        _, small = factorize(jnp.concatenate(rows, 0), S)
        for i in range(3):
            chosen = place(small, 0, CHAIN[i][0]) + place(small, 1, CHAIN[i][1]) + place(small, 2, CHAIN[i][2])
            coords_ref[i] = lax.dot_general(
                chosen, upper, (((1,), (1,)), ((), ())), precision=highest, preferred_element_type=f32
            )
        lane = lax.broadcasted_iota(jnp.int32, (V, 128), 1)
        matrix = jnp.where(lane < S + B, inverse, 0.0)
        matrix = matrix + place(inverse, 3, 4) + place(inverse, 4, 5) + place(inverse, 4, 6)
        matrix = matrix[:, :A]
        high = matrix.astype(bf16)
        matrix_ref[:V] = high
        matrix_ref[V:] = (matrix - high.astype(f32)).astype(bf16)

    return call(
        body,
        (((2 * V, A), bf16, VMEM), ((3, S, V), f32, VMEM)),
        ((packed, VMEM),),
        limit=4,
    )


def write_basis(parts, matrix, px, py, cz):
    halves = py // 8

    def body(parts_in, matrix_ref, out_ref, parts_ref, turned, ready, sems, in_sems):
        weights = matrix_ref[...]

        def fetch(chunk):
            p, h = chunk // halves, chunk % halves
            here = (p, pl.ds(8 * h, 8))
            return pltpu.make_async_copy(parts_in.at[here], parts_ref.at[here], in_sems.at[chunk])

        for chunk in range(px * halves):
            fetch(chunk).start()

        def copy(chunk):
            p, h = chunk // halves, chunk % halves
            return pltpu.make_async_copy(ready.at[chunk], out_ref.at[:, p, pl.ds(8 * h, 8), :], sems.at[chunk])

        def step(chunk, carry):
            p, h = chunk // halves, chunk % halves
            fetch(chunk).wait()
            for y in range(8):
                out = jnp.dot(weights, parts_ref[p, 8 * h + y], preferred_element_type=f32)
                turned[y] = out[:V] + out[V:]
            ready[chunk] = jnp.swapaxes(turned[...], 0, 1)
            copy(chunk).start()
            return carry

        lax.fori_loop(0, px * halves, step, 0)
        for chunk in range(px * halves):
            copy(chunk).wait()

    return call(
        body,
        (((V, px, py, cz), f32, ANY),),
        ((parts, pltpu.HBM), (matrix, VMEM)),
        (
            pltpu.VMEM((px, py, A, cz), bf16),
            pltpu.VMEM((8, V, cz), f32),
            pltpu.VMEM((px * halves, V, 8, cz), f32),
            pltpu.SemaphoreType.DMA((px * halves,)),
            pltpu.SemaphoreType.DMA((px * halves,)),
        ),
        20,
    )[0]


def per_device(labels, start):
    px, py, cz = labels.shape
    cells_total = labels.size * lax.axis_size(PLANE) * lax.axis_size("depth")
    fields, *edges = read_start(start.reshape((S, px, py, cz)), px, py, cz)
    edges = exchange(*edges)
    start_gram = start_products(fields, px, py)
    lifted, *ends = first_lift(labels, fields, start_gram, edges, px, py, cz)
    ends = exchange(*ends)
    halves, middle_gram = lifted_products(fields, lifted, px, py, cz)
    parts, packed = second_lift(labels, fields, lifted, ends, halves, (start_gram, middle_gram), px, py, cz)
    matrix, turned = algebra(sum_all(packed), cells_total)
    return (write_basis(parts, matrix, px, py, cz), jnp.swapaxes(turned, 1, 2))


def solution(mesh):
    finer = Mesh(
        mesh.devices.reshape(4, 8, 2, mesh.shape["depth"]),
        ("plane_0", "plane_1", "plane_2", "depth"),
    )
    return jax.shard_map(
        per_device,
        mesh=finer,
        in_specs=(P(PLANE, "depth", None), P(None, None, PLANE, "depth", None)),
        out_specs=(P(None, PLANE, "depth", None), P()),
        check_vma=False,
    )
```

time: 122 us -> 103 us (0.84)
  waiting for transfers between devices: 16.4 us -> 9.04 us
  Pallas kernels: 37.3 us -> 30.2 us
  blocking collectives: 41.1 us -> 37.4 us
  local copies, waits for them, and re-layouts: 5.81 us -> 3.22 us
  starting transfers between devices: 20.2 us -> 22.2 us
    all_to_all x2, blocking collectives: 41.1 us -> 30.4 us  [sum_over(): return jnp.sum(lax.all_to_all(copies, axes, 0, 0, tiled=True), axis=0)]
    ppermute x8, waiting for transfers between devices: 16.4 us -> 9.04 us  [shift(): return lax.ppermute(edge, axis, pairs)]
    pallas_call x5 -> x7, Pallas kernels: 37.3 us -> 30.2 us  [call(): pl.pallas_call(body, out_shape=tuple(shapes), in_specs=specs, out_specs=t...]
    all_gather x0 -> x2, blocking collectives: none -> 7.07 us  [the longest x1 5.24 us: sum_all(): return lax.all_gather(own, 'plane_2', tiled=True)]
    unnamed x7 -> x9, local copies, waits for them, and re-layouts: 5.75 us -> 3.2 us
    ppermute x8, starting transfers between devices: 20.2 us -> 22.2 us  [shift(): return lax.ppermute(edge, axis, pairs)]
  transfers between devices with their start and end apart: 8 -> 8, of which waited for: 5 -> 5; matrix products, arithmetic and copies ran while one was open for 0% -> 0% of each run, Pallas kernels for 0% -> 3%
where the time goes in v1:
time: 103 us
  blocking collectives  37.4 us (36%)
  Pallas kernels  30.2 us (29%)
  starting transfers between devices  22.2 us (22%)
  waiting for transfers between devices  9.04 us (9%)
  local copies, waits for them, and re-layouts  3.22 us (3%)
    all_to_all x2, blocking collectives, sum_over(): return jnp.sum(lax.all_to_all(copies, axes, 0, 0, tiled=True), axis=0)  30.4 us
    pallas_call x7, Pallas kernels, call(): pl.pallas_call(body, out_shape=tuple(shapes), in_specs=specs, out_specs=t...  30.2 us
    ppermute x8, starting transfers between devices, shift(): return lax.ppermute(edge, axis, pairs)  22.2 us
    ppermute x8, waiting for transfers between devices, shift(): return lax.ppermute(edge, axis, pairs)  9.04 us
    all_gather x1, blocking collectives, sum_all(): return lax.all_gather(own, 'plane_2', tiled=True)  5.24 us
    unnamed x9, local copies, waits for them, and re-layouts  3.2 us
  transfers between devices with their start and end apart: 8, of which 5 were waited for; matrix products, arithmetic and copies ran while one was open for 0% of the time, Pallas kernels for 3%

profile of v1, /device:TPU:1, one launch (start us, length us, event | category | flops | bytes accessed | tf_op | source)
XLA Modules:
  0.0 103.0 jit_solution(5695813120398665295)
XLA Ops:
  0.6 0.0 copy-start.3
  0.6 2.7 %shard_map.41 = (bf16[4,16,48,384]{3,2,1,0:T(8,128)(2,1)S(1)}, f32[16,32,384]{2,1,0:T(8,128)S(1)}, f32[16,32,384]{2,1,0:T(8,128)S(1)}, f32[4,32,384]{2,1,0:T(8,128)S(1)}, f32[4,32,384]{2,1,0:T(8,128)S(1)}) custom-call(s32[48,4,16,384]{3,2,1,0:T(8,128)} %bitcast.4), custom_call_target="tpu_custom_call" | custom-call | tf_op jit(solution)/shard_map/pallas_call | solution.py:63
  3.3 4.9 %collective-permute-start = (f32[16,32,384]{2,1,0:T(8,128)S(1)}, f32[16,32,384]{2,1,0:T(8,128)S(1)}, u32[]{:S(2)}, u32[]{:S(2)}) collective-permute-start(f32[16,32,384]{2,1,0:T(8,128)S(1)} %get-tuple-element.19), channel_id=1, source_target_pairs={{0,4},{4,8},{8,12},{12,16},{16,20},{20,24},{24,28},{28,32},{32,36}... | collective-permute-start | bytes 2359304 | tf_op jit(solution)/shard_map/ppermute | solution.py:46
  8.3 1.9 %collective-permute-start.1 = (f32[16,32,384]{2,1,0:T(8,128)S(1)}, f32[16,32,384]{2,1,0:T(8,128)S(1)}, u32[]{:S(2)}, u32[]{:S(2)}) collective-permute-start(f32[16,32,384]{2,1,0:T(8,128)S(1)} %get-tuple-element.20), channel_id=1, source_target_pairs={{4,0},{8,4},{12,8},{16,12},{20,16},{24,20},{28,24},{32,28},{36,32}... | collective-permute-start | bytes 2359304 | tf_op jit(solution)/shard_map/ppermute | solution.py:46
  10.2 3.2 %collective-permute-start.2 = (f32[4,32,384]{2,1,0:T(8,128)S(1)}, f32[4,32,384]{2,1,0:T(8,128)S(1)}, u32[]{:S(2)}, u32[]{:S(2)}) collective-permute-start(f32[4,32,384]{2,1,0:T(8,128)S(1)} %get-tuple-element.21), channel_id=1, source_target_pairs={{0,1},{1,2},{2,3},{4,5},{5,6},{6,7},{8,9},{9,10},{10,11},{12,13},{... | collective-permute-start | bytes 589832 | tf_op jit(solution)/shard_map/ppermute | solution.py:46
  13.4 1.3 %collective-permute-start.3 = (f32[4,32,384]{2,1,0:T(8,128)S(1)}, f32[4,32,384]{2,1,0:T(8,128)S(1)}, u32[]{:S(2)}, u32[]{:S(2)}) collective-permute-start(f32[4,32,384]{2,1,0:T(8,128)S(1)} %get-tuple-element.22), channel_id=1, source_target_pairs={{1,0},{2,1},{3,2},{5,4},{6,5},{7,6},{9,8},{10,9},{11,10},{13,12},{... | collective-permute-start | bytes 589832 | tf_op jit(solution)/shard_map/ppermute | solution.py:46
  14.7 1.3 %shard_map.42.gram_ref.start_ref = f32[48,48]{1,0:T(8,128)S(1)} custom-call(bf16[4,16,48,384]{3,2,1,0:T(8,128)(2,1)S(1)} %get-tuple-element.18.fields_ref), custom_call_target="tpu_custom_call" | custom-call | flops 1000000000 | tf_op jit(solution)/shard_map/pallas_call | solution.py:63
  16.0 0.3 collective-permute-done.2.before
  16.3 4.1 %collective-permute-done.3.behind = f32[4,32,384]{2,1,0:T(8,128)S(1)} collective-permute-done((f32[4,32,384]{2,1,0:T(8,128)S(1)}, f32[4,32,384]{2,1,0:T(8,128)S(1)}, u32[]{:S(2)}, u32[]{:S(2)}) %collective-permute-start.3) | collective-permute-done | bytes 196640 | tf_op jit(solution)/shard_map/ppermute | solution.py:46
  20.4 0.0 collective-permute-done.below
  20.4 1.2 %collective-permute-done.1.above = f32[16,32,384]{2,1,0:T(8,128)S(1)} collective-permute-done((f32[16,32,384]{2,1,0:T(8,128)S(1)}, f32[16,32,384]{2,1,0:T(8,128)S(1)}, u32[]{:S(2)}, u32[]{:S(2)}) %collective-permute-start.1) | collective-permute-done | bytes 786464 | tf_op jit(solution)/shard_map/ppermute | solution.py:46
  21.6 0.0 copy-done.3
  21.6 3.6 %shard_map.43 = (f32[4,16,16,384]{3,2,1,0:T(8,128)S(1)}, f32[16,32,384]{2,1,0:T(8,128)}, f32[16,32,384]{2,1,0:T(8,128)}, f32[4,32,384]{2,1,0:T(8,128)}, f32[4,32,384]{2,1,0:T(8,128)}) custom-call(s32[4,16,384]{2,1,0:T(8,128)S(1)} %copy-done.3, bf16[4,16,48,384]{3,2,1,0:T(8,128)(2,1)S(1)} %get-tuple-element.18.fields_ref, ...), custom_call_target="tpu_custom_call" | custom-call | tf_op jit(solution)/shard_map/pallas_call | solution.py:63
  25.1 0.0 copy-start
  25.1 1.1 %copy-done = f32[4,16,16,384]{3,2,1,0:T(8,128)} copy-done((f32[4,16,16,384]{3,2,1,0:T(8,128)}, f32[4,16,16,384]{3,2,1,0:T(8,128)S(1)}, u32[]{:S(2)}) %copy-start) | copy-done | bytes 1572888
  26.3 4.5 %collective-permute-start.4 = (f32[16,32,384]{2,1,0:T(8,128)}, f32[16,32,384]{2,1,0:T(8,128)S(1)}, u32[]{:S(2)}, u32[]{:S(2)}) collective-permute-start(f32[16,32,384]{2,1,0:T(8,128)} %get-tuple-element.26), channel_id=1, source_target_pairs={{0,4},{4,8},{8,12},{12,16},{16,20},{20,24},{24,28},{28,32},{32,36}... | collective-permute-start | bytes 2359304 | tf_op jit(solution)/shard_map/ppermute | solution.py:46
  30.8 1.9 %collective-permute-start.5 = (f32[16,32,384]{2,1,0:T(8,128)}, f32[16,32,384]{2,1,0:T(8,128)}, u32[]{:S(2)}, u32[]{:S(2)}) collective-permute-start(f32[16,32,384]{2,1,0:T(8,128)} %get-tuple-element.27), channel_id=1, source_target_pairs={{4,0},{8,4},{12,8},{16,12},{20,16},{24,20},{28,24},{32,28},{36,32}... | collective-permute-start | bytes 2359304 | tf_op jit(solution)/shard_map/ppermute | solution.py:46
  32.7 3.2 %collective-permute-start.6 = (f32[4,32,384]{2,1,0:T(8,128)}, f32[4,32,384]{2,1,0:T(8,128)S(1)}, u32[]{:S(2)}, u32[]{:S(2)}) collective-permute-start(f32[4,32,384]{2,1,0:T(8,128)} %get-tuple-element.28), channel_id=1, source_target_pairs={{0,1},{1,2},{2,3},{4,5},{5,6},{6,7},{8,9},{9,10},{10,11},{12,13},{... | collective-permute-start | bytes 589832 | tf_op jit(solution)/shard_map/ppermute | solution.py:46
  35.9 1.3 %collective-permute-start.7 = (f32[4,32,384]{2,1,0:T(8,128)}, f32[4,32,384]{2,1,0:T(8,128)}, u32[]{:S(2)}, u32[]{:S(2)}) collective-permute-start(f32[4,32,384]{2,1,0:T(8,128)} %get-tuple-element.29), channel_id=1, source_target_pairs={{1,0},{2,1},{3,2},{5,4},{6,5},{7,6},{9,8},{10,9},{11,10},{13,12},{... | collective-permute-start | bytes 589832 | tf_op jit(solution)/shard_map/ppermute | solution.py:46
  37.2 0.0 copy-start.1
  37.2 1.4 %copy-done.1 = f32[4,16,16,384]{3,2,1,0:T(8,128)S(1)} copy-done((f32[4,16,16,384]{3,2,1,0:T(8,128)S(1)}, f32[4,16,16,384]{3,2,1,0:T(8,128)}, u32[]{:S(2)}) %copy-start.1) | copy-done | bytes 1572888
  38.6 0.0 copy-start.2
  38.6 2.3 %shard_map.44 = (bf16[4,16,32,384]{3,2,1,0:T(8,128)(2,1)S(1)}, f32[80,32]{1,0:T(8,128)S(1)}) custom-call(bf16[4,16,48,384]{3,2,1,0:T(8,128)(2,1)S(1)} %get-tuple-element.18.fields_ref, f32[4,16,16,384]{3,2,1,0:T(8,128)S(1)} %copy-done.1), custom_call_target="tpu_custom_call" | custom-call | flops 1000000000 | tf_op jit(solution)/shard_map/pallas_call | solution.py:63
  40.9 0.0 collective-permute-done.6.refs_2_
  41.0 1.9 %collective-permute-done.7.refs_3_ = f32[4,32,384]{2,1,0:T(8,128)} collective-permute-done((f32[4,32,384]{2,1,0:T(8,128)}, f32[4,32,384]{2,1,0:T(8,128)}, u32[]{:S(2)}, u32[]{:S(2)}) %collective-permute-start.7) | collective-permute-done | bytes 196640 | tf_op jit(solution)/shard_map/ppermute | solution.py:46
  42.8 0.0 collective-permute-done.4.refs_0_
  42.8 1.6 %collective-permute-done.5.refs_1_ = f32[16,32,384]{2,1,0:T(8,128)} collective-permute-done((f32[16,32,384]{2,1,0:T(8,128)}, f32[16,32,384]{2,1,0:T(8,128)}, u32[]{:S(2)}, u32[]{:S(2)}) %collective-permute-start.5) | collective-permute-done | bytes 786464 | tf_op jit(solution)/shard_map/ppermute | solution.py:46
  44.4 0.0 copy-done.2
  44.4 6.8 %shard_map.45 = (bf16[4,16,112,384]{3,2,1,0:T(8,128)(2,1)}, f32[32,128]{1,0:T(8,128)S(1)}) custom-call(s32[4,16,384]{2,1,0:T(8,128)S(1)} %copy-done.3, bf16[4,16,48,384]{3,2,1,0:T(8,128)(2,1)S(1)} %get-tuple-element.18.fields_ref, f32[4,16,16,384]{3,2,1,0:T(8,128)S(1)} %copy-done.2, bf16[4,16,32,384]{3,2,1,0:T(8,128)(2,1)S(1)} %get-tuple-element.24.halves_ref, ...), custom_call_target="tpu_custom_call" | custom-call | tf_op jit(solution)/shard_map/pallas_call | solution.py:63
  51.2 1.8 %all-gather = f32[64,128]{1,0:T(8,128)S(1)} all-gather(f32[32,128]{1,0:T(8,128)S(1)} %get-tuple-element.31), channel_id=2, replica_groups=mesh['plane_0'=4,'plane_1'=8,'plane_2'=2,'depth'=4] {'plane_2'}, dimensions={0}, use_global_device_ids=true | all-gather | bytes 49152 | tf_op jit(solution)/shard_map/all_gather | solution.py:37
  53.1 22.3 %all_to_all.10 = f32[32,16,128]{2,1,0:T(8,128)S(1)} all-to-all(f32[32,16,128]{2,1,0:T(8,128)S(1)} %broadcast_in_dim.4), channel_id=1, replica_groups=mesh['plane_0'=4,'plane_1'=8,'plane_2'=2,'depth'=4] {'plane_1','depth'}, dimensions={0} | all-to-all | bytes 524288 | tf_op jit(solution)/shard_map/all_to_all | solution.py:33
  75.4 8.1 %all_to_all.11 = f32[4,16,128]{2,1,0:T(8,128)S(1)} all-to-all(f32[4,16,128]{2,1,0:T(8,128)S(1)} %broadcast_in_dim.5), channel_id=1, replica_groups=mesh['plane_0'=4,'plane_1'=8,'plane_2'=2,'depth'=4] {'plane_0'}, dimensions={0} | all-to-all | bytes 65536 | tf_op jit(solution)/shard_map/all_to_all | solution.py:33
  83.5 5.2 %all_gather.11.packed_ref = f32[32,128]{1,0:T(8,128)S(1)} all-gather(f32[16,128]{1,0:T(8,128)S(1)} %reduce_sum.29), channel_id=1, replica_groups=mesh['plane_0'=4,'plane_1'=8,'plane_2'=2,'depth'=4] {'plane_2'}, dimensions={0}, use_global_device_ids=true | all-gather | bytes 24576 | tf_op jit(solution)/shard_map/all_gather | solution.py:40
  88.7 7.1 %shard_map.46 = (bf16[160,112]{1,0:T(8,128)(2,1)S(1)}, f32[3,48,80]{2,1,0:T(8,128)S(1)}) custom-call(f32[32,128]{1,0:T(8,128)S(1)} %all_gather.11.packed_ref), custom_call_target="tpu_custom_call" | custom-call | tf_op jit(solution)/shard_map/pallas_call | solution.py:63
  95.8 0.6 copy.4
  96.5 6.5 %shard_map.47 = f32[80,4,16,384]{3,2,1,0:T(8,128)} custom-call(bf16[4,16,112,384]{3,2,1,0:T(8,128)(2,1)} %get-tuple-element.30.parts_in, bf16[160,112]{1,0:T(8,128)(2,1)S(1)} %get-tuple-element.32.matrix_ref), custom_call_target="tpu_custom_call" | custom-call | tf_op jit(solution)/shard_map/pallas_call | solution.py:63
  (6 shorter events, 0.1 us)
Async XLA Ops:
  0.6 20.9 %copy-start.3 = (s32[4,16,384]{2,1,0:T(8,128)S(1)}, s32[4,16,384]{2,1,0:T(8,128)}, u32[]{:S(2)}) copy-start(s32[4,16,384]{2,1,0:T(8,128)} %labels_ref.3) | copy-start | bytes 294916
  3.3 17.1 %collective-permute-start = (f32[16,32,384]{2,1,0:T(8,128)S(1)}, f32[16,32,384]{2,1,0:T(8,128)S(1)}, u32[]{:S(2)}, u32[]{:S(2)}) collective-permute-start(f32[16,32,384]{2,1,0:T(8,128)S(1)} %get-tuple-element.19), channel_id=1, source_target_pairs={{0,4},{4,8},{8,12},{12,16},{16,20},{20,24},{24,28},{28,32},{32,36}... | collective-permute-start | bytes 2359304 | tf_op jit(solution)/shard_map/ppermute | solution.py:46
  8.3 13.3 %collective-permute-start.1 = (f32[16,32,384]{2,1,0:T(8,128)S(1)}, f32[16,32,384]{2,1,0:T(8,128)S(1)}, u32[]{:S(2)}, u32[]{:S(2)}) collective-permute-start(f32[16,32,384]{2,1,0:T(8,128)S(1)} %get-tuple-element.20), channel_id=1, source_target_pairs={{4,0},{8,4},{12,8},{16,12},{20,16},{24,20},{28,24},{32,28},{36,32}... | collective-permute-start | bytes 2359304 | tf_op jit(solution)/shard_map/ppermute | solution.py:46
  10.2 6.1 %collective-permute-start.2 = (f32[4,32,384]{2,1,0:T(8,128)S(1)}, f32[4,32,384]{2,1,0:T(8,128)S(1)}, u32[]{:S(2)}, u32[]{:S(2)}) collective-permute-start(f32[4,32,384]{2,1,0:T(8,128)S(1)} %get-tuple-element.21), channel_id=1, source_target_pairs={{0,1},{1,2},{2,3},{4,5},{5,6},{6,7},{8,9},{9,10},{10,11},{12,13},{... | collective-permute-start | bytes 589832 | tf_op jit(solution)/shard_map/ppermute | solution.py:46
  13.4 7.0 %collective-permute-start.3 = (f32[4,32,384]{2,1,0:T(8,128)S(1)}, f32[4,32,384]{2,1,0:T(8,128)S(1)}, u32[]{:S(2)}, u32[]{:S(2)}) collective-permute-start(f32[4,32,384]{2,1,0:T(8,128)S(1)} %get-tuple-element.22), channel_id=1, source_target_pairs={{1,0},{2,1},{3,2},{5,4},{6,5},{7,6},{9,8},{10,9},{11,10},{13,12},{... | collective-permute-start | bytes 589832 | tf_op jit(solution)/shard_map/ppermute | solution.py:46
  25.1 1.1 %copy-start = (f32[4,16,16,384]{3,2,1,0:T(8,128)}, f32[4,16,16,384]{3,2,1,0:T(8,128)S(1)}, u32[]{:S(2)}) copy-start(f32[4,16,16,384]{3,2,1,0:T(8,128)S(1)} %get-tuple-element.23.lifted_ref) | copy-start | bytes 4718596
  26.3 16.6 %collective-permute-start.4 = (f32[16,32,384]{2,1,0:T(8,128)}, f32[16,32,384]{2,1,0:T(8,128)S(1)}, u32[]{:S(2)}, u32[]{:S(2)}) collective-permute-start(f32[16,32,384]{2,1,0:T(8,128)} %get-tuple-element.26), channel_id=1, source_target_pairs={{0,4},{4,8},{8,12},{12,16},{16,20},{20,24},{24,28},{28,32},{32,36}... | collective-permute-start | bytes 2359304 | tf_op jit(solution)/shard_map/ppermute | solution.py:46
  30.8 13.6 %collective-permute-start.5 = (f32[16,32,384]{2,1,0:T(8,128)}, f32[16,32,384]{2,1,0:T(8,128)}, u32[]{:S(2)}, u32[]{:S(2)}) collective-permute-start(f32[16,32,384]{2,1,0:T(8,128)} %get-tuple-element.27), channel_id=1, source_target_pairs={{4,0},{8,4},{12,8},{16,12},{20,16},{24,20},{28,24},{32,28},{36,32}... | collective-permute-start | bytes 2359304 | tf_op jit(solution)/shard_map/ppermute | solution.py:46
  32.7 8.2 %collective-permute-start.6 = (f32[4,32,384]{2,1,0:T(8,128)}, f32[4,32,384]{2,1,0:T(8,128)S(1)}, u32[]{:S(2)}, u32[]{:S(2)}) collective-permute-start(f32[4,32,384]{2,1,0:T(8,128)} %get-tuple-element.28), channel_id=1, source_target_pairs={{0,1},{1,2},{2,3},{4,5},{5,6},{6,7},{8,9},{9,10},{10,11},{12,13},{... | collective-permute-start | bytes 589832 | tf_op jit(solution)/shard_map/ppermute | solution.py:46
  35.9 6.9 %collective-permute-start.7 = (f32[4,32,384]{2,1,0:T(8,128)}, f32[4,32,384]{2,1,0:T(8,128)}, u32[]{:S(2)}, u32[]{:S(2)}) collective-permute-start(f32[4,32,384]{2,1,0:T(8,128)} %get-tuple-element.29), channel_id=1, source_target_pairs={{1,0},{2,1},{3,2},{5,4},{6,5},{7,6},{9,8},{10,9},{11,10},{13,12},{... | collective-permute-start | bytes 589832 | tf_op jit(solution)/shard_map/ppermute | solution.py:46
  37.2 1.4 %copy-start.1 = (f32[4,16,16,384]{3,2,1,0:T(8,128)S(1)}, f32[4,16,16,384]{3,2,1,0:T(8,128)}, u32[]{:S(2)}) copy-start(f32[4,16,16,384]{3,2,1,0:T(8,128)} %copy-done) | copy-start | bytes 4718596
  38.6 5.8 %copy-start.2 = (f32[4,16,16,384]{3,2,1,0:T(8,128)S(1)}, f32[4,16,16,384]{3,2,1,0:T(8,128)}, u32[]{:S(2)}) copy-start(f32[4,16,16,384]{3,2,1,0:T(8,128)} %copy-done) | copy-start | bytes 4718596

commit v2 on v1

v2 whole, which is shorter than its diff:
```python
import itertools

import jax
import jax.numpy as jnp
from jax import lax
from jax.experimental import pallas as pl
from jax.experimental.pallas import tpu as pltpu
from jax.sharding import Mesh
from jax.sharding import PartitionSpec as P

PLANE = ("plane_0", "plane_1", "plane_2")
WIDE = ("plane_1", "depth")
NARROW = ("plane_0", "plane_2")
B = 16
S = 3 * B
V = 5 * B
A = V + 2 * B
GROUP = 8

f32 = jnp.float32
bf16 = jnp.bfloat16
highest = lax.Precision.HIGHEST
permittivity_table = (1.0, 2.5, 4.0, 6.5)
damping_table = (0.3, 1.2, 0.05, 2.0)
outer_table = (1.0, 0.5, 2.0, 0.8)
inner_table = (1.0, 3.0, 0.6, 1.5)
CHAIN = ((0, 3, 4), (1, 0, 3), (2, 1, 0))
BLOCKS = [(i, j) for j in range(5) for i in range(j + 1)]

VMEM = pltpu.VMEM
ANY = pl.ANY


def parities():
    return lax.axis_index("plane_2"), lax.axis_index("depth") % 2


def spread(pieces, copies, halved=False):
    def body(pieces_ref, out_ref):
        total = pieces_ref[0]
        for i in range(1, pieces.shape[0]):
            total = total + pieces_ref[i]
        if halved:
            total = jnp.where(parities()[0] == 0, total[:B], total[B:])
        for i in range(copies):
            out_ref[i] = total

    return call(body, (((copies, B, 128), f32, VMEM),), ((pieces, VMEM),), limit=4)[0]


def sum_all(table):
    both = lax.all_gather(table, "plane_2")
    own = spread(both, lax.axis_size(WIDE), True)
    own = spread(lax.all_to_all(own, WIDE, 0, 0, tiled=True), lax.axis_size(NARROW))
    return lax.all_to_all(own, NARROW, 0, 0, tiled=True)


def swap(edge, axis, first):
    peers = lax.axis_size(axis)
    pairs = [(i, i + 1) for i in range(first, peers - 1, 2)]
    return lax.ppermute(edge, axis, pairs + [(b, a) for a, b in pairs])


def exchange(plane_even, plane_odd, row_even, row_odd):
    out = []
    for edge, axis, first in (
        (plane_even, PLANE, 0), (plane_odd, PLANE, 1), (row_even, "depth", 0), (row_odd, "depth", 1)
    ):
        out.append(swap(edge, axis, first))
    return tuple(out)


def call(body, outs, operands, scratch=(), limit=16, work=0):
    specs, shapes, results = [], [], []
    for operand, space in operands:
        specs.append(pl.BlockSpec(memory_space=space))
        results.append(operand if space is pl.ANY else pltpu.with_memory_space_constraint(operand, space))
    out_specs = []
    for shape, kind, space in outs:
        out_specs.append(pl.BlockSpec(memory_space=space))
        shapes.append(jax.ShapeDtypeStruct(shape, kind) if space is pl.ANY else space(shape, kind))
    return pl.pallas_call(
        body,
        out_shape=tuple(shapes),
        in_specs=specs,
        out_specs=tuple(out_specs),
        scratch_shapes=list(scratch),
        cost_estimate=pl.CostEstimate(flops=work, bytes_accessed=0, transcendentals=0),
        compiler_params=pltpu.CompilerParams(vmem_limit_bytes=limit * 2**20),
    )(*results)


def sweep(px, py, step):
    group = next(count for count in (7, 6, 5, 4, 3, 2, 1) if (py - 2) % count == 0)
    for p in range(px):
        step(p, 0)

        def several(j, carry):
            for i in range(group):
                step(p, 1 + group * j + i)
            return carry

        lax.fori_loop(0, (py - 2) // group, several, 0)
        step(p, py - 1)


def read_start(labels, start, px, py, cz):
    halves = py // 8

    def body(labels_in, start_ref, fields_ref, coefs, plane_even, plane_odd, row_even, row_odd, raw, labels_ref, sems, labels_sem):
        q, r = parities()
        fetch = pltpu.make_async_copy(labels_in, labels_ref, labels_sem)

        def copy(chunk):
            p, h = chunk // halves, chunk % halves
            return pltpu.make_async_copy(start_ref.at[:, p, pl.ds(8 * h, 8), :], raw.at[chunk], sems.at[chunk])

        for chunk in range(px * halves):
            copy(chunk).start()
        fetch.start()

        def step(chunk, carry):
            copy(chunk).wait()
            p, h = chunk // halves, chunk % halves
            rows = pl.multiple_of(8 * h, 8)
            turned = jnp.swapaxes(raw[chunk].astype(f32), 0, 1)
            sent = jnp.concatenate([turned[:, :B], turned[:, 2 * B :]], 1)
            fields_ref[p, pl.ds(rows, 8)] = turned.astype(bf16)

            @pl.when(p == (1 - q) * (px - 1))
            def _():
                plane_even[pl.ds(rows, 8)] = sent

            @pl.when(p == q * (px - 1))
            def _():
                plane_odd[pl.ds(rows, 8)] = sent

            edge = jnp.where(h == 0, sent[0], sent[7])

            @pl.when(h == (1 - r) * (halves - 1))
            def _():
                row_even[p] = edge

            @pl.when(h == r * (halves - 1))
            def _():
                row_odd[p] = edge

            return carry

        lax.fori_loop(0, px * halves, step, 0)
        fetch.wait()
        for p in range(px):
            for which, table in enumerate((outer_table, damping_table, inner_table)):
                coefs[which, p] = coef(labels_ref[p], table)
        plane_even[py, :py] = labels_ref[(1 - q) * (px - 1)].astype(f32)
        plane_odd[py, :py] = labels_ref[q * (px - 1)].astype(f32)
        for p in range(px):
            row_even[px, p : p + 1] = labels_ref[p, pl.ds((1 - r) * (py - 1), 1), :].astype(f32)
            row_odd[px, p : p + 1] = labels_ref[p, pl.ds(r * (py - 1), 1), :].astype(f32)

    plane, row = ((py + 1, 2 * B, cz), f32, VMEM), ((px + 1, 2 * B, cz), f32, VMEM)
    return call(
        body,
        (((px, py, S, cz), bf16, VMEM), ((3, px, py, cz), f32, VMEM), plane, plane, row, row),
        ((labels, pltpu.HBM), (start, pltpu.HBM)),
        (
            pltpu.VMEM((px * halves, S, 8, cz), jnp.int32),
            pltpu.VMEM((px, py, cz), jnp.int32),
            pltpu.SemaphoreType.DMA((px * halves,)),
            pltpu.SemaphoreType.DMA,
        ),
    )


def outside(edges, p, y, px, py):
    plane_even, plane_odd, row_even, row_odd = edges
    q, r = parities()
    if p < 0:
        return jnp.where(q == 0, plane_odd[y], plane_even[y])
    if p == px:
        return jnp.where(q == 0, plane_even[y], plane_odd[y])
    if isinstance(y, int) and y < 0:
        return jnp.where(r == 0, row_odd[p], row_even[p])
    if isinstance(y, int) and y == py:
        return jnp.where(r == 0, row_even[p], row_odd[p])
    return None


def laplace(inside, p, y, at, px, py, cz, edges=None, edge_at=0):
    def get(p, y):
        if 0 <= p < px and (not isinstance(y, int) or 0 <= y < py):
            return [inside[p, y, at : at + B]]
        if edges is None:
            return []
        return [outside(edges, p, y, px, py)[edge_at : edge_at + B].astype(inside.dtype)]

    wide = get(p, y)[0].astype(f32)
    lane = lax.broadcasted_iota(jnp.int32, (B, cz), 1)
    left = jnp.where(lane == 0, 0.0, pltpu.roll(wide, 1, 1))
    right = jnp.where(lane == cz - 1, 0.0, pltpu.roll(wide, cz - 1, 1))
    beside, *others = get(p + 1, y) + get(p - 1, y) + get(p, y + 1) + get(p, y - 1)
    for other in others:
        beside = beside + other
    return 6.0 * wide - (beside.astype(f32) + (left + right))


def coef(labels, table):
    values = [-entry / eps for entry, eps in zip(table, permittivity_table)]
    result = jnp.full(labels.shape, values[0], f32)
    for region in range(1, 4):
        result = jnp.where(labels == region, values[region], result)
    return result


def first_lift(coefs, fields, gram, edges, px, py, cz):
    def body(coefs, fields_ref, gram_ref, *refs):
        around, (lifted, halves, plane_even, plane_odd, row_even, row_odd, theirs) = refs[:4], refs[4:]

        def step(p, y):
            outer, damping, inner = [coefs[k, p, pl.ds(y, 1), :] for k in range(3)]
            middle = fields_ref[p, y, B : 2 * B, :].astype(f32)
            out = (
                outer * laplace(fields_ref, p, y, 0, px, py, cz, around, 0)
                + damping * middle
                + inner * laplace(fields_ref, p, y, 2 * B, px, py, cz, around, B)
            )
            lifted[p, y] = out
            halves[p, y] = split(out)

        sweep(px, py, step)
        q, r = parities()

        for at, received in enumerate(around):
            labels = received[py if at < 2 else px, :py]
            theirs[at, 0], theirs[at, 1] = coef(labels, outer_table), coef(labels, inner_table)

        def edge(at, line, p, y):
            outer, inner = theirs[at, 0, line : line + 1, :], theirs[at, 1, line : line + 1, :]
            return outer * lifted[p, y] + inner * fields_ref[p, y, B : 2 * B, :].astype(f32)

        for y in range(py):
            plane_even[y] = edge(0, y, (1 - q) * (px - 1), y)
            plane_odd[y] = edge(1, y, q * (px - 1), y)
        for p in range(px):
            row_even[p] = edge(2, p, p, (1 - r) * (py - 1))
            row_odd[p] = edge(3, p, p, r * (py - 1))

    plane, row = ((py, B, cz), f32, VMEM), ((px, B, cz), f32, VMEM)
    return call(
        body,
        (((px, py, B, cz), f32, VMEM), ((px, py, 2 * B, cz), bf16, VMEM), plane, plane, row, row),
        ((coefs, VMEM), (fields, VMEM), (gram, ANY)) + tuple((edge, VMEM) for edge in edges),
        (pltpu.VMEM((4, 2, py, cz), f32),),
        4,
    )


def gram_loop(count, rows, left, right, shape):
    def step(j, total):
        lhs = jnp.concatenate([left(j * count + i) for i in range(count)], 1)
        rhs = jnp.concatenate([right(j * count + i) for i in range(count)], 1)
        return total + lax.dot_general(lhs, rhs, (((1,), (1,)), ((), ())), preferred_element_type=f32)

    return lax.fori_loop(0, rows // count, step, jnp.zeros(shape, f32))


def start_products(fields, px, py):
    def body(fields_ref, gram_ref):
        def row(r):
            return fields_ref[r // py, r % py]

        gram_ref[...] = gram_loop(16, px * py, row, row, (S, S))

    return call(body, (((S, S), f32, VMEM),), ((fields, VMEM),), limit=4, work=10**9)[0]


def split(values):
    high = values.astype(bf16)
    return jnp.concatenate([high, (values - high.astype(f32)).astype(bf16)], 0)


def lifted_products(fields, halves, px, py):
    def body(fields_ref, halves_ref, gram_ref):
        def both(r):
            return jnp.concatenate([fields_ref[r // py, r % py], halves_ref[r // py, r % py]], 0)

        def right(r):
            return halves_ref[r // py, r % py]

        gram_ref[...] = gram_loop(8, px * py, both, right, (S + 2 * B, 2 * B))

    return call(
        body,
        (((S + 2 * B, 2 * B), f32, VMEM),),
        ((fields, VMEM), (halves, VMEM)),
        limit=4,
        work=10**9,
    )[0]


def second_lift(coefs, fields, lifted, ends, halves, grams, px, py, cz):
    def body(coefs, fields_ref, lifted_ref, halves_ref, start_ref, middle_ref, *refs):
        end_refs, (parts, packed) = refs[:4], refs[4:]

        def step(p, y):
            outer, damping, inner = [coefs[k, p, pl.ds(y, 1), :] for k in range(3)]
            now = fields_ref[p, y]
            second = (
                outer * laplace(lifted_ref, p, y, 0, px, py, cz)
                + damping * now[:B].astype(f32)
                + inner * laplace(fields_ref, p, y, B, px, py, cz)
            )
            for other in ((p - 1, y), (p + 1, y), (p, y - 1), (p, y + 1)):
                received = outside(end_refs, *other, px, py)
                if received is not None:
                    second = second - received
            parts[p, y] = jnp.concatenate([now, halves_ref[p, y], split(second)], 0)

        def left(r):
            return parts[r // py, r % py]

        def right(r):
            return parts[r // py, r % py, S + 2 * B :]

        sweep(px, py, step)
        last = gram_loop(8, px * py, left, right, (A, 2 * B))
        last = jnp.concatenate([last, jnp.zeros((A, 128 - 2 * B), f32)], 1)
        last = last + pltpu.roll(last, 128 - B, 1)
        middle = jnp.concatenate([middle_ref[...], jnp.zeros((S + 2 * B, 128 - 2 * B), f32)], 1)
        middle = middle + pltpu.roll(middle, 128 - B, 1)
        middle = jnp.concatenate([middle[:S], middle[S : S + B] + middle[S + B :]], 0)
        last = jnp.concatenate([last[:S], last[S : S + B] + last[S + B : S + 2 * B], last[S + 2 * B : S + 3 * B] + last[S + 3 * B :]], 0)
        first = jnp.concatenate([start_ref[...], jnp.zeros((S, 128 - S), f32)], 1)
        lane = lax.broadcasted_iota(jnp.int32, (B, 128), 1)
        sums = [jnp.zeros((B, 128), f32)] * 2
        for at, (i, j) in enumerate(BLOCKS):
            source, column = (first, j) if j < 3 else ((middle, 0) if j == 3 else (last, 0))
            moved = pltpu.roll(source[B * i : B * i + B], (B * (at % 8 - column)) % 128, 1)
            kept = (lane >= B * (at % 8)) & (lane < B * (at % 8) + B)
            sums[at // 8] = jnp.where(kept, moved, sums[at // 8])
        packed[...] = jnp.concatenate(sums, 0)

    return call(
        body,
        (((px, py, A, cz), bf16, VMEM), ((2 * B, 128), f32, VMEM)),
        tuple((x, VMEM) for x in (coefs, fields, lifted, halves) + tuple(grams) + ends),
        limit=4,
    )


def eliminate(matrix, count, found):
    shape = (8, 128)
    lane = lax.broadcasted_iota(jnp.int32, shape, 1)
    sub = lax.broadcasted_iota(jnp.int32, shape, 0)
    tiles = [matrix[8 * j : 8 * j + 8] for j in range(count // 8)]
    right = [jnp.where(lane == sub + 8 * j, 1.0, 0.0) for j in range(count // 8)]
    upper, inverse = [], []

    def row(tile, s):
        return jnp.broadcast_to(tile[s : s + 1], shape)

    for k in range(0, count, GROUP):
        own, s = k // 8, k % 8
        cols = {
            j: [jnp.broadcast_to(tiles[j][:, k + i : k + i + 1], shape) for i in range(GROUP)]
            for j in range(own, count // 8)
        }
        inner = [[row(cols[own][i], s + n) for i in range(n + 1)] for n in range(GROUP)]
        rows = [row(tiles[own], s + n) for n in range(GROUP)]
        others = [row(right[own], s + n) for n in range(GROUP)]
        for i in range(GROUP):
            scale = lax.rsqrt(inner[i][i])
            rows[i], others[i] = rows[i] * scale, others[i] * scale
            factors = {n: inner[n][i] * scale for n in range(i + 1, GROUP)}
            for j in cols:
                cols[j][i] = cols[j][i] * scale
            for n, factor in factors.items():
                for m in range(i + 1, n + 1):
                    inner[n][m] = inner[n][m] - factor * factors[m]
                rows[n] = rows[n] - factor * rows[i]
                others[n] = others[n] - factor * others[i]
                for j in cols:
                    cols[j][n] = cols[j][n] - cols[j][i] * factor
        for i in range(GROUP):
            upper.append(rows[i][:1])
            inverse.append(others[i][:1])
        for j in cols:
            for i in range(GROUP):
                factor = cols[j][i]
                if j == own:
                    factor = jnp.where(sub >= s + GROUP, factor, 0.0)
                tiles[j] = tiles[j] - factor * rows[i]
                right[j] = right[j] - factor * others[i]
        yield
    lane = lax.broadcasted_iota(jnp.int32, (count, 128), 1)
    sub = lax.broadcasted_iota(jnp.int32, (count, 128), 0)
    upper = jnp.concatenate(upper, 0)
    found.append(jnp.where((lane >= sub) & (lane < count), upper, 0.0))
    found.append(jnp.concatenate(inverse, 0))


def factorize(*jobs):
    results = [[] for _ in jobs]
    running = [eliminate(matrix, count, found) for (matrix, count), found in zip(jobs, results)]
    for _ in itertools.zip_longest(*running):
        pass
    return results


def place(strip, origin, target):
    lane = lax.broadcasted_iota(jnp.int32, strip.shape, 1)
    moved = pltpu.roll(strip, (B * (target - origin)) % 128, 1) if target != origin else strip
    return jnp.where((lane >= B * target) & (lane < B * target + B), moved, 0.0)


def finish(packed, parts, cells_total, px, py, cz):
    halves = py // 8

    def body(packed_ref, parts_ref, out_ref, coords_out, turned, ready, coords_ref, sems, coords_sem):
        pieces = [packed_ref[i] for i in range(packed.shape[0])]
        sums = [sum(pieces[c::2][1:], pieces[c]) for c in range(2)]
        table = jnp.concatenate(sums, 0) * (1.0 / cells_total)
        rows = [jnp.zeros((B, 128), f32)] * 8
        for at, (i, j) in enumerate(BLOCKS):
            rows[i] = rows[i] + place(table[B * (at // 8) : B * (at // 8) + B], at % 8, j)
        square = jnp.concatenate(rows, 0)
        lane = lax.broadcasted_iota(jnp.int32, (128, 128), 1)
        sub = lax.broadcasted_iota(jnp.int32, (128, 128), 0)
        gram = jnp.where(lane // B >= sub // B, square, square.T)[:V]
        rows = []
        for i in range(3):
            total = jnp.zeros((B, 128), f32)
            for blocks in CHAIN:
                strip = gram[B * blocks[i] : B * blocks[i] + B]
                for j in range(3):
                    total = total + place(strip, blocks[j], j)
            rows.append(total)
        (upper, inverse), (_, small) = factorize((gram, V), (jnp.concatenate(rows, 0), S))
        lane = lax.broadcasted_iota(jnp.int32, (V, 128), 1)
        matrix = jnp.where(lane < S + B, inverse, 0.0)
        matrix = matrix + place(inverse, 3, 4) + place(inverse, 4, 5) + place(inverse, 4, 6)
        matrix = matrix[:, :A]
        high = matrix.astype(bf16)
        weights = jnp.concatenate([high, (matrix - high.astype(f32)).astype(bf16)], 0)

        def copy(chunk):
            p, h = chunk // halves, chunk % halves
            return pltpu.make_async_copy(ready.at[chunk], out_ref.at[:, p, pl.ds(8 * h, 8), :], sems.at[chunk])

        def step(chunk, carry):
            p, h = chunk // halves, chunk % halves
            for y in range(8):
                out = jnp.dot(weights, parts_ref[p, 8 * h + y], preferred_element_type=f32)
                turned[y] = out[:V] + out[V:]
            ready[chunk] = jnp.swapaxes(turned[...], 0, 1)
            copy(chunk).start()
            return carry

        lax.fori_loop(0, px * halves, step, 0)
        for i in range(3):
            chosen = place(small, 0, CHAIN[i][0]) + place(small, 1, CHAIN[i][1]) + place(small, 2, CHAIN[i][2])
            coords_ref[i] = lax.dot_general(
                chosen, upper, (((1,), (1,)), ((), ())), precision=highest, preferred_element_type=f32
            )
        whole = pltpu.make_async_copy(coords_ref, coords_out, coords_sem)
        whole.start()
        for chunk in range(px * halves):
            copy(chunk).wait()
        whole.wait()

    return call(
        body,
        (((V, px, py, cz), f32, ANY), ((3, S, V), f32, ANY)),
        ((packed, VMEM), (parts, VMEM)),
        (
            pltpu.VMEM((8, V, cz), f32),
            pltpu.VMEM((px * halves, V, 8, cz), f32),
            pltpu.VMEM((3, S, V), f32),
            pltpu.SemaphoreType.DMA((px * halves,)),
            pltpu.SemaphoreType.DMA,
        ),
        16,
    )


def steps(labels, start):
    px, py, cz = labels.shape
    cells_total = labels.size * lax.axis_size(PLANE) * lax.axis_size("depth")
    fields, coefs, *edges = read_start(labels, start.reshape((S, px, py, cz)), px, py, cz)
    edges = exchange(*edges)
    start_gram = start_products(fields, px, py)
    lifted, halves, *ends = first_lift(coefs, fields, start_gram, edges, px, py, cz)
    ends = exchange(*ends)
    middle_gram = lifted_products(fields, halves, px, py)
    parts, packed = second_lift(coefs, fields, lifted, ends, halves, (start_gram, middle_gram), px, py, cz)
    basis_cols, turned = finish(sum_all(packed), parts, cells_total, px, py, cz)
    return (basis_cols, jnp.swapaxes(turned, 1, 2))


def solution(mesh):
    finer = Mesh(
        mesh.devices.reshape(4, 8, 2, mesh.shape["depth"]),
        ("plane_0", "plane_1", "plane_2", "depth"),
    )
    return jax.shard_map(
        steps,
        mesh=finer,
        in_specs=(P(PLANE, "depth", None), P(None, None, PLANE, "depth", None)),
        out_specs=(P(None, PLANE, "depth", None), P()),
        check_vma=False,
    )
```

time: 103 us -> 83.9 us (0.81)
  starting transfers between devices: 22.2 us -> 11.7 us
  Pallas kernels: 30.2 us -> 23.2 us
  local copies, waits for them, and re-layouts: 3.22 us -> 0 us
  waiting for transfers between devices: 9.04 us -> 11 us
    ppermute x8, starting transfers between devices: 22.2 us -> 11.7 us  [swap(): return lax.ppermute(edge, axis, pairs + [(b, a) for a, b in pairs])]
    pallas_call x7 -> x8, Pallas kernels: 30.2 us -> 23.2 us  [call(): pl.pallas_call(body, out_shape=tuple(shapes), in_specs=specs, out_specs=t...]
    all_gather x2 -> x1, blocking collectives: 7.07 us -> 1.83 us  [sum_all(): both = lax.all_gather(table, 'plane_2')]
    all_to_all x2, blocking collectives: 30.4 us -> 35.1 us  [the longest x1 23.8 us: sum_all(): lax.all_to_all(own, WIDE, 0, 0, tiled=True)]
    unnamed x9 -> x0, local copies, waits for them, and re-layouts: 3.2 us -> none
    ppermute x8, waiting for transfers between devices: 9.04 us -> 11 us  [swap(): return lax.ppermute(edge, axis, pairs + [(b, a) for a, b in pairs])]
  transfers between devices with their start and end apart: 8 -> 8, of which waited for: 5 -> 3; matrix products, arithmetic and copies ran while one was open for 0% -> 0% of each run, Pallas kernels for 3% -> 4%
where the time goes in v2:
time: 83.9 us; the launch traced here: 83.6 us
  blocking collectives  36.9 us (44%)
  Pallas kernels  23.2 us (28%)
  starting transfers between devices  11.7 us (14%)
  waiting for transfers between devices  11 us (13%)
    all_to_all x1, blocking collectives, sum_all(): lax.all_to_all(own, WIDE, 0, 0, tiled=True)  23.8 us
    pallas_call x8, Pallas kernels, call(): pl.pallas_call(body, out_shape=tuple(shapes), in_specs=specs, out_specs=t...  23.2 us
    ppermute x8, starting transfers between devices, swap(): return lax.ppermute(edge, axis, pairs + [(b, a) for a, b in pairs])  11.7 us
    all_to_all x1, blocking collectives, sum_all(): return lax.all_to_all(own, NARROW, 0, 0, tiled=True)  11.3 us
    ppermute x8, waiting for transfers between devices, swap(): return lax.ppermute(edge, axis, pairs + [(b, a) for a, b in pairs])  11 us
    all_gather x1, blocking collectives, sum_all(): both = lax.all_gather(table, 'plane_2')  1.83 us
  transfers between devices with their start and end apart: 8, of which 3 were waited for; matrix products, arithmetic and copies ran while one was open for 0% of the time, Pallas kernels for 4%

profile of v2, /device:TPU:1, one launch (start us, length us, event | category | flops | bytes accessed | tf_op | source)
XLA Modules:
  0.0 83.6 jit_solution(7710851966597113162)
XLA Ops:
  0.6 2.7 %shard_map.41 = (bf16[4,16,48,384]{3,2,1,0:T(8,128)(2,1)S(1)}, f32[3,4,16,384]{3,2,1,0:T(8,128)S(1)}, f32[17,32,384]{2,1,0:T(8,128)S(1)}, f32[17,32,384]{2,1,0:T...) custom-call(s32[4,16,384]{2,1,0:T(8,128)} %labels_in.1, s32[48,4,16,384]{3,2,1,0:T(8,128)} %bitcast.4), custom_call_target="tpu_custom_call" | custom-call | tf_op jit(solution)/shard_map/pallas_call | solution.py:82
  3.4 3.3 %collective-permute-start = (f32[17,32,384]{2,1,0:T(8,128)S(1)}, f32[17,32,384]{2,1,0:T(8,128)S(1)}, u32[]{:S(2)}, u32[]{:S(2)}) collective-permute-start(f32[17,32,384]{2,1,0:T(8,128)S(1)} %get-tuple-element.20), channel_id=1, source_target_pairs={{0,4},{8,12},{16,20},{24,28},{32,36},{40,44},{48,52},{56,60},{64,6... | collective-permute-start | bytes 2506760 | tf_op jit(solution)/shard_map/ppermute | solution.py:61
  6.7 1.9 %collective-permute-start.1 = (f32[17,32,384]{2,1,0:T(8,128)S(1)}, f32[17,32,384]{2,1,0:T(8,128)S(1)}, u32[]{:S(2)}, u32[]{:S(2)}) collective-permute-start(f32[17,32,384]{2,1,0:T(8,128)S(1)} %get-tuple-element.21), channel_id=1, source_target_pairs={{4,8},{12,16},{20,24},{28,32},{36,40},{44,48},{52,56},{60,64},{68,... | collective-permute-start | bytes 2506760 | tf_op jit(solution)/shard_map/ppermute | solution.py:61
  8.6 1.2 %collective-permute-start.2 = (f32[5,32,384]{2,1,0:T(8,128)S(1)}, f32[5,32,384]{2,1,0:T(8,128)S(1)}, u32[]{:S(2)}, u32[]{:S(2)}) collective-permute-start(f32[5,32,384]{2,1,0:T(8,128)S(1)} %get-tuple-element.22), channel_id=1, source_target_pairs={{0,1},{2,3},{1,0},{3,2},{4,5},{6,7},{5,4},{7,6},{8,9},{10,11},{9,8... | collective-permute-start | bytes 737288 | tf_op jit(solution)/shard_map/ppermute | solution.py:61
  9.8 0.7 collective-permute-start.3
  10.5 1.3 %shard_map.42.gram_ref.start_ref = f32[48,48]{1,0:T(8,128)S(1)} custom-call(bf16[4,16,48,384]{3,2,1,0:T(8,128)(2,1)S(1)} %get-tuple-element.19.fields_ref), custom_call_target="tpu_custom_call" | custom-call | flops 1000000000 | tf_op jit(solution)/shard_map/pallas_call | solution.py:82
  11.7 3.9 %collective-permute-done.2.refs_2_ = f32[5,32,384]{2,1,0:T(8,128)S(1)} collective-permute-done((f32[5,32,384]{2,1,0:T(8,128)S(1)}, f32[5,32,384]{2,1,0:T(8,128)S(1)}, u32[]{:S(2)}, u32[]{:S(2)}) %collective-permute-start.2) | collective-permute-done | bytes 245792 | tf_op jit(solution)/shard_map/ppermute | solution.py:61
  15.6 0.0 collective-permute-done.3.refs_3_
  15.6 0.0 collective-permute-done.refs_0_
  15.6 4.9 %collective-permute-done.1.refs_1_ = f32[17,32,384]{2,1,0:T(8,128)S(1)} collective-permute-done((f32[17,32,384]{2,1,0:T(8,128)S(1)}, f32[17,32,384]{2,1,0:T(8,128)S(1)}, u32[]{:S(2)}, u32[]{:S(2)}) %collective-permute-start.1) | collective-permute-done | bytes 835616 | tf_op jit(solution)/shard_map/ppermute | solution.py:61
  20.5 2.7 %shard_map.43 = (f32[4,16,16,384]{3,2,1,0:T(8,128)S(1)}, bf16[4,16,32,384]{3,2,1,0:T(8,128)(2,1)S(1)}, f32[16,16,384]{2,1,0:T(8,128)S(1)}, f32[16,16,384]{2,1,0:...) custom-call(f32[3,4,16,384]{3,2,1,0:T(8,128)S(1)} %get-tuple-element.18.coefs, ...), custom_call_target="tpu_custom_call" | custom-call | tf_op jit(solution)/shard_map/pallas_call | solution.py:82
  23.2 0.1 collective-permute-start.4
  23.3 2.2 %collective-permute-start.5 = (f32[16,16,384]{2,1,0:T(8,128)S(1)}, f32[16,16,384]{2,1,0:T(8,128)S(1)}, u32[]{:S(2)}, u32[]{:S(2)}) collective-permute-start(f32[16,16,384]{2,1,0:T(8,128)S(1)} %get-tuple-element.27), channel_id=1, source_target_pairs={{4,8},{12,16},{20,24},{28,32},{36,40},{44,48},{52,56},{60,64},{68,... | collective-permute-start | bytes 1179656 | tf_op jit(solution)/shard_map/ppermute | solution.py:61
  25.5 1.7 %collective-permute-start.6 = (f32[4,16,384]{2,1,0:T(8,128)S(1)}, f32[4,16,384]{2,1,0:T(8,128)S(1)}, u32[]{:S(2)}, u32[]{:S(2)}) collective-permute-start(f32[4,16,384]{2,1,0:T(8,128)S(1)} %get-tuple-element.28), channel_id=1, source_target_pairs={{0,1},{2,3},{1,0},{3,2},{4,5},{6,7},{5,4},{7,6},{8,9},{10,11},{9,8... | collective-permute-start | bytes 294920 | tf_op jit(solution)/shard_map/ppermute | solution.py:61
  27.2 0.7 collective-permute-start.7
  27.9 2.2 %shard_map.44.middle_ref = f32[80,32]{1,0:T(8,128)S(1)} custom-call(bf16[4,16,48,384]{3,2,1,0:T(8,128)(2,1)S(1)} %get-tuple-element.19.fields_ref, bf16[4,16,32,384]{3,2,1,0:T(8,128)(2,1)S(1)} %get-tuple-element.25.halves_ref), custom_call_target="tpu_custom_call" | custom-call | flops 1000000000 | tf_op jit(solution)/shard_map/pallas_call | solution.py:82
  30.1 0.0 collective-permute-done.6.refs_2_
  30.1 0.0 collective-permute-done.7.refs_3_
  30.1 0.0 collective-permute-done.4.refs_0_
  30.2 2.2 %collective-permute-done.5.refs_1_ = f32[16,16,384]{2,1,0:T(8,128)S(1)} collective-permute-done((f32[16,16,384]{2,1,0:T(8,128)S(1)}, f32[16,16,384]{2,1,0:T(8,128)S(1)}, u32[]{:S(2)}, u32[]{:S(2)}) %collective-permute-start.5) | collective-permute-done | bytes 393248 | tf_op jit(solution)/shard_map/ppermute | solution.py:61
  32.4 5.6 %shard_map.45 = (bf16[4,16,112,384]{3,2,1,0:T(8,128)(2,1)S(1)}, f32[32,128]{1,0:T(8,128)S(1)}) custom-call(f32[3,4,16,384]{3,2,1,0:T(8,128)S(1)} %get-tuple-element.18.coefs, bf16[4,16,48,384]{3,2,1,0:T(8,128)(2,1)S(1)} %get-tuple-element.19.fields_ref, f32[4,16,16,384]{3,2,1,0:T(8,128)S(1)} %get-tuple-element.24.lifted_ref, ...), custom_call_target="tpu_custom_call" | custom-call | tf_op jit(solution)/shard_map/pallas_call | solution.py:82
  38.0 1.8 %all-gather = f32[64,128]{1,0:T(8,128)S(1)} all-gather(f32[32,128]{1,0:T(8,128)S(1)} %get-tuple-element.30), channel_id=2, replica_groups=mesh['plane_0'=4,'plane_1'=8,'plane_2'=2,'depth'=4] {'plane_2'}, dimensions={0}, use_global_device_ids=true | all-gather | bytes 49152 | tf_op jit(solution)/shard_map/all_gather | solution.py:52
  39.8 23.8 %all_to_all.10.pieces_ref = f32[32,16,128]{2,1,0:T(8,128)S(1)} all-to-all(f32[32,16,128]{2,1,0:T(8,128)S(1)} %shard_map.46), channel_id=1, replica_groups=mesh['plane_0'=4,'plane_1'=8,'plane_2'=2,'depth'=4] {'plane_1','depth'}, dimensions={0} | all-to-all | bytes 524288 | tf_op jit(solution)/shard_map/all_to_all | solution.py:54
  63.7 11.3 %all_to_all.11.packed_ref = f32[8,16,128]{2,1,0:T(8,128)S(1)} all-to-all(f32[8,16,128]{2,1,0:T(8,128)S(1)} %shard_map.47), channel_id=1, replica_groups=mesh['plane_0'=4,'plane_1'=8,'plane_2'=2,'depth'=4] {'plane_0','plane_2'}, dimensions={0} | all-to-all | bytes 131072 | tf_op jit(solution)/shard_map/all_to_all | solution.py:55
  75.0 8.7 %shard_map.48 = (f32[80,4,16,384]{3,2,1,0:T(8,128)}, f32[3,48,80]{2,1,0:T(8,128)}) custom-call(f32[8,16,128]{2,1,0:T(8,128)S(1)} %all_to_all.11.packed_ref, bf16[4,16,112,384]{3,2,1,0:T(8,128)(2,1)S(1)} %get-tuple-element.31.parts_ref), custom_call_target="tpu_custom_call" | custom-call | tf_op jit(solution)/shard_map/pallas_call | solution.py:82
  (2 shorter events, 0.1 us)
Async XLA Ops:
  3.4 12.3 %collective-permute-start = (f32[17,32,384]{2,1,0:T(8,128)S(1)}, f32[17,32,384]{2,1,0:T(8,128)S(1)}, u32[]{:S(2)}, u32[]{:S(2)}) collective-permute-start(f32[17,32,384]{2,1,0:T(8,128)S(1)} %get-tuple-element.20), channel_id=1, source_target_pairs={{0,4},{8,12},{16,20},{24,28},{32,36},{40,44},{48,52},{56,60},{64,6... | collective-permute-start | bytes 2506760 | tf_op jit(solution)/shard_map/ppermute | solution.py:61
  6.7 13.8 %collective-permute-start.1 = (f32[17,32,384]{2,1,0:T(8,128)S(1)}, f32[17,32,384]{2,1,0:T(8,128)S(1)}, u32[]{:S(2)}, u32[]{:S(2)}) collective-permute-start(f32[17,32,384]{2,1,0:T(8,128)S(1)} %get-tuple-element.21), channel_id=1, source_target_pairs={{4,8},{12,16},{20,24},{28,32},{36,40},{44,48},{52,56},{60,64},{68,... | collective-permute-start | bytes 2506760 | tf_op jit(solution)/shard_map/ppermute | solution.py:61
  8.6 7.0 %collective-permute-start.2 = (f32[5,32,384]{2,1,0:T(8,128)S(1)}, f32[5,32,384]{2,1,0:T(8,128)S(1)}, u32[]{:S(2)}, u32[]{:S(2)}) collective-permute-start(f32[5,32,384]{2,1,0:T(8,128)S(1)} %get-tuple-element.22), channel_id=1, source_target_pairs={{0,1},{2,3},{1,0},{3,2},{4,5},{6,7},{5,4},{7,6},{8,9},{10,11},{9,8... | collective-permute-start | bytes 737288 | tf_op jit(solution)/shard_map/ppermute | solution.py:61
  9.8 5.8 %collective-permute-start.3 = (f32[5,32,384]{2,1,0:T(8,128)S(1)}, f32[5,32,384]{2,1,0:T(8,128)S(1)}, u32[]{:S(2)}, u32[]{:S(2)}) collective-permute-start(f32[5,32,384]{2,1,0:T(8,128)S(1)} %get-tuple-element.23), channel_id=1, source_target_pairs={{1,2},{2,1},{5,6},{6,5},{9,10},{10,9},{13,14},{14,13},{17,18},{18,... | collective-permute-start | bytes 737288 | tf_op jit(solution)/shard_map/ppermute | solution.py:61
  23.2 7.0 %collective-permute-start.4 = (f32[16,16,384]{2,1,0:T(8,128)S(1)}, f32[16,16,384]{2,1,0:T(8,128)S(1)}, u32[]{:S(2)}, u32[]{:S(2)}) collective-permute-start(f32[16,16,384]{2,1,0:T(8,128)S(1)} %get-tuple-element.26), channel_id=1, source_target_pairs={{0,4},{8,12},{16,20},{24,28},{32,36},{40,44},{48,52},{56,60},{64,6... | collective-permute-start | bytes 1179656 | tf_op jit(solution)/shard_map/ppermute | solution.py:61
  23.3 9.1 %collective-permute-start.5 = (f32[16,16,384]{2,1,0:T(8,128)S(1)}, f32[16,16,384]{2,1,0:T(8,128)S(1)}, u32[]{:S(2)}, u32[]{:S(2)}) collective-permute-start(f32[16,16,384]{2,1,0:T(8,128)S(1)} %get-tuple-element.27), channel_id=1, source_target_pairs={{4,8},{12,16},{20,24},{28,32},{36,40},{44,48},{52,56},{60,64},{68,... | collective-permute-start | bytes 1179656 | tf_op jit(solution)/shard_map/ppermute | solution.py:61
  25.5 4.6 %collective-permute-start.6 = (f32[4,16,384]{2,1,0:T(8,128)S(1)}, f32[4,16,384]{2,1,0:T(8,128)S(1)}, u32[]{:S(2)}, u32[]{:S(2)}) collective-permute-start(f32[4,16,384]{2,1,0:T(8,128)S(1)} %get-tuple-element.28), channel_id=1, source_target_pairs={{0,1},{2,3},{1,0},{3,2},{4,5},{6,7},{5,4},{7,6},{8,9},{10,11},{9,8... | collective-permute-start | bytes 294920 | tf_op jit(solution)/shard_map/ppermute | solution.py:61
  27.2 2.9 %collective-permute-start.7 = (f32[4,16,384]{2,1,0:T(8,128)S(1)}, f32[4,16,384]{2,1,0:T(8,128)S(1)}, u32[]{:S(2)}, u32[]{:S(2)}) collective-permute-start(f32[4,16,384]{2,1,0:T(8,128)S(1)} %get-tuple-element.29), channel_id=1, source_target_pairs={{1,2},{2,1},{5,6},{6,5},{9,10},{10,9},{13,14},{14,13},{17,18},{18,... | collective-permute-start | bytes 294920 | tf_op jit(solution)/shard_map/ppermute | solution.py:61

commit v3 on v2

--- a/solution.py
+++ b/solution.py
@@ -62,12 +62,9 @@
 
 
 def exchange(plane_even, plane_odd, row_even, row_odd):
-    out = []
-    for edge, axis, first in (
-        (plane_even, PLANE, 0), (plane_odd, PLANE, 1), (row_even, "depth", 0), (row_odd, "depth", 1)
-    ):
-        out.append(swap(edge, axis, first))
-    return tuple(out)
+    return (
+        swap(plane_even, PLANE, 0), swap(plane_odd, PLANE, 1), swap(row_even, "depth", 0), swap(row_odd, "depth", 1)
+    )
 
 
 def call(body, outs, operands, scratch=(), limit=16, work=0):
@@ -90,109 +87,125 @@
     )(*results)
 
 
-def sweep(px, py, step):
+def sweep(px, py, step, carry):
     group = next(count for count in (7, 6, 5, 4, 3, 2, 1) if (py - 2) % count == 0)
     for p in range(px):
-        step(p, 0)
-
-        def several(j, carry):
-            for i in range(group):
-                step(p, 1 + group * j + i)
-            return carry
-
-        lax.fori_loop(0, (py - 2) // group, several, 0)
-        step(p, py - 1)
+        carry = step(p, (0, py - 1), carry)
+
+        def several(j, value, p=p):
+            return step(p, [1 + group * j + i for i in range(group)], value)
+
+        carry = lax.fori_loop(0, (py - 2) // group, several, carry)
+    return carry
+
+
+def read_face(labels, start, px, py, cz):
+    halves = py // 8
+
+    def body(labels_in, start_ref, face, raw, labels_ref, sems):
+        p = parities()[0] * (px - 1)
+        copies = [pltpu.make_async_copy(labels_in.at[p], labels_ref, sems.at[2 * halves])]
+        for h in range(halves):
+            for i in range(2):
+                source = start_ref.at[pl.ds(2 * B * i, B), p, pl.ds(8 * h, 8), :]
+                copies.append(pltpu.make_async_copy(source, raw.at[h, pl.ds(B * i, B)], sems.at[2 * h + i]))
+        for each in copies:
+            each.start()
+        for each in copies:
+            each.wait()
+        for h in range(halves):
+            turned = jnp.swapaxes(raw[h].astype(f32), 0, 1)
+            for i in range(8):
+                face[16 * h + 2 * i] = turned[i, :B]
+                face[16 * h + 2 * i + 1] = turned[i, B:]
+        face[2 * py, :py] = labels_ref[...].astype(f32)
+
+    return call(
+        body,
+        (((2 * py + 1, B, cz), f32, VMEM),),
+        ((labels, pltpu.HBM), (start, pltpu.HBM)),
+        (
+            pltpu.VMEM((halves, 2 * B, 8, cz), jnp.int32),
+            pltpu.VMEM((py, cz), jnp.int32),
+            pltpu.SemaphoreType.DMA((2 * halves + 1,)),
+        ),
+        4,
+    )[0]
 
 
 def read_start(labels, start, px, py, cz):
     halves = py // 8
 
-    def body(labels_in, start_ref, fields_ref, coefs, plane_even, plane_odd, row_even, row_odd, raw, labels_ref, sems, labels_sem):
+    def body(labels_ref, start_ref, fields_ref, coefs, plane_even, row_even, row_odd):
         q, r = parities()
-        fetch = pltpu.make_async_copy(labels_in, labels_ref, labels_sem)
-
-        def copy(chunk):
-            p, h = chunk // halves, chunk % halves
-            return pltpu.make_async_copy(start_ref.at[:, p, pl.ds(8 * h, 8), :], raw.at[chunk], sems.at[chunk])
-
-        for chunk in range(px * halves):
-            copy(chunk).start()
-        fetch.start()
+
 
         def step(chunk, carry):
-            copy(chunk).wait()
             p, h = chunk // halves, chunk % halves
             rows = pl.multiple_of(8 * h, 8)
-            turned = jnp.swapaxes(raw[chunk].astype(f32), 0, 1)
-            sent = jnp.concatenate([turned[:, :B], turned[:, 2 * B :]], 1)
+            turned = jnp.swapaxes(start_ref[:, p, pl.ds(rows, 8), :].astype(f32), 0, 1)
             fields_ref[p, pl.ds(rows, 8)] = turned.astype(bf16)
 
             @pl.when(p == (1 - q) * (px - 1))
             def _():
-                plane_even[pl.ds(rows, 8)] = sent
-
-            @pl.when(p == q * (px - 1))
-            def _():
-                plane_odd[pl.ds(rows, 8)] = sent
-
-            edge = jnp.where(h == 0, sent[0], sent[7])
+                for i in range(8):
+                    plane_even[2 * (rows + i)] = turned[i, :B]
+                    plane_even[2 * (rows + i) + 1] = turned[i, 2 * B :]
+
+            edge = jnp.where(h == 0, turned[0], turned[7])
 
             @pl.when(h == (1 - r) * (halves - 1))
             def _():
-                row_even[p] = edge
+                row_even[2 * p] = edge[:B]
+                row_even[2 * p + 1] = edge[2 * B :]
 
             @pl.when(h == r * (halves - 1))
             def _():
-                row_odd[p] = edge
+                row_odd[2 * p] = edge[:B]
+                row_odd[2 * p + 1] = edge[2 * B :]
 
             return carry
 
         lax.fori_loop(0, px * halves, step, 0)
-        fetch.wait()
         for p in range(px):
             for which, table in enumerate((outer_table, damping_table, inner_table)):
                 coefs[which, p] = coef(labels_ref[p], table)
-        plane_even[py, :py] = labels_ref[(1 - q) * (px - 1)].astype(f32)
-        plane_odd[py, :py] = labels_ref[q * (px - 1)].astype(f32)
+        plane_even[2 * py, :py] = labels_ref[(1 - q) * (px - 1)].astype(f32)
         for p in range(px):
-            row_even[px, p : p + 1] = labels_ref[p, pl.ds((1 - r) * (py - 1), 1), :].astype(f32)
-            row_odd[px, p : p + 1] = labels_ref[p, pl.ds(r * (py - 1), 1), :].astype(f32)
-
-    plane, row = ((py + 1, 2 * B, cz), f32, VMEM), ((px + 1, 2 * B, cz), f32, VMEM)
+            row_even[2 * px, p : p + 1] = labels_ref[p, pl.ds((1 - r) * (py - 1), 1), :].astype(f32)
+            row_odd[2 * px, p : p + 1] = labels_ref[p, pl.ds(r * (py - 1), 1), :].astype(f32)
+
+    plane, row = ((2 * py + 1, B, cz), f32, VMEM), ((2 * px + 1, B, cz), f32, VMEM)
     return call(
         body,
-        (((px, py, S, cz), bf16, VMEM), ((3, px, py, cz), f32, VMEM), plane, plane, row, row),
-        ((labels, pltpu.HBM), (start, pltpu.HBM)),
-        (
-            pltpu.VMEM((px * halves, S, 8, cz), jnp.int32),
-            pltpu.VMEM((px, py, cz), jnp.int32),
-            pltpu.SemaphoreType.DMA((px * halves,)),
-            pltpu.SemaphoreType.DMA,
-        ),
-    )
-
-
-def outside(edges, p, y, px, py):
+        (((px, py, S, cz), bf16, VMEM), ((3, px, py, cz), f32, VMEM), plane, row, row),
+        ((labels, VMEM), (start, VMEM)),
+    )
+
+
+def outside(edges, p, y, px, py, blocks=1, block=0):
     plane_even, plane_odd, row_even, row_odd = edges
     q, r = parities()
     if p < 0:
-        return jnp.where(q == 0, plane_odd[y], plane_even[y])
-    if p == px:
-        return jnp.where(q == 0, plane_even[y], plane_odd[y])
-    if isinstance(y, int) and y < 0:
-        return jnp.where(r == 0, row_odd[p], row_even[p])
-    if isinstance(y, int) and y == py:
-        return jnp.where(r == 0, row_even[p], row_odd[p])
-    return None
-
-
-def laplace(inside, p, y, at, px, py, cz, edges=None, edge_at=0):
+        first, second, parity, at = plane_odd, plane_even, q, y
+    elif p == px:
+        first, second, parity, at = plane_even, plane_odd, q, y
+    elif isinstance(y, int) and y < 0:
+        first, second, parity, at = row_odd, row_even, r, p
+    elif isinstance(y, int) and y == py:
+        first, second, parity, at = row_even, row_odd, r, p
+    else:
+        return None
+    return jnp.where(parity == 0, first[blocks * at + block], second[blocks * at + block])
+
+
+def laplace(inside, p, y, at, px, py, cz, edges=None, block=0):
     def get(p, y):
         if 0 <= p < px and (not isinstance(y, int) or 0 <= y < py):
             return [inside[p, y, at : at + B]]
         if edges is None:
             return []
-        return [outside(edges, p, y, px, py)[edge_at : edge_at + B].astype(inside.dtype)]
+        return [outside(edges, p, y, px, py, 2, block).astype(inside.dtype)]
 
     wide = get(p, y)[0].astype(f32)
     lane = lax.broadcasted_iota(jnp.int32, (B, cz), 1)
@@ -216,22 +229,23 @@
     def body(coefs, fields_ref, gram_ref, *refs):
         around, (lifted, halves, plane_even, plane_odd, row_even, row_odd, theirs) = refs[:4], refs[4:]
 
-        def step(p, y):
-            outer, damping, inner = [coefs[k, p, pl.ds(y, 1), :] for k in range(3)]
-            middle = fields_ref[p, y, B : 2 * B, :].astype(f32)
-            out = (
-                outer * laplace(fields_ref, p, y, 0, px, py, cz, around, 0)
-                + damping * middle
-                + inner * laplace(fields_ref, p, y, 2 * B, px, py, cz, around, B)
-            )
-            lifted[p, y] = out
-            halves[p, y] = split(out)
-
-        sweep(px, py, step)
+        def step(p, rows, carry):
+            for y in rows:
+                outer, damping, inner = [coefs[k, p, pl.ds(y, 1), :] for k in range(3)]
+                out = (
+                    outer * laplace(fields_ref, p, y, 0, px, py, cz, around, 0)
+                    + damping * fields_ref[p, y, B : 2 * B, :].astype(f32)
+                    + inner * laplace(fields_ref, p, y, 2 * B, px, py, cz, around, 1)
+                )
+                lifted[p, y] = out
+                halves[p, y] = split(out)
+            return carry
+
+        sweep(px, py, step, 0)
         q, r = parities()
 
         for at, received in enumerate(around):
-            labels = received[py if at < 2 else px, :py]
+            labels = received[2 * py if at < 2 else 2 * px, :py]
             theirs[at, 0], theirs[at, 1] = coef(labels, outer_table), coef(labels, inner_table)
 
         def edge(at, line, p, y):
@@ -302,28 +316,28 @@
     def body(coefs, fields_ref, lifted_ref, halves_ref, start_ref, middle_ref, *refs):
         end_refs, (parts, packed) = refs[:4], refs[4:]
 
-        def step(p, y):
-            outer, damping, inner = [coefs[k, p, pl.ds(y, 1), :] for k in range(3)]
-            now = fields_ref[p, y]
-            second = (
-                outer * laplace(lifted_ref, p, y, 0, px, py, cz)
-                + damping * now[:B].astype(f32)
-                + inner * laplace(fields_ref, p, y, B, px, py, cz)
+        def step(p, rows, gram):
+            every = []
+            for y in rows:
+                outer, damping, inner = [coefs[k, p, pl.ds(y, 1), :] for k in range(3)]
+                now = fields_ref[p, y]
+                second = (
+                    outer * laplace(lifted_ref, p, y, 0, px, py, cz)
+                    + damping * now[:B].astype(f32)
+                    + inner * laplace(fields_ref, p, y, B, px, py, cz)
+                )
+                for other in ((p - 1, y), (p + 1, y), (p, y - 1), (p, y + 1)):
+                    received = outside(end_refs, *other, px, py)
+                    if received is not None:
+                        second = second - received
+                every.append(jnp.concatenate([now, halves_ref[p, y], split(second)], 0))
+                parts[p, y] = every[-1]
+            every = jnp.concatenate(every, 1)
+            return gram + lax.dot_general(
+                every, every[S + 2 * B :], (((1,), (1,)), ((), ())), preferred_element_type=f32
             )
-            for other in ((p - 1, y), (p + 1, y), (p, y - 1), (p, y + 1)):
-                received = outside(end_refs, *other, px, py)
-                if received is not None:
-                    second = second - received
-            parts[p, y] = jnp.concatenate([now, halves_ref[p, y], split(second)], 0)
-
-        def left(r):
-            return parts[r // py, r % py]
-
-        def right(r):
-            return parts[r // py, r % py, S + 2 * B :]
-
-        sweep(px, py, step)
-        last = gram_loop(8, px * py, left, right, (A, 2 * B))
+
+        last = sweep(px, py, step, jnp.zeros((A, 2 * B), f32))
         last = jnp.concatenate([last, jnp.zeros((A, 128 - 2 * B), f32)], 1)
         last = last + pltpu.roll(last, 128 - B, 1)
         middle = jnp.concatenate([middle_ref[...], jnp.zeros((S + 2 * B, 128 - 2 * B), f32)], 1)
@@ -416,7 +430,7 @@
 def finish(packed, parts, cells_total, px, py, cz):
     halves = py // 8
 
-    def body(packed_ref, parts_ref, out_ref, coords_out, turned, ready, coords_ref, sems, coords_sem):
+    def body(packed_ref, parts_ref, out_ref, coords_out, ready, coords_ref, sems, coords_sem):
         pieces = [packed_ref[i] for i in range(packed.shape[0])]
         sums = [sum(pieces[c::2][1:], pieces[c]) for c in range(2)]
         table = jnp.concatenate(sums, 0) * (1.0 / cells_total)
@@ -441,7 +455,7 @@
         matrix = matrix + place(inverse, 3, 4) + place(inverse, 4, 5) + place(inverse, 4, 6)
         matrix = matrix[:, :A]
         high = matrix.astype(bf16)
-        weights = jnp.concatenate([high, (matrix - high.astype(f32)).astype(bf16)], 0)
+        weights = jnp.concatenate([high, (matrix - high.astype(f32)).astype(bf16)], 1)
 
         def copy(chunk):
             p, h = chunk // halves, chunk % halves
@@ -449,10 +463,11 @@
 
         def step(chunk, carry):
             p, h = chunk // halves, chunk % halves
-            for y in range(8):
-                out = jnp.dot(weights, parts_ref[p, 8 * h + y], preferred_element_type=f32)
-                turned[y] = out[:V] + out[V:]
-            ready[chunk] = jnp.swapaxes(turned[...], 0, 1)
+            for y in range(0, 8, 2):
+                part = jnp.concatenate([parts_ref[p, 8 * h + y + i] for i in range(2)], 1)
+                out = jnp.dot(weights, jnp.concatenate([part, part], 0), preferred_element_type=f32)
+                for i in range(2):
+                    ready[chunk, :, y + i, :] = out[:, cz * i : cz * i + cz]
             copy(chunk).start()
             return carry
 
@@ -473,7 +488,6 @@
         (((V, px, py, cz), f32, ANY), ((3, S, V), f32, ANY)),
         ((packed, VMEM), (parts, VMEM)),
         (
-            pltpu.VMEM((8, V, cz), f32),
             pltpu.VMEM((px * halves, V, 8, cz), f32),
             pltpu.VMEM((3, S, V), f32),
             pltpu.SemaphoreType.DMA((px * halves,)),
@@ -486,8 +500,10 @@
 def steps(labels, start):
     px, py, cz = labels.shape
     cells_total = labels.size * lax.axis_size(PLANE) * lax.axis_size("depth")
-    fields, coefs, *edges = read_start(labels, start.reshape((S, px, py, cz)), px, py, cz)
-    edges = exchange(*edges)
+    start = start.reshape((S, px, py, cz))
+    face = read_face(labels, start, px, py, cz)
+    fields, coefs, plane_even, *rows = read_start(labels, start, px, py, cz)
+    edges = exchange(plane_even, face, *rows)
     start_gram = start_products(fields, px, py)
     lifted, halves, *ends = first_lift(coefs, fields, start_gram, edges, px, py, cz)
     ends = exchange(*ends)

time: 83.9 us -> 81.7 us (0.974)
  waiting for transfers between devices: 11 us -> 4.85 us
  starting transfers between devices: 11.7 us -> 15.3 us
    ppermute x8, waiting for transfers between devices: 11 us -> 4.85 us  [swap(): return lax.ppermute(edge, axis, pairs + [(b, a) for a, b in pairs])]
    ppermute x8, starting transfers between devices: 11.7 us -> 15.3 us  [swap(): return lax.ppermute(edge, axis, pairs + [(b, a) for a, b in pairs])]
    pallas_call x8 -> x9, Pallas kernels: 23.2 us -> 22.8 us  [call(): pl.pallas_call(body, out_shape=tuple(shapes), in_specs=specs, out_specs=t...]
  transfers between devices with their start and end apart: 8 -> 8, of which waited for: 3 -> 2; matrix products, arithmetic and copies ran while one was open for 0% -> 0% of each run, Pallas kernels for 4% -> 6%
where the time goes in v3:
time: 81.7 us; the launch traced here: 81.4 us
  blocking collectives  37.7 us (46%)
  Pallas kernels  22.8 us (28%)
  starting transfers between devices  15.3 us (19%)
  waiting for transfers between devices  4.85 us (6%)
    all_to_all x1, blocking collectives, sum_all(): lax.all_to_all(own, WIDE, 0, 0, tiled=True)  24.6 us
    pallas_call x9, Pallas kernels, call(): pl.pallas_call(body, out_shape=tuple(shapes), in_specs=specs, out_specs=t...  22.8 us
    ppermute x8, starting transfers between devices, swap(): return lax.ppermute(edge, axis, pairs + [(b, a) for a, b in pairs])  15.3 us
    all_to_all x1, blocking collectives, sum_all(): return lax.all_to_all(own, NARROW, 0, 0, tiled=True)  11.2 us
    ppermute x8, waiting for transfers between devices, swap(): return lax.ppermute(edge, axis, pairs + [(b, a) for a, b in pairs])  4.85 us
    all_gather x1, blocking collectives, sum_all(): both = lax.all_gather(table, 'plane_2')  1.83 us
  transfers between devices with their start and end apart: 8, of which 2 were waited for; matrix products, arithmetic and copies ran while one was open for 0% of the time, Pallas kernels for 6%

profile of v3, /device:TPU:1, one launch (start us, length us, event | category | flops | bytes accessed | tf_op | source)
XLA Modules:
  0.0 81.4 jit_solution(1986141566373032113)
XLA Ops:
  0.6 0.0 copy-start.1
  0.6 0.0 copy-start
  0.6 1.6 %shard_map.43 = f32[33,16,384]{2,1,0:T(8,128)S(1)} custom-call(s32[4,16,384]{2,1,0:T(8,128)} %labels_in.1, s32[48,4,16,384]{3,2,1,0:T(8,128)} %bitcast.3), custom_call_target="tpu_custom_call" | custom-call | tf_op jit(solution)/shard_map/pallas_call | solution.py:79
  2.3 5.1 %collective-permute-start.1 = (f32[33,16,384]{2,1,0:T(8,128)S(1)}, f32[33,16,384]{2,1,0:T(8,128)S(1)}, u32[]{:S(2)}, u32[]{:S(2)}) collective-permute-start(f32[33,16,384]{2,1,0:T(8,128)S(1)} %shard_map.43), channel_id=1, source_target_pairs={{4,8},{12,16},{20,24},{28,32},{36,40},{44,48},{52,56},{60,64},{68,... | collective-permute-start | bytes 2433032 | tf_op jit(solution)/shard_map/ppermute | solution.py:61
  7.3 0.0 copy-done.1
  7.3 0.0 copy-done
  7.4 1.6 %shard_map.41 = (bf16[4,16,48,384]{3,2,1,0:T(8,128)(2,1)S(1)}, f32[3,4,16,384]{3,2,1,0:T(8,128)S(1)}, f32[33,16,384]{2,1,0:T(8,128)S(1)}, f32[9,16,384]{2,1,0:T(8,128)S(1)}, f32[9,16,384]{2,1,0:T(8,128)S(1)}) custom-call(s32[4,16,384]{2,1,0:T(8,128)S(1)} %copy-done.1, s32[48,4,16,384]{3,2,1,0:T(8,128)S(1)} %bitcast.4), custom_call_target="tpu_custom_call" | custom-call | tf_op jit(solution)/shard_map/pallas_call | solution.py:79
  9.0 0.1 collective-permute-start
  9.1 1.4 %collective-permute-start.2 = (f32[9,16,384]{2,1,0:T(8,128)S(1)}, f32[9,16,384]{2,1,0:T(8,128)S(1)}, u32[]{:S(2)}, u32[]{:S(2)}) collective-permute-start(f32[9,16,384]{2,1,0:T(8,128)S(1)} %get-tuple-element.20), channel_id=1, source_target_pairs={{0,1},{2,3},{1,0},{3,2},{4,5},{6,7},{5,4},{7,6},{8,9},{10,11},{9,8... | collective-permute-start | bytes 663560 | tf_op jit(solution)/shard_map/ppermute | solution.py:61
  10.5 0.7 collective-permute-start.3
  11.2 1.3 %shard_map.42.gram_ref.start_ref = f32[48,48]{1,0:T(8,128)S(1)} custom-call(bf16[4,16,48,384]{3,2,1,0:T(8,128)(2,1)S(1)} %get-tuple-element.18.fields_ref), custom_call_target="tpu_custom_call" | custom-call | flops 1000000000 | tf_op jit(solution)/shard_map/pallas_call | solution.py:79
  12.4 3.3 %collective-permute-done.2.refs_2_ = f32[9,16,384]{2,1,0:T(8,128)S(1)} collective-permute-done((f32[9,16,384]{2,1,0:T(8,128)S(1)}, f32[9,16,384]{2,1,0:T(8,128)S(1)}, u32[]{:S(2)}, u32[]{:S(2)}) %collective-permute-start.2) | collective-permute-done | bytes 221216 | tf_op jit(solution)/shard_map/ppermute | solution.py:61
  15.8 0.0 collective-permute-done.3.refs_3_
  15.8 1.5 %collective-permute-done.1.refs_1_ = f32[33,16,384]{2,1,0:T(8,128)S(1)} collective-permute-done((f32[33,16,384]{2,1,0:T(8,128)S(1)}, f32[33,16,384]{2,1,0:T(8,128)S(1)}, u32[]{:S(2)}, u32[]{:S(2)}) %collective-permute-start.1) | collective-permute-done | bytes 811040 | tf_op jit(solution)/shard_map/ppermute | solution.py:61
  17.3 0.0 collective-permute-done.refs_0_
  17.3 2.7 %shard_map.44 = (f32[4,16,16,384]{3,2,1,0:T(8,128)S(1)}, bf16[4,16,32,384]{3,2,1,0:T(8,128)(2,1)S(1)}, f32[16,16,384]{2,1,0:T(8,128)S(1)}, f32[16,16,384]{2,1,0:...) custom-call(f32[3,4,16,384]{3,2,1,0:T(8,128)S(1)} %get-tuple-element.17.coefs, ...), custom_call_target="tpu_custom_call" | custom-call | tf_op jit(solution)/shard_map/pallas_call | solution.py:79
  20.0 0.1 collective-permute-start.4
  20.1 3.9 %collective-permute-start.5 = (f32[16,16,384]{2,1,0:T(8,128)S(1)}, f32[16,16,384]{2,1,0:T(8,128)S(1)}, u32[]{:S(2)}, u32[]{:S(2)}) collective-permute-start(f32[16,16,384]{2,1,0:T(8,128)S(1)} %get-tuple-element.25), channel_id=1, source_target_pairs={{4,8},{12,16},{20,24},{28,32},{36,40},{44,48},{52,56},{60,64},{68,... | collective-permute-start | bytes 1179656 | tf_op jit(solution)/shard_map/ppermute | solution.py:61
  24.0 3.4 %collective-permute-start.6 = (f32[4,16,384]{2,1,0:T(8,128)S(1)}, f32[4,16,384]{2,1,0:T(8,128)S(1)}, u32[]{:S(2)}, u32[]{:S(2)}) collective-permute-start(f32[4,16,384]{2,1,0:T(8,128)S(1)} %get-tuple-element.26), channel_id=1, source_target_pairs={{0,1},{2,3},{1,0},{3,2},{4,5},{6,7},{5,4},{7,6},{8,9},{10,11},{9,8... | collective-permute-start | bytes 294920 | tf_op jit(solution)/shard_map/ppermute | solution.py:61
  27.4 0.7 collective-permute-start.7
  28.1 2.2 %shard_map.45.middle_ref = f32[80,32]{1,0:T(8,128)S(1)} custom-call(bf16[4,16,48,384]{3,2,1,0:T(8,128)(2,1)S(1)} %get-tuple-element.18.fields_ref, bf16[4,16,32,384]{3,2,1,0:T(8,128)(2,1)S(1)} %get-tuple-element.23.halves_ref), custom_call_target="tpu_custom_call" | custom-call | flops 1000000000 | tf_op jit(solution)/shard_map/pallas_call | solution.py:79
  30.3 0.0 collective-permute-done.6.refs_2_
  30.3 0.0 collective-permute-done.7.refs_3_
  30.3 0.0 collective-permute-done.4.refs_0_
  30.3 0.0 collective-permute-done.5.refs_1_
  30.3 5.2 %shard_map.46 = (bf16[4,16,112,384]{3,2,1,0:T(8,128)(2,1)S(1)}, f32[32,128]{1,0:T(8,128)S(1)}) custom-call(f32[3,4,16,384]{3,2,1,0:T(8,128)S(1)} %get-tuple-element.17.coefs, bf16[4,16,48,384]{3,2,1,0:T(8,128)(2,1)S(1)} %get-tuple-element.18.fields_ref, f32[4,16,16,384]{3,2,1,0:T(8,128)S(1)} %get-tuple-element.22.lifted_ref, ...), custom_call_target="tpu_custom_call" | custom-call | tf_op jit(solution)/shard_map/pallas_call | solution.py:79
  35.6 1.8 %all-gather = f32[64,128]{1,0:T(8,128)S(1)} all-gather(f32[32,128]{1,0:T(8,128)S(1)} %get-tuple-element.28), channel_id=2, replica_groups=mesh['plane_0'=4,'plane_1'=8,'plane_2'=2,'depth'=4] {'plane_2'}, dimensions={0}, use_global_device_ids=true | all-gather | bytes 49152 | tf_op jit(solution)/shard_map/all_gather | solution.py:52
  37.4 24.6 %all_to_all.10.pieces_ref = f32[32,16,128]{2,1,0:T(8,128)S(1)} all-to-all(f32[32,16,128]{2,1,0:T(8,128)S(1)} %shard_map.47), channel_id=1, replica_groups=mesh['plane_0'=4,'plane_1'=8,'plane_2'=2,'depth'=4] {'plane_1','depth'}, dimensions={0} | all-to-all | bytes 524288 | tf_op jit(solution)/shard_map/all_to_all | solution.py:54
  62.1 11.2 %all_to_all.11.packed_ref = f32[8,16,128]{2,1,0:T(8,128)S(1)} all-to-all(f32[8,16,128]{2,1,0:T(8,128)S(1)} %shard_map.48), channel_id=1, replica_groups=mesh['plane_0'=4,'plane_1'=8,'plane_2'=2,'depth'=4] {'plane_0','plane_2'}, dimensions={0} | all-to-all | bytes 131072 | tf_op jit(solution)/shard_map/all_to_all | solution.py:55
  73.3 8.1 %shard_map.49 = (f32[80,4,16,384]{3,2,1,0:T(8,128)}, f32[3,48,80]{2,1,0:T(8,128)}) custom-call(f32[8,16,128]{2,1,0:T(8,128)S(1)} %all_to_all.11.packed_ref, bf16[4,16,112,384]{3,2,1,0:T(8,128)(2,1)S(1)} %get-tuple-element.29.parts_ref), custom_call_target="tpu_custom_call" | custom-call | tf_op jit(solution)/shard_map/pallas_call | solution.py:79
  (2 shorter events, 0.1 us)
Async XLA Ops:
  0.6 6.7 %copy-start.1 = (s32[4,16,384]{2,1,0:T(8,128)S(1)}, s32[4,16,384]{2,1,0:T(8,128)}, u32[]{:S(2)}) copy-start(s32[4,16,384]{2,1,0:T(8,128)} %labels_in.1) | copy-start | bytes 294916
  0.6 6.7 %copy-start = (s32[3,16,4,16,384]{4,3,2,1,0:T(8,128)S(1)}, s32[3,16,4,16,384]{4,3,2,1,0:T(8,128)}, u32[]{:S(2)}) copy-start(s32[3,16,4,16,384]{4,3,2,1,0:T(8,128)} %param.3) | copy-start | bytes 14155780
  2.3 15.0 %collective-permute-start.1 = (f32[33,16,384]{2,1,0:T(8,128)S(1)}, f32[33,16,384]{2,1,0:T(8,128)S(1)}, u32[]{:S(2)}, u32[]{:S(2)}) collective-permute-start(f32[33,16,384]{2,1,0:T(8,128)S(1)} %shard_map.43), channel_id=1, source_target_pairs={{4,8},{12,16},{20,24},{28,32},{36,40},{44,48},{52,56},{60,64},{68,... | collective-permute-start | bytes 2433032 | tf_op jit(solution)/shard_map/ppermute | solution.py:61
  9.0 8.3 %collective-permute-start = (f32[33,16,384]{2,1,0:T(8,128)S(1)}, f32[33,16,384]{2,1,0:T(8,128)S(1)}, u32[]{:S(2)}, u32[]{:S(2)}) collective-permute-start(f32[33,16,384]{2,1,0:T(8,128)S(1)} %get-tuple-element.19), channel_id=1, source_target_pairs={{0,4},{8,12},{16,20},{24,28},{32,36},{40,44},{48,52},{56,60},{64,6... | collective-permute-start | bytes 2433032 | tf_op jit(solution)/shard_map/ppermute | solution.py:61
  9.1 6.7 %collective-permute-start.2 = (f32[9,16,384]{2,1,0:T(8,128)S(1)}, f32[9,16,384]{2,1,0:T(8,128)S(1)}, u32[]{:S(2)}, u32[]{:S(2)}) collective-permute-start(f32[9,16,384]{2,1,0:T(8,128)S(1)} %get-tuple-element.20), channel_id=1, source_target_pairs={{0,1},{2,3},{1,0},{3,2},{4,5},{6,7},{5,4},{7,6},{8,9},{10,11},{9,8... | collective-permute-start | bytes 663560 | tf_op jit(solution)/shard_map/ppermute | solution.py:61
  10.5 5.3 %collective-permute-start.3 = (f32[9,16,384]{2,1,0:T(8,128)S(1)}, f32[9,16,384]{2,1,0:T(8,128)S(1)}, u32[]{:S(2)}, u32[]{:S(2)}) collective-permute-start(f32[9,16,384]{2,1,0:T(8,128)S(1)} %get-tuple-element.21), channel_id=1, source_target_pairs={{1,2},{2,1},{5,6},{6,5},{9,10},{10,9},{13,14},{14,13},{17,18},{18,... | collective-permute-start | bytes 663560 | tf_op jit(solution)/shard_map/ppermute | solution.py:61
  20.0 10.4 %collective-permute-start.4 = (f32[16,16,384]{2,1,0:T(8,128)S(1)}, f32[16,16,384]{2,1,0:T(8,128)S(1)}, u32[]{:S(2)}, u32[]{:S(2)}) collective-permute-start(f32[16,16,384]{2,1,0:T(8,128)S(1)} %get-tuple-element.24), channel_id=1, source_target_pairs={{0,4},{8,12},{16,20},{24,28},{32,36},{40,44},{48,52},{56,60},{64,6... | collective-permute-start | bytes 1179656 | tf_op jit(solution)/shard_map/ppermute | solution.py:61
  20.1 10.3 %collective-permute-start.5 = (f32[16,16,384]{2,1,0:T(8,128)S(1)}, f32[16,16,384]{2,1,0:T(8,128)S(1)}, u32[]{:S(2)}, u32[]{:S(2)}) collective-permute-start(f32[16,16,384]{2,1,0:T(8,128)S(1)} %get-tuple-element.25), channel_id=1, source_target_pairs={{4,8},{12,16},{20,24},{28,32},{36,40},{44,48},{52,56},{60,64},{68,... | collective-permute-start | bytes 1179656 | tf_op jit(solution)/shard_map/ppermute | solution.py:61
  24.0 6.3 %collective-permute-start.6 = (f32[4,16,384]{2,1,0:T(8,128)S(1)}, f32[4,16,384]{2,1,0:T(8,128)S(1)}, u32[]{:S(2)}, u32[]{:S(2)}) collective-permute-start(f32[4,16,384]{2,1,0:T(8,128)S(1)} %get-tuple-element.26), channel_id=1, source_target_pairs={{0,1},{2,3},{1,0},{3,2},{4,5},{6,7},{5,4},{7,6},{8,9},{10,11},{9,8... | collective-permute-start | bytes 294920 | tf_op jit(solution)/shard_map/ppermute | solution.py:61
  27.4 2.9 %collective-permute-start.7 = (f32[4,16,384]{2,1,0:T(8,128)S(1)}, f32[4,16,384]{2,1,0:T(8,128)S(1)}, u32[]{:S(2)}, u32[]{:S(2)}) collective-permute-start(f32[4,16,384]{2,1,0:T(8,128)S(1)} %get-tuple-element.27), channel_id=1, source_target_pairs={{1,2},{2,1},{5,6},{6,5},{9,10},{10,9},{13,14},{14,13},{17,18},{18,... | collective-permute-start | bytes 294920 | tf_op jit(solution)/shard_map/ppermute | solution.py:61

commit v4 on v3

--- a/solution.py
+++ b/solution.py
@@ -67,7 +67,7 @@
     )
 
 
-def call(body, outs, operands, scratch=(), limit=16, work=0):
+def call(body, outs, operands, scratch=(), limit=16, work=0, aliases=None):
     specs, shapes, results = [], [], []
     for operand, space in operands:
         specs.append(pl.BlockSpec(memory_space=space))
@@ -82,20 +82,24 @@
         in_specs=specs,
         out_specs=tuple(out_specs),
         scratch_shapes=list(scratch),
+        input_output_aliases=aliases or {},
         cost_estimate=pl.CostEstimate(flops=work, bytes_accessed=0, transcendentals=0),
         compiler_params=pltpu.CompilerParams(vmem_limit_bytes=limit * 2**20),
     )(*results)
 
 
-def sweep(px, py, step, carry):
+def sweep(px, py, inner, step, carry):
     group = next(count for count in (7, 6, 5, 4, 3, 2, 1) if (py - 2) % count == 0)
     for p in range(px):
-        carry = step(p, (0, py - 1), carry)
+        between = 0 < p < px - 1
+        if not inner:
+            carry = step(p, (0, py - 1), carry)
 
         def several(j, value, p=p):
             return step(p, [1 + group * j + i for i in range(group)], value)
 
-        carry = lax.fori_loop(0, (py - 2) // group, several, carry)
+        if inner == between:
+            carry = lax.fori_loop(0, (py - 2) // group, several, carry)
     return carry
 
 
@@ -225,23 +229,39 @@
     return result
 
 
-def first_lift(coefs, fields, gram, edges, px, py, cz):
-    def body(coefs, fields_ref, gram_ref, *refs):
+def first_rows(coefs, fields_ref, around, lifted, halves, inner, px, py, cz):
+    def step(p, rows, carry):
+        for y in rows:
+            outer, damping, middle = [coefs[k, p, pl.ds(y, 1), :] for k in range(3)]
+            out = (
+                outer * laplace(fields_ref, p, y, 0, px, py, cz, around, 0)
+                + damping * fields_ref[p, y, B : 2 * B, :].astype(f32)
+                + middle * laplace(fields_ref, p, y, 2 * B, px, py, cz, around, 1)
+            )
+            lifted[p, y] = out
+            halves[p, y] = split(out)
+        return carry
+
+    sweep(px, py, inner, step, 0)
+
+
+def first_lift_inner(coefs, fields, px, py, cz):
+    def body(coefs, fields_ref, lifted, halves):
+        first_rows(coefs, fields_ref, None, lifted, halves, True, px, py, cz)
+
+    return call(
+        body,
+        (((px, py, B, cz), f32, VMEM), ((px, py, 2 * B, cz), bf16, VMEM)),
+        ((coefs, VMEM), (fields, VMEM)),
+        limit=4,
+        work=10**9,
+    )
+
+
+def first_lift(coefs, fields, gram, lifted, halves, edges, px, py, cz):
+    def body(coefs, fields_ref, gram_ref, lifted_in, halves_in, *refs):
         around, (lifted, halves, plane_even, plane_odd, row_even, row_odd, theirs) = refs[:4], refs[4:]
-
-        def step(p, rows, carry):
-            for y in rows:
-                outer, damping, inner = [coefs[k, p, pl.ds(y, 1), :] for k in range(3)]
-                out = (
-                    outer * laplace(fields_ref, p, y, 0, px, py, cz, around, 0)
-                    + damping * fields_ref[p, y, B : 2 * B, :].astype(f32)
-                    + inner * laplace(fields_ref, p, y, 2 * B, px, py, cz, around, 1)
-                )
-                lifted[p, y] = out
-                halves[p, y] = split(out)
-            return carry
-
-        sweep(px, py, step, 0)
+        first_rows(coefs, fields_ref, around, lifted, halves, False, px, py, cz)
         q, r = parities()
 
         for at, received in enumerate(around):
@@ -263,9 +283,11 @@
     return call(
         body,
         (((px, py, B, cz), f32, VMEM), ((px, py, 2 * B, cz), bf16, VMEM), plane, plane, row, row),
-        ((coefs, VMEM), (fields, VMEM), (gram, ANY)) + tuple((edge, VMEM) for edge in edges),
+        ((coefs, VMEM), (fields, VMEM), (gram, ANY), (lifted, VMEM), (halves, VMEM))
+        + tuple((edge, VMEM) for edge in edges),
         (pltpu.VMEM((4, 2, py, cz), f32),),
         4,
+        aliases={3: 0, 4: 1},
     )
 
 
@@ -312,32 +334,49 @@
     )[0]
 
 
-def second_lift(coefs, fields, lifted, ends, halves, grams, px, py, cz):
-    def body(coefs, fields_ref, lifted_ref, halves_ref, start_ref, middle_ref, *refs):
+def second_rows(coefs, fields_ref, lifted_ref, halves_ref, around, parts, inner, px, py, cz):
+    def step(p, rows, gram):
+        every = []
+        for y in rows:
+            outer, damping, middle = [coefs[k, p, pl.ds(y, 1), :] for k in range(3)]
+            now = fields_ref[p, y]
+            second = (
+                outer * laplace(lifted_ref, p, y, 0, px, py, cz)
+                + damping * now[:B].astype(f32)
+                + middle * laplace(fields_ref, p, y, B, px, py, cz)
+            )
+            for other in ((p - 1, y), (p + 1, y), (p, y - 1), (p, y + 1)):
+                received = None if inner else outside(around, *other, px, py)
+                if received is not None:
+                    second = second - received
+            every.append(jnp.concatenate([now, halves_ref[p, y], split(second)], 0))
+            parts[p, y] = every[-1]
+        every = jnp.concatenate(every, 1)
+        return gram + lax.dot_general(
+            every, every[S + 2 * B :], (((1,), (1,)), ((), ())), preferred_element_type=f32
+        )
+
+    return sweep(px, py, inner, step, jnp.zeros((A, 2 * B), f32))
+
+
+def second_lift_inner(coefs, fields, lifted, halves, px, py, cz):
+    def body(coefs, fields_ref, lifted_ref, halves_ref, parts, gram_ref):
+        gram_ref[...] = second_rows(coefs, fields_ref, lifted_ref, halves_ref, None, parts, True, px, py, cz)
+
+    return call(
+        body,
+        (((px, py, A, cz), bf16, VMEM), ((A, 2 * B), f32, VMEM)),
+        tuple((x, VMEM) for x in (coefs, fields, lifted, halves)),
+        limit=4,
+        work=10**9,
+    )
+
+
+def second_lift(coefs, fields, lifted, ends, halves, parts, grams, px, py, cz):
+    def body(coefs, fields_ref, lifted_ref, halves_ref, parts_in, start_ref, middle_ref, inner_ref, *refs):
         end_refs, (parts, packed) = refs[:4], refs[4:]
-
-        def step(p, rows, gram):
-            every = []
-            for y in rows:
-                outer, damping, inner = [coefs[k, p, pl.ds(y, 1), :] for k in range(3)]
-                now = fields_ref[p, y]
-                second = (
-                    outer * laplace(lifted_ref, p, y, 0, px, py, cz)
-                    + damping * now[:B].astype(f32)
-                    + inner * laplace(fields_ref, p, y, B, px, py, cz)
-                )
-                for other in ((p - 1, y), (p + 1, y), (p, y - 1), (p, y + 1)):
-                    received = outside(end_refs, *other, px, py)
-                    if received is not None:
-                        second = second - received
-                every.append(jnp.concatenate([now, halves_ref[p, y], split(second)], 0))
-                parts[p, y] = every[-1]
-            every = jnp.concatenate(every, 1)
-            return gram + lax.dot_general(
-                every, every[S + 2 * B :], (((1,), (1,)), ((), ())), preferred_element_type=f32
-            )
-
-        last = sweep(px, py, step, jnp.zeros((A, 2 * B), f32))
+        last = second_rows(coefs, fields_ref, lifted_ref, halves_ref, end_refs, parts, False, px, py, cz)
+        last = last + inner_ref[...]
         last = jnp.concatenate([last, jnp.zeros((A, 128 - 2 * B), f32)], 1)
         last = last + pltpu.roll(last, 128 - B, 1)
         middle = jnp.concatenate([middle_ref[...], jnp.zeros((S + 2 * B, 128 - 2 * B), f32)], 1)
@@ -357,8 +396,9 @@
     return call(
         body,
         (((px, py, A, cz), bf16, VMEM), ((2 * B, 128), f32, VMEM)),
-        tuple((x, VMEM) for x in (coefs, fields, lifted, halves) + tuple(grams) + ends),
+        tuple((x, VMEM) for x in (coefs, fields, lifted, halves, parts) + tuple(grams) + ends),
         limit=4,
+        aliases={4: 0},
     )
 
 
@@ -505,10 +545,13 @@
     fields, coefs, plane_even, *rows = read_start(labels, start, px, py, cz)
     edges = exchange(plane_even, face, *rows)
     start_gram = start_products(fields, px, py)
-    lifted, halves, *ends = first_lift(coefs, fields, start_gram, edges, px, py, cz)
+    lifted, halves = first_lift_inner(coefs, fields, px, py, cz)
+    lifted, halves, *ends = first_lift(coefs, fields, start_gram, lifted, halves, edges, px, py, cz)
     ends = exchange(*ends)
     middle_gram = lifted_products(fields, halves, px, py)
-    parts, packed = second_lift(coefs, fields, lifted, ends, halves, (start_gram, middle_gram), px, py, cz)
+    parts, inner_gram = second_lift_inner(coefs, fields, lifted, halves, px, py, cz)
+    grams = (start_gram, middle_gram, inner_gram)
+    parts, packed = second_lift(coefs, fields, lifted, ends, halves, parts, grams, px, py, cz)
     basis_cols, turned = finish(sum_all(packed), parts, cells_total, px, py, cz)
     return (basis_cols, jnp.swapaxes(turned, 1, 2))
 

time: 81.7 us -> 78.3 us (0.958)
  blocking collectives: 37.7 us -> 35.7 us
  waiting for transfers between devices: 4.85 us -> 3.88 us
    all_to_all x1, blocking collectives: 24.6 us -> 22.7 us  [sum_all(): lax.all_to_all(own, WIDE, 0, 0, tiled=True)]
    ppermute x8, waiting for transfers between devices: 4.85 us -> 3.88 us  [swap(): return lax.ppermute(edge, axis, pairs + [(b, a) for a, b in pairs])]
    pallas_call x9 -> x11, Pallas kernels: 22.8 us -> 22.3 us  [call(): pl.pallas_call(body, out_shape=tuple(shapes), in_specs=specs, out_specs=t...]
  transfers between devices with their start and end apart: 8 -> 8, of which waited for: 2 -> 2; matrix products, arithmetic and copies ran while one was open for 0% -> 0% of each run, Pallas kernels for 6% -> 10%
where the time goes in v4:
time: 78.3 us; the launch traced here: 78 us
  blocking collectives  35.7 us (46%)
  Pallas kernels  22.3 us (28%)
  starting transfers between devices  15.3 us (20%)
  waiting for transfers between devices  3.88 us (5%)
  between operations  0.81 us (1%)
    all_to_all x1, blocking collectives, sum_all(): lax.all_to_all(own, WIDE, 0, 0, tiled=True)  22.7 us
    pallas_call x11, Pallas kernels, call(): pl.pallas_call(body, out_shape=tuple(shapes), in_specs=specs, out_specs=t...  22.3 us
    ppermute x8, starting transfers between devices, swap(): return lax.ppermute(edge, axis, pairs + [(b, a) for a, b in pairs])  15.3 us
    all_to_all x1, blocking collectives, sum_all(): return lax.all_to_all(own, NARROW, 0, 0, tiled=True)  11.2 us
    ppermute x8, waiting for transfers between devices, swap(): return lax.ppermute(edge, axis, pairs + [(b, a) for a, b in pairs])  3.88 us
    all_gather x1, blocking collectives, sum_all(): both = lax.all_gather(table, 'plane_2')  1.83 us
  transfers between devices with their start and end apart: 8, of which 2 were waited for; matrix products, arithmetic and copies ran while one was open for 0% of the time, Pallas kernels for 10%

profile of v4, /device:TPU:1, one launch (start us, length us, event | category | flops | bytes accessed | tf_op | source)
XLA Modules:
  0.0 78.0 jit_solution(10009568711133035369)
XLA Ops:
  0.6 0.0 copy-start
  0.6 0.0 copy-start.1
  0.6 1.6 %shard_map.44 = f32[33,16,384]{2,1,0:T(8,128)S(1)} custom-call(s32[4,16,384]{2,1,0:T(8,128)} %labels_in.1, s32[48,4,16,384]{3,2,1,0:T(8,128)} %bitcast.3), custom_call_target="tpu_custom_call" | custom-call | tf_op jit(solution)/shard_map/pallas_call | solution.py:79
  2.3 5.1 %collective-permute-start.1 = (f32[33,16,384]{2,1,0:T(8,128)S(1)}, f32[33,16,384]{2,1,0:T(8,128)S(1)}, u32[]{:S(2)}, u32[]{:S(2)}) collective-permute-start(f32[33,16,384]{2,1,0:T(8,128)S(1)} %shard_map.44), channel_id=1, source_target_pairs={{4,8},{12,16},{20,24},{28,32},{36,40},{44,48},{52,56},{60,64},{68,... | collective-permute-start | bytes 2433032 | tf_op jit(solution)/shard_map/ppermute | solution.py:61
  7.3 0.0 copy-done
  7.3 0.0 copy-done.1
  7.4 1.6 %shard_map.41 = (bf16[4,16,48,384]{3,2,1,0:T(8,128)(2,1)S(1)}, f32[3,4,16,384]{3,2,1,0:T(8,128)S(1)}, f32[33,16,384]{2,1,0:T(8,128)S(1)}, f32[9,16,384]{2,1,0:T(8,128)S(1)}, f32[9,16,384]{2,1,0:T(8,128)S(1)}) custom-call(s32[4,16,384]{2,1,0:T(8,128)S(1)} %copy-done.1, s32[48,4,16,384]{3,2,1,0:T(8,128)S(1)} %bitcast.4), custom_call_target="tpu_custom_call" | custom-call | tf_op jit(solution)/shard_map/pallas_call | solution.py:79
  9.0 0.1 collective-permute-start
  9.1 1.4 %collective-permute-start.2 = (f32[9,16,384]{2,1,0:T(8,128)S(1)}, f32[9,16,384]{2,1,0:T(8,128)S(1)}, u32[]{:S(2)}, u32[]{:S(2)}) collective-permute-start(f32[9,16,384]{2,1,0:T(8,128)S(1)} %get-tuple-element.26), channel_id=1, source_target_pairs={{0,1},{2,3},{1,0},{3,2},{4,5},{6,7},{5,4},{7,6},{8,9},{10,11},{9,8... | collective-permute-start | bytes 663560 | tf_op jit(solution)/shard_map/ppermute | solution.py:61
  10.5 0.7 collective-permute-start.3
  11.2 1.3 %shard_map.42.gram_ref.start_ref = f32[48,48]{1,0:T(8,128)S(1)} custom-call(bf16[4,16,48,384]{3,2,1,0:T(8,128)(2,1)S(1)} %get-tuple-element.22.fields_ref), custom_call_target="tpu_custom_call" | custom-call | flops 1000000000 | tf_op jit(solution)/shard_map/pallas_call | solution.py:79
  12.4 1.0 %shard_map.43 = (f32[4,16,16,384]{3,2,1,0:T(8,128)S(1)}, bf16[4,16,32,384]{3,2,1,0:T(8,128)(2,1)S(1)}) custom-call(f32[3,4,16,384]{3,2,1,0:T(8,128)S(1)} %get-tuple-element.21.coefs, bf16[4,16,48,384]{3,2,1,0:T(8,128)(2,1)S(1)} %get-tuple-element.22.fields_ref), custom_call_target="tpu_custom_call" | custom-call | flops 1000000000 | tf_op jit(solution)/shard_map/pallas_call | solution.py:79
  13.4 2.4 %collective-permute-done.2.refs_2_ = f32[9,16,384]{2,1,0:T(8,128)S(1)} collective-permute-done((f32[9,16,384]{2,1,0:T(8,128)S(1)}, f32[9,16,384]{2,1,0:T(8,128)S(1)}, u32[]{:S(2)}, u32[]{:S(2)}) %collective-permute-start.2) | collective-permute-done | bytes 221216 | tf_op jit(solution)/shard_map/ppermute | solution.py:61
  15.8 0.0 collective-permute-done.3.refs_3_
  15.8 1.5 %collective-permute-done.1.refs_1_ = f32[33,16,384]{2,1,0:T(8,128)S(1)} collective-permute-done((f32[33,16,384]{2,1,0:T(8,128)S(1)}, f32[33,16,384]{2,1,0:T(8,128)S(1)}, u32[]{:S(2)}, u32[]{:S(2)}) %collective-permute-start.1) | collective-permute-done | bytes 811040 | tf_op jit(solution)/shard_map/ppermute | solution.py:61
  17.3 0.0 collective-permute-done.refs_0_
  17.3 1.6 %shard_map.45 = (f32[4,16,16,384]{3,2,1,0:T(8,128)S(1)}, bf16[4,16,32,384]{3,2,1,0:T(8,128)(2,1)S(1)}, f32[16,16,384]{2,1,0:T(8,128)S(1)}, f32[16,16,384]{2,1,0:...) custom-call(f32[3,4,16,384]{3,2,1,0:T(8,128)S(1)} %get-tuple-element, ...), custom_call_target="tpu_custom_call", output_to_operand_aliasing={{0}: (3, {}), {1}: (4, {})} | custom-call | tf_op jit(solution)/shard_map/pallas_call | solution.py:79
  18.9 0.1 collective-permute-start.4
  19.0 3.9 %collective-permute-start.5 = (f32[16,16,384]{2,1,0:T(8,128)S(1)}, f32[16,16,384]{2,1,0:T(8,128)S(1)}, u32[]{:S(2)}, u32[]{:S(2)}) collective-permute-start(f32[16,16,384]{2,1,0:T(8,128)S(1)} %get-tuple-element.33), channel_id=1, source_target_pairs={{4,8},{12,16},{20,24},{28,32},{36,40},{44,48},{52,56},{60,64},{68,... | collective-permute-start | bytes 1179656 | tf_op jit(solution)/shard_map/ppermute | solution.py:61
  22.9 3.4 %collective-permute-start.6 = (f32[4,16,384]{2,1,0:T(8,128)S(1)}, f32[4,16,384]{2,1,0:T(8,128)S(1)}, u32[]{:S(2)}, u32[]{:S(2)}) collective-permute-start(f32[4,16,384]{2,1,0:T(8,128)S(1)} %get-tuple-element.34), channel_id=1, source_target_pairs={{0,1},{2,3},{1,0},{3,2},{4,5},{6,7},{5,4},{7,6},{8,9},{10,11},{9,8... | collective-permute-start | bytes 294920 | tf_op jit(solution)/shard_map/ppermute | solution.py:61
  26.3 0.7 collective-permute-start.7
  27.0 2.2 %shard_map.47.middle_ref = f32[80,32]{1,0:T(8,128)S(1)} custom-call(bf16[4,16,48,384]{3,2,1,0:T(8,128)(2,1)S(1)} %get-tuple-element.22.fields_ref, bf16[4,16,32,384]{3,2,1,0:T(8,128)(2,1)S(1)} %get-tuple-element.29.halves_ref), custom_call_target="tpu_custom_call" | custom-call | flops 1000000000 | tf_op jit(solution)/shard_map/pallas_call | solution.py:79
  29.2 1.9 %shard_map.46 = (bf16[4,16,112,384]{3,2,1,0:T(8,128)(2,1)S(1)}, f32[112,32]{1,0:T(8,128)S(1)}) custom-call(f32[3,4,16,384]{3,2,1,0:T(8,128)S(1)} %get-tuple-element.21.coefs, bf16[4,16,48,384]{3,2,1,0:T(8,128)(2,1)S(1)} %get-tuple-element.22.fields_ref, f32[4,16,16,384]{3,2,1,0:T(8,128)S(1)} %get-tuple-element.28.lifted_ref, ...), custom_call_target="tpu_custom_call" | custom-call | flops 1000000000 | tf_op jit(solution)/shard_map/pallas_call | solution.py:79
  31.1 0.0 collective-permute-done.6.refs_2_
  31.1 0.0 collective-permute-done.7.refs_3_
  31.2 0.0 collective-permute-done.4.refs_0_
  31.2 0.0 collective-permute-done.5.refs_1_
  31.2 2.9 %shard_map.48 = (bf16[4,16,112,384]{3,2,1,0:T(8,128)(2,1)S(1)}, f32[32,128]{1,0:T(8,128)S(1)}) custom-call(f32[3,4,16,384]{3,2,1,0:T(8,128)S(1)} %get-tuple-element.21.coefs, bf16[4,16,48,384]{3,2,1,0:T(8,128)(2,1)S(1)} %get-tuple-element.22.fields_ref, f32[4,16,16,384]{3,2,1,0:T(8,128)S(1)} %get-tuple-element.28.lifted_ref, ...), custom_call_target="tpu_custom_call", output_to_operand_aliasing={{0}: (4, {})} | custom-call | tf_op jit(solution)/shard_map/pallas_call | solution.py:79
  34.1 1.8 %all-gather = f32[64,128]{1,0:T(8,128)S(1)} all-gather(f32[32,128]{1,0:T(8,128)S(1)} %get-tuple-element.36), channel_id=2, replica_groups=mesh['plane_0'=4,'plane_1'=8,'plane_2'=2,'depth'=4] {'plane_2'}, dimensions={0}, use_global_device_ids=true | all-gather | bytes 49152 | tf_op jit(solution)/shard_map/all_gather | solution.py:52
  35.9 22.7 %all_to_all.10.pieces_ref = f32[32,16,128]{2,1,0:T(8,128)S(1)} all-to-all(f32[32,16,128]{2,1,0:T(8,128)S(1)} %shard_map.49), channel_id=1, replica_groups=mesh['plane_0'=4,'plane_1'=8,'plane_2'=2,'depth'=4] {'plane_1','depth'}, dimensions={0} | all-to-all | bytes 524288 | tf_op jit(solution)/shard_map/all_to_all | solution.py:54
  58.6 11.2 %all_to_all.11.packed_ref = f32[8,16,128]{2,1,0:T(8,128)S(1)} all-to-all(f32[8,16,128]{2,1,0:T(8,128)S(1)} %shard_map.50), channel_id=1, replica_groups=mesh['plane_0'=4,'plane_1'=8,'plane_2'=2,'depth'=4] {'plane_0','plane_2'}, dimensions={0} | all-to-all | bytes 131072 | tf_op jit(solution)/shard_map/all_to_all | solution.py:55
  69.9 8.1 %shard_map.51 = (f32[80,4,16,384]{3,2,1,0:T(8,128)}, f32[3,48,80]{2,1,0:T(8,128)}) custom-call(f32[8,16,128]{2,1,0:T(8,128)S(1)} %all_to_all.11.packed_ref, bf16[4,16,112,384]{3,2,1,0:T(8,128)(2,1)S(1)} %get-tuple-element.37.parts_ref), custom_call_target="tpu_custom_call" | custom-call | tf_op jit(solution)/shard_map/pallas_call | solution.py:79
  (2 shorter events, 0.1 us)
Async XLA Ops:
  0.6 6.7 %copy-start = (s32[3,16,4,16,384]{4,3,2,1,0:T(8,128)S(1)}, s32[3,16,4,16,384]{4,3,2,1,0:T(8,128)}, u32[]{:S(2)}) copy-start(s32[3,16,4,16,384]{4,3,2,1,0:T(8,128)} %param.3) | copy-start | bytes 14155780
  0.6 6.7 %copy-start.1 = (s32[4,16,384]{2,1,0:T(8,128)S(1)}, s32[4,16,384]{2,1,0:T(8,128)}, u32[]{:S(2)}) copy-start(s32[4,16,384]{2,1,0:T(8,128)} %labels_in.1) | copy-start | bytes 294916
  2.3 15.0 %collective-permute-start.1 = (f32[33,16,384]{2,1,0:T(8,128)S(1)}, f32[33,16,384]{2,1,0:T(8,128)S(1)}, u32[]{:S(2)}, u32[]{:S(2)}) collective-permute-start(f32[33,16,384]{2,1,0:T(8,128)S(1)} %shard_map.44), channel_id=1, source_target_pairs={{4,8},{12,16},{20,24},{28,32},{36,40},{44,48},{52,56},{60,64},{68,... | collective-permute-start | bytes 2433032 | tf_op jit(solution)/shard_map/ppermute | solution.py:61
  9.0 8.3 %collective-permute-start = (f32[33,16,384]{2,1,0:T(8,128)S(1)}, f32[33,16,384]{2,1,0:T(8,128)S(1)}, u32[]{:S(2)}, u32[]{:S(2)}) collective-permute-start(f32[33,16,384]{2,1,0:T(8,128)S(1)} %get-tuple-element.25), channel_id=1, source_target_pairs={{0,4},{8,12},{16,20},{24,28},{32,36},{40,44},{48,52},{56,60},{64,6... | collective-permute-start | bytes 2433032 | tf_op jit(solution)/shard_map/ppermute | solution.py:61
  9.1 6.7 %collective-permute-start.2 = (f32[9,16,384]{2,1,0:T(8,128)S(1)}, f32[9,16,384]{2,1,0:T(8,128)S(1)}, u32[]{:S(2)}, u32[]{:S(2)}) collective-permute-start(f32[9,16,384]{2,1,0:T(8,128)S(1)} %get-tuple-element.26), channel_id=1, source_target_pairs={{0,1},{2,3},{1,0},{3,2},{4,5},{6,7},{5,4},{7,6},{8,9},{10,11},{9,8... | collective-permute-start | bytes 663560 | tf_op jit(solution)/shard_map/ppermute | solution.py:61
  10.5 5.3 %collective-permute-start.3 = (f32[9,16,384]{2,1,0:T(8,128)S(1)}, f32[9,16,384]{2,1,0:T(8,128)S(1)}, u32[]{:S(2)}, u32[]{:S(2)}) collective-permute-start(f32[9,16,384]{2,1,0:T(8,128)S(1)} %get-tuple-element.27), channel_id=1, source_target_pairs={{1,2},{2,1},{5,6},{6,5},{9,10},{10,9},{13,14},{14,13},{17,18},{18,... | collective-permute-start | bytes 663560 | tf_op jit(solution)/shard_map/ppermute | solution.py:61
  18.9 12.3 %collective-permute-start.4 = (f32[16,16,384]{2,1,0:T(8,128)S(1)}, f32[16,16,384]{2,1,0:T(8,128)S(1)}, u32[]{:S(2)}, u32[]{:S(2)}) collective-permute-start(f32[16,16,384]{2,1,0:T(8,128)S(1)} %get-tuple-element.32), channel_id=1, source_target_pairs={{0,4},{8,12},{16,20},{24,28},{32,36},{40,44},{48,52},{56,60},{64,6... | collective-permute-start | bytes 1179656 | tf_op jit(solution)/shard_map/ppermute | solution.py:61
  19.0 12.2 %collective-permute-start.5 = (f32[16,16,384]{2,1,0:T(8,128)S(1)}, f32[16,16,384]{2,1,0:T(8,128)S(1)}, u32[]{:S(2)}, u32[]{:S(2)}) collective-permute-start(f32[16,16,384]{2,1,0:T(8,128)S(1)} %get-tuple-element.33), channel_id=1, source_target_pairs={{4,8},{12,16},{20,24},{28,32},{36,40},{44,48},{52,56},{60,64},{68,... | collective-permute-start | bytes 1179656 | tf_op jit(solution)/shard_map/ppermute | solution.py:61
  22.9 8.2 %collective-permute-start.6 = (f32[4,16,384]{2,1,0:T(8,128)S(1)}, f32[4,16,384]{2,1,0:T(8,128)S(1)}, u32[]{:S(2)}, u32[]{:S(2)}) collective-permute-start(f32[4,16,384]{2,1,0:T(8,128)S(1)} %get-tuple-element.34), channel_id=1, source_target_pairs={{0,1},{2,3},{1,0},{3,2},{4,5},{6,7},{5,4},{7,6},{8,9},{10,11},{9,8... | collective-permute-start | bytes 294920 | tf_op jit(solution)/shard_map/ppermute | solution.py:61
  26.3 4.8 %collective-permute-start.7 = (f32[4,16,384]{2,1,0:T(8,128)S(1)}, f32[4,16,384]{2,1,0:T(8,128)S(1)}, u32[]{:S(2)}, u32[]{:S(2)}) collective-permute-start(f32[4,16,384]{2,1,0:T(8,128)S(1)} %get-tuple-element.35), channel_id=1, source_target_pairs={{1,2},{2,1},{5,6},{6,5},{9,10},{10,9},{13,14},{14,13},{17,18},{18,... | collective-permute-start | bytes 294920 | tf_op jit(solution)/shard_map/ppermute | solution.py:61

commit v5 on v4

--- a/solution.py
+++ b/solution.py
@@ -108,20 +108,21 @@
 
     def body(labels_in, start_ref, face, raw, labels_ref, sems):
         p = parities()[0] * (px - 1)
-        copies = [pltpu.make_async_copy(labels_in.at[p], labels_ref, sems.at[2 * halves])]
+        copies = []
         for h in range(halves):
             for i in range(2):
                 source = start_ref.at[pl.ds(2 * B * i, B), p, pl.ds(8 * h, 8), :]
                 copies.append(pltpu.make_async_copy(source, raw.at[h, pl.ds(B * i, B)], sems.at[2 * h + i]))
+        copies.append(pltpu.make_async_copy(labels_in.at[p], labels_ref, sems.at[2 * halves]))
         for each in copies:
             each.start()
-        for each in copies:
-            each.wait()
         for h in range(halves):
-            turned = jnp.swapaxes(raw[h].astype(f32), 0, 1)
-            for i in range(8):
-                face[16 * h + 2 * i] = turned[i, :B]
-                face[16 * h + 2 * i + 1] = turned[i, B:]
+            for j in range(2):
+                copies[2 * h + j].wait()
+                turned = jnp.swapaxes(raw[h, B * j : B * j + B].astype(f32), 0, 1)
+                for i in range(8):
+                    face[16 * h + 2 * i + j] = turned[i]
+        copies[-1].wait()
         face[2 * py, :py] = labels_ref[...].astype(f32)
 
     return call(
@@ -245,13 +246,26 @@
     sweep(px, py, inner, step, 0)
 
 
+def lifted_rows(fields_ref, halves_ref, inner, px, py):
+    def step(p, rows, gram):
+        both = jnp.concatenate([jnp.concatenate([fields_ref[p, y], halves_ref[p, y]], 0) for y in rows], 1)
+        return gram + lax.dot_general(both, both[S:], (((1,), (1,)), ((), ())), preferred_element_type=f32)
+
+    return sweep(px, py, inner, step, jnp.zeros((S + 2 * B, 2 * B), f32))
+
+
 def first_lift_inner(coefs, fields, px, py, cz):
-    def body(coefs, fields_ref, lifted, halves):
+    def body(coefs, fields_ref, lifted, halves, gram_ref):
         first_rows(coefs, fields_ref, None, lifted, halves, True, px, py, cz)
-
-    return call(
-        body,
-        (((px, py, B, cz), f32, VMEM), ((px, py, 2 * B, cz), bf16, VMEM)),
+        gram_ref[...] = lifted_rows(fields_ref, halves, True, px, py)
+
+    return call(
+        body,
+        (
+            ((px, py, B, cz), f32, VMEM),
+            ((px, py, 2 * B, cz), bf16, VMEM),
+            ((S + 2 * B, 2 * B), f32, VMEM),
+        ),
         ((coefs, VMEM), (fields, VMEM)),
         limit=4,
         work=10**9,
@@ -317,13 +331,7 @@
 
 def lifted_products(fields, halves, px, py):
     def body(fields_ref, halves_ref, gram_ref):
-        def both(r):
-            return jnp.concatenate([fields_ref[r // py, r % py], halves_ref[r // py, r % py]], 0)
-
-        def right(r):
-            return halves_ref[r // py, r % py]
-
-        gram_ref[...] = gram_loop(8, px * py, both, right, (S + 2 * B, 2 * B))
+        gram_ref[...] = lifted_rows(fields_ref, halves_ref, False, px, py)
 
     return call(
         body,
@@ -373,13 +381,13 @@
 
 
 def second_lift(coefs, fields, lifted, ends, halves, parts, grams, px, py, cz):
-    def body(coefs, fields_ref, lifted_ref, halves_ref, parts_in, start_ref, middle_ref, inner_ref, *refs):
+    def body(coefs, fields_ref, lifted_ref, halves_ref, parts_in, start_ref, middle_ref, within_ref, inner_ref, *refs):
         end_refs, (parts, packed) = refs[:4], refs[4:]
         last = second_rows(coefs, fields_ref, lifted_ref, halves_ref, end_refs, parts, False, px, py, cz)
         last = last + inner_ref[...]
         last = jnp.concatenate([last, jnp.zeros((A, 128 - 2 * B), f32)], 1)
         last = last + pltpu.roll(last, 128 - B, 1)
-        middle = jnp.concatenate([middle_ref[...], jnp.zeros((S + 2 * B, 128 - 2 * B), f32)], 1)
+        middle = jnp.concatenate([middle_ref[...] + within_ref[...], jnp.zeros((S + 2 * B, 128 - 2 * B), f32)], 1)
         middle = middle + pltpu.roll(middle, 128 - B, 1)
         middle = jnp.concatenate([middle[:S], middle[S : S + B] + middle[S + B :]], 0)
         last = jnp.concatenate([last[:S], last[S : S + B] + last[S + B : S + 2 * B], last[S + 2 * B : S + 3 * B] + last[S + 3 * B :]], 0)
@@ -495,7 +503,8 @@
         matrix = matrix + place(inverse, 3, 4) + place(inverse, 4, 5) + place(inverse, 4, 6)
         matrix = matrix[:, :A]
         high = matrix.astype(bf16)
-        weights = jnp.concatenate([high, (matrix - high.astype(f32)).astype(bf16)], 1)
+        low = (matrix - high.astype(f32)).astype(bf16)
+        weights = jnp.concatenate([high, low[:, : S + B], low[:, S + 2 * B : S + 3 * B]], 1)
 
         def copy(chunk):
             p, h = chunk // halves, chunk % halves
@@ -505,7 +514,7 @@
             p, h = chunk // halves, chunk % halves
             for y in range(0, 8, 2):
                 part = jnp.concatenate([parts_ref[p, 8 * h + y + i] for i in range(2)], 1)
-                out = jnp.dot(weights, jnp.concatenate([part, part], 0), preferred_element_type=f32)
+                out = jnp.dot(weights, jnp.concatenate([part, part[: S + B], part[S + 2 * B : S + 3 * B]], 0), preferred_element_type=f32)
                 for i in range(2):
                     ready[chunk, :, y + i, :] = out[:, cz * i : cz * i + cz]
             copy(chunk).start()
@@ -545,12 +554,12 @@
     fields, coefs, plane_even, *rows = read_start(labels, start, px, py, cz)
     edges = exchange(plane_even, face, *rows)
     start_gram = start_products(fields, px, py)
-    lifted, halves = first_lift_inner(coefs, fields, px, py, cz)
+    lifted, halves, within_gram = first_lift_inner(coefs, fields, px, py, cz)
     lifted, halves, *ends = first_lift(coefs, fields, start_gram, lifted, halves, edges, px, py, cz)
     ends = exchange(*ends)
     middle_gram = lifted_products(fields, halves, px, py)
     parts, inner_gram = second_lift_inner(coefs, fields, lifted, halves, px, py, cz)
-    grams = (start_gram, middle_gram, inner_gram)
+    grams = (start_gram, middle_gram, within_gram, inner_gram)
     parts, packed = second_lift(coefs, fields, lifted, ends, halves, parts, grams, px, py, cz)
     basis_cols, turned = finish(sum_all(packed), parts, cells_total, px, py, cz)
     return (basis_cols, jnp.swapaxes(turned, 1, 2))

time: 78.3 us -> 77.9 us (level)
  waiting for transfers between devices: 3.88 us -> 2.84 us
  blocking collectives: 35.7 us -> 36.5 us
    ppermute x8, waiting for transfers between devices: 3.88 us -> 2.84 us  [swap(): return lax.ppermute(edge, axis, pairs + [(b, a) for a, b in pairs])]
    all_to_all x1, blocking collectives: 22.7 us -> 23.5 us  [sum_all(): lax.all_to_all(own, WIDE, 0, 0, tiled=True)]
  transfers between devices with their start and end apart: 8 -> 8, of which waited for: 2 -> 2; matrix products, arithmetic and copies ran while one was open for 0% -> 0% of each run, Pallas kernels for 10% -> 11%
where the time goes in v5:
time: 77.9 us; the launch traced here: 77.6 us
  blocking collectives  36.5 us (47%)
  Pallas kernels  22.1 us (28%)
  starting transfers between devices  15.3 us (20%)
  waiting for transfers between devices  2.84 us (4%)
  between operations  0.81 us (1%)
    all_to_all x1, blocking collectives, sum_all(): lax.all_to_all(own, WIDE, 0, 0, tiled=True)  23.5 us
    pallas_call x11, Pallas kernels, call(): pl.pallas_call(body, out_shape=tuple(shapes), in_specs=specs, out_specs=t...  22.1 us
    ppermute x8, starting transfers between devices, swap(): return lax.ppermute(edge, axis, pairs + [(b, a) for a, b in pairs])  15.3 us
    all_to_all x1, blocking collectives, sum_all(): return lax.all_to_all(own, NARROW, 0, 0, tiled=True)  11.2 us
    ppermute x8, waiting for transfers between devices, swap(): return lax.ppermute(edge, axis, pairs + [(b, a) for a, b in pairs])  2.84 us
    all_gather x1, blocking collectives, sum_all(): both = lax.all_gather(table, 'plane_2')  1.83 us
  transfers between devices with their start and end apart: 8, of which 2 were waited for; matrix products, arithmetic and copies ran while one was open for 0% of the time, Pallas kernels for 11%

profile of v5, /device:TPU:1, one launch (start us, length us, event | category | flops | bytes accessed | tf_op | source)
XLA Modules:
  0.0 77.6 jit_solution(4453822517689733113)
XLA Ops:
  0.6 0.0 copy-start
  0.6 0.0 copy-start.1
  0.6 1.5 %shard_map.44 = f32[33,16,384]{2,1,0:T(8,128)S(1)} custom-call(s32[4,16,384]{2,1,0:T(8,128)} %labels_in.1, s32[48,4,16,384]{3,2,1,0:T(8,128)} %bitcast.3), custom_call_target="tpu_custom_call" | custom-call | tf_op jit(solution)/shard_map/pallas_call | solution.py:79
  2.1 5.1 %collective-permute-start.1 = (f32[33,16,384]{2,1,0:T(8,128)S(1)}, f32[33,16,384]{2,1,0:T(8,128)S(1)}, u32[]{:S(2)}, u32[]{:S(2)}) collective-permute-start(f32[33,16,384]{2,1,0:T(8,128)S(1)} %shard_map.44), channel_id=1, source_target_pairs={{4,8},{12,16},{20,24},{28,32},{36,40},{44,48},{52,56},{60,64},{68,... | collective-permute-start | bytes 2433032 | tf_op jit(solution)/shard_map/ppermute | solution.py:61
  7.2 0.0 copy-done
  7.2 0.0 copy-done.1
  7.2 1.6 %shard_map.41 = (bf16[4,16,48,384]{3,2,1,0:T(8,128)(2,1)S(1)}, f32[3,4,16,384]{3,2,1,0:T(8,128)S(1)}, f32[33,16,384]{2,1,0:T(8,128)S(1)}, f32[9,16,384]{2,1,0:T(8,128)S(1)}, f32[9,16,384]{2,1,0:T(8,128)S(1)}) custom-call(s32[4,16,384]{2,1,0:T(8,128)S(1)} %copy-done.1, s32[48,4,16,384]{3,2,1,0:T(8,128)S(1)} %bitcast.4), custom_call_target="tpu_custom_call" | custom-call | tf_op jit(solution)/shard_map/pallas_call | solution.py:79
  8.9 0.1 collective-permute-start
  9.0 1.4 %collective-permute-start.2 = (f32[9,16,384]{2,1,0:T(8,128)S(1)}, f32[9,16,384]{2,1,0:T(8,128)S(1)}, u32[]{:S(2)}, u32[]{:S(2)}) collective-permute-start(f32[9,16,384]{2,1,0:T(8,128)S(1)} %get-tuple-element.27), channel_id=1, source_target_pairs={{0,1},{2,3},{1,0},{3,2},{4,5},{6,7},{5,4},{7,6},{8,9},{10,11},{9,8... | collective-permute-start | bytes 663560 | tf_op jit(solution)/shard_map/ppermute | solution.py:61
  10.3 0.7 collective-permute-start.3
  11.0 1.3 %shard_map.42.gram_ref.start_ref = f32[48,48]{1,0:T(8,128)S(1)} custom-call(bf16[4,16,48,384]{3,2,1,0:T(8,128)(2,1)S(1)} %get-tuple-element.23.fields_ref), custom_call_target="tpu_custom_call" | custom-call | flops 1000000000 | tf_op jit(solution)/shard_map/pallas_call | solution.py:79
  12.3 2.0 %shard_map.43 = (f32[4,16,16,384]{3,2,1,0:T(8,128)S(1)}, bf16[4,16,32,384]{3,2,1,0:T(8,128)(2,1)S(1)}, f32[80,32]{1,0:T(8,128)S(1)}) custom-call(f32[3,4,16,384]{3,2,1,0:T(8,128)S(1)} %get-tuple-element.22.coefs, bf16[4,16,48,384]{3,2,1,0:T(8,128)(2,1)S(1)} %get-tuple-element.23.fields_ref), custom_call_target="tpu_custom_call" | custom-call | flops 1000000000 | tf_op jit(solution)/shard_map/pallas_call | solution.py:79
  14.3 1.3 %collective-permute-done.2.refs_2_ = f32[9,16,384]{2,1,0:T(8,128)S(1)} collective-permute-done((f32[9,16,384]{2,1,0:T(8,128)S(1)}, f32[9,16,384]{2,1,0:T(8,128)S(1)}, u32[]{:S(2)}, u32[]{:S(2)}) %collective-permute-start.2) | collective-permute-done | bytes 221216 | tf_op jit(solution)/shard_map/ppermute | solution.py:61
  15.6 0.0 collective-permute-done.3.refs_3_
  15.6 1.5 %collective-permute-done.1.refs_1_ = f32[33,16,384]{2,1,0:T(8,128)S(1)} collective-permute-done((f32[33,16,384]{2,1,0:T(8,128)S(1)}, f32[33,16,384]{2,1,0:T(8,128)S(1)}, u32[]{:S(2)}, u32[]{:S(2)}) %collective-permute-start.1) | collective-permute-done | bytes 811040 | tf_op jit(solution)/shard_map/ppermute | solution.py:61
  17.1 0.0 collective-permute-done.refs_0_
  17.1 1.6 %shard_map.45 = (f32[4,16,16,384]{3,2,1,0:T(8,128)S(1)}, bf16[4,16,32,384]{3,2,1,0:T(8,128)(2,1)S(1)}, f32[16,16,384]{2,1,0:T(8,128)S(1)}, f32[16,16,384]{2,1,0:...) custom-call(f32[3,4,16,384]{3,2,1,0:T(8,128)S(1)} %get-tuple-element, ...), custom_call_target="tpu_custom_call", output_to_operand_aliasing={{0}: (3, {}), {1}: (4, {})} | custom-call | tf_op jit(solution)/shard_map/pallas_call | solution.py:79
  18.7 0.1 collective-permute-start.4
  18.8 3.9 %collective-permute-start.5 = (f32[16,16,384]{2,1,0:T(8,128)S(1)}, f32[16,16,384]{2,1,0:T(8,128)S(1)}, u32[]{:S(2)}, u32[]{:S(2)}) collective-permute-start(f32[16,16,384]{2,1,0:T(8,128)S(1)} %get-tuple-element.35), channel_id=1, source_target_pairs={{4,8},{12,16},{20,24},{28,32},{36,40},{44,48},{52,56},{60,64},{68,... | collective-permute-start | bytes 1179656 | tf_op jit(solution)/shard_map/ppermute | solution.py:61
  22.7 3.4 %collective-permute-start.6 = (f32[4,16,384]{2,1,0:T(8,128)S(1)}, f32[4,16,384]{2,1,0:T(8,128)S(1)}, u32[]{:S(2)}, u32[]{:S(2)}) collective-permute-start(f32[4,16,384]{2,1,0:T(8,128)S(1)} %get-tuple-element.36), channel_id=1, source_target_pairs={{0,1},{2,3},{1,0},{3,2},{4,5},{6,7},{5,4},{7,6},{8,9},{10,11},{9,8... | collective-permute-start | bytes 294920 | tf_op jit(solution)/shard_map/ppermute | solution.py:61
  26.2 0.7 collective-permute-start.7
  26.8 1.4 %shard_map.47.middle_ref = f32[80,32]{1,0:T(8,128)S(1)} custom-call(bf16[4,16,48,384]{3,2,1,0:T(8,128)(2,1)S(1)} %get-tuple-element.23.fields_ref, bf16[4,16,32,384]{3,2,1,0:T(8,128)(2,1)S(1)} %get-tuple-element.30.halves_ref), custom_call_target="tpu_custom_call" | custom-call | flops 1000000000 | tf_op jit(solution)/shard_map/pallas_call | solution.py:79
  28.2 1.9 %shard_map.46 = (bf16[4,16,112,384]{3,2,1,0:T(8,128)(2,1)S(1)}, f32[112,32]{1,0:T(8,128)S(1)}) custom-call(f32[3,4,16,384]{3,2,1,0:T(8,128)S(1)} %get-tuple-element.22.coefs, bf16[4,16,48,384]{3,2,1,0:T(8,128)(2,1)S(1)} %get-tuple-element.23.fields_ref, f32[4,16,16,384]{3,2,1,0:T(8,128)S(1)} %get-tuple-element.29.lifted_ref, ...), custom_call_target="tpu_custom_call" | custom-call | flops 1000000000 | tf_op jit(solution)/shard_map/pallas_call | solution.py:79
  30.2 0.0 collective-permute-done.6.refs_2_
  30.2 0.0 collective-permute-done.7.refs_3_
  30.2 0.0 collective-permute-done.4.refs_0_
  30.2 0.0 collective-permute-done.5.refs_1_
  30.2 2.9 %shard_map.48 = (bf16[4,16,112,384]{3,2,1,0:T(8,128)(2,1)S(1)}, f32[32,128]{1,0:T(8,128)S(1)}) custom-call(f32[3,4,16,384]{3,2,1,0:T(8,128)S(1)} %get-tuple-element.22.coefs, bf16[4,16,48,384]{3,2,1,0:T(8,128)(2,1)S(1)} %get-tuple-element.23.fields_ref, f32[4,16,16,384]{3,2,1,0:T(8,128)S(1)} %get-tuple-element.29.lifted_ref, ...), custom_call_target="tpu_custom_call", output_to_operand_aliasing={{0}: (4, {})} | custom-call | tf_op jit(solution)/shard_map/pallas_call | solution.py:79
  33.1 1.8 %all-gather = f32[64,128]{1,0:T(8,128)S(1)} all-gather(f32[32,128]{1,0:T(8,128)S(1)} %get-tuple-element.38), channel_id=2, replica_groups=mesh['plane_0'=4,'plane_1'=8,'plane_2'=2,'depth'=4] {'plane_2'}, dimensions={0}, use_global_device_ids=true | all-gather | bytes 49152 | tf_op jit(solution)/shard_map/all_gather | solution.py:52
  34.9 23.5 %all_to_all.10.pieces_ref = f32[32,16,128]{2,1,0:T(8,128)S(1)} all-to-all(f32[32,16,128]{2,1,0:T(8,128)S(1)} %shard_map.49), channel_id=1, replica_groups=mesh['plane_0'=4,'plane_1'=8,'plane_2'=2,'depth'=4] {'plane_1','depth'}, dimensions={0} | all-to-all | bytes 524288 | tf_op jit(solution)/shard_map/all_to_all | solution.py:54
  58.5 11.2 %all_to_all.11.packed_ref = f32[8,16,128]{2,1,0:T(8,128)S(1)} all-to-all(f32[8,16,128]{2,1,0:T(8,128)S(1)} %shard_map.50), channel_id=1, replica_groups=mesh['plane_0'=4,'plane_1'=8,'plane_2'=2,'depth'=4] {'plane_0','plane_2'}, dimensions={0} | all-to-all | bytes 131072 | tf_op jit(solution)/shard_map/all_to_all | solution.py:55
  69.7 7.9 %shard_map.51 = (f32[80,4,16,384]{3,2,1,0:T(8,128)}, f32[3,48,80]{2,1,0:T(8,128)}) custom-call(f32[8,16,128]{2,1,0:T(8,128)S(1)} %all_to_all.11.packed_ref, bf16[4,16,112,384]{3,2,1,0:T(8,128)(2,1)S(1)} %get-tuple-element.39.parts_ref), custom_call_target="tpu_custom_call" | custom-call | tf_op jit(solution)/shard_map/pallas_call | solution.py:79
  (2 shorter events, 0.1 us)
Async XLA Ops:
  0.6 6.6 %copy-start = (s32[3,16,4,16,384]{4,3,2,1,0:T(8,128)S(1)}, s32[3,16,4,16,384]{4,3,2,1,0:T(8,128)}, u32[]{:S(2)}) copy-start(s32[3,16,4,16,384]{4,3,2,1,0:T(8,128)} %param.3) | copy-start | bytes 14155780
  0.6 6.6 %copy-start.1 = (s32[4,16,384]{2,1,0:T(8,128)S(1)}, s32[4,16,384]{2,1,0:T(8,128)}, u32[]{:S(2)}) copy-start(s32[4,16,384]{2,1,0:T(8,128)} %labels_in.1) | copy-start | bytes 294916
  2.1 15.0 %collective-permute-start.1 = (f32[33,16,384]{2,1,0:T(8,128)S(1)}, f32[33,16,384]{2,1,0:T(8,128)S(1)}, u32[]{:S(2)}, u32[]{:S(2)}) collective-permute-start(f32[33,16,384]{2,1,0:T(8,128)S(1)} %shard_map.44), channel_id=1, source_target_pairs={{4,8},{12,16},{20,24},{28,32},{36,40},{44,48},{52,56},{60,64},{68,... | collective-permute-start | bytes 2433032 | tf_op jit(solution)/shard_map/ppermute | solution.py:61
  8.9 8.3 %collective-permute-start = (f32[33,16,384]{2,1,0:T(8,128)S(1)}, f32[33,16,384]{2,1,0:T(8,128)S(1)}, u32[]{:S(2)}, u32[]{:S(2)}) collective-permute-start(f32[33,16,384]{2,1,0:T(8,128)S(1)} %get-tuple-element.26), channel_id=1, source_target_pairs={{0,4},{8,12},{16,20},{24,28},{32,36},{40,44},{48,52},{56,60},{64,6... | collective-permute-start | bytes 2433032 | tf_op jit(solution)/shard_map/ppermute | solution.py:61
  9.0 6.7 %collective-permute-start.2 = (f32[9,16,384]{2,1,0:T(8,128)S(1)}, f32[9,16,384]{2,1,0:T(8,128)S(1)}, u32[]{:S(2)}, u32[]{:S(2)}) collective-permute-start(f32[9,16,384]{2,1,0:T(8,128)S(1)} %get-tuple-element.27), channel_id=1, source_target_pairs={{0,1},{2,3},{1,0},{3,2},{4,5},{6,7},{5,4},{7,6},{8,9},{10,11},{9,8... | collective-permute-start | bytes 663560 | tf_op jit(solution)/shard_map/ppermute | solution.py:61
  10.3 5.3 %collective-permute-start.3 = (f32[9,16,384]{2,1,0:T(8,128)S(1)}, f32[9,16,384]{2,1,0:T(8,128)S(1)}, u32[]{:S(2)}, u32[]{:S(2)}) collective-permute-start(f32[9,16,384]{2,1,0:T(8,128)S(1)} %get-tuple-element.28), channel_id=1, source_target_pairs={{1,2},{2,1},{5,6},{6,5},{9,10},{10,9},{13,14},{14,13},{17,18},{18,... | collective-permute-start | bytes 663560 | tf_op jit(solution)/shard_map/ppermute | solution.py:61
  18.7 11.5 %collective-permute-start.4 = (f32[16,16,384]{2,1,0:T(8,128)S(1)}, f32[16,16,384]{2,1,0:T(8,128)S(1)}, u32[]{:S(2)}, u32[]{:S(2)}) collective-permute-start(f32[16,16,384]{2,1,0:T(8,128)S(1)} %get-tuple-element.34), channel_id=1, source_target_pairs={{0,4},{8,12},{16,20},{24,28},{32,36},{40,44},{48,52},{56,60},{64,6... | collective-permute-start | bytes 1179656 | tf_op jit(solution)/shard_map/ppermute | solution.py:61
  18.8 11.4 %collective-permute-start.5 = (f32[16,16,384]{2,1,0:T(8,128)S(1)}, f32[16,16,384]{2,1,0:T(8,128)S(1)}, u32[]{:S(2)}, u32[]{:S(2)}) collective-permute-start(f32[16,16,384]{2,1,0:T(8,128)S(1)} %get-tuple-element.35), channel_id=1, source_target_pairs={{4,8},{12,16},{20,24},{28,32},{36,40},{44,48},{52,56},{60,64},{68,... | collective-permute-start | bytes 1179656 | tf_op jit(solution)/shard_map/ppermute | solution.py:61
  22.7 7.4 %collective-permute-start.6 = (f32[4,16,384]{2,1,0:T(8,128)S(1)}, f32[4,16,384]{2,1,0:T(8,128)S(1)}, u32[]{:S(2)}, u32[]{:S(2)}) collective-permute-start(f32[4,16,384]{2,1,0:T(8,128)S(1)} %get-tuple-element.36), channel_id=1, source_target_pairs={{0,1},{2,3},{1,0},{3,2},{4,5},{6,7},{5,4},{7,6},{8,9},{10,11},{9,8... | collective-permute-start | bytes 294920 | tf_op jit(solution)/shard_map/ppermute | solution.py:61
  26.2 4.0 %collective-permute-start.7 = (f32[4,16,384]{2,1,0:T(8,128)S(1)}, f32[4,16,384]{2,1,0:T(8,128)S(1)}, u32[]{:S(2)}, u32[]{:S(2)}) collective-permute-start(f32[4,16,384]{2,1,0:T(8,128)S(1)} %get-tuple-element.37), channel_id=1, source_target_pairs={{1,2},{2,1},{5,6},{6,5},{9,10},{10,9},{13,14},{14,13},{17,18},{18,... | collective-permute-start | bytes 294920 | tf_op jit(solution)/shard_map/ppermute | solution.py:61
